TPU v7x, 32 devices: a whole 2x2x4 slice. The times are simulated.
32 devices in a mesh: dp: 8 (over z, x), ctx: 4 (over y, core).
Axes of the slice: x: 2, y: 2, z: 4, core: 2. Of those that a mesh axis runs over, the one named last changes fastest.
Arguments:
- tokens: bfloat16 [8, 512, 4096], P('dp', 'ctx'), may hold values from -6 to 6
- w_query: bfloat16 [4096, 512], P('dp', 'ctx'), may hold values from -0.09375 to 0.09375
- w_key: bfloat16 [4096, 512], P('dp', 'ctx'), may hold values from -0.09375 to 0.09375
- w_value: bfloat16 [4096, 1024], P('dp', 'ctx'), may hold values from -0.09375 to 0.09375
- decay_log: float32 [8, 2, 512], P('dp'), may hold values from -1 to 0, as said below
- group_gain: float32 [1024], P('ctx'), may hold values from 0.1 to 1.9
Outputs:
- retained: bfloat16 [8, 512, 1024], P('dp', 'ctx')
Inputs may be any that keep to these rules, and one draw needn't show every extreme that they name: `decay_log`: every entry is negative.
All inputs are finite; a program needn't handle non-finite values.
Results may differ from a plain program's by a relative error of at most 0.0068.
Values may be sent and summed in bfloat16 or wider, within the bound.
No kernel may reach another device: no remote copies, remote signals or barrier semaphores. Data moves between devices by JAX's collectives and lax.ppermute only.
A program may use at most 64 MiB of HBM per device.

v0:
```python
import jax
import jax.numpy as jnp
from jax import lax
from jax.sharding import PartitionSpec as P

VAL = 512
BLOCK = 512


norm_eps = 1e-05


def swapped(value, axis, bit):
    mask = 2**bit
    pairs = [(source, source ^ mask) for source in range(lax.axis_size(axis))]
    return lax.ppermute(value, axis, pairs)


def retain(query, keys, values, decay):
    length = query.shape[0]
    blocks = length // BLOCK
    scaling = query.shape[1] ** (-0.5)
    summed = jnp.cumsum(decay)
    q_blocks = query.reshape(blocks, BLOCK, query.shape[1])
    k_blocks = keys.reshape(blocks, BLOCK, keys.shape[1])
    v_blocks = values.reshape(blocks, BLOCK, values.shape[1])
    a_blocks = summed.reshape(blocks, BLOCK)
    row_ids = lax.broadcasted_iota(jnp.int32, (BLOCK, BLOCK), 0)
    col_ids = lax.broadcasted_iota(jnp.int32, (BLOCK, BLOCK), 1)
    causal = row_ids >= col_ids

    def advance(carried_in, pieces):
        memory, prior_log = carried_in
        q_block, k_block, v_block, a_block = pieces
        scores = jnp.dot(q_block, k_block.T, preferred_element_type=jnp.float32) * scaling
        spread_log = jnp.where(causal, a_block[:, None] - a_block[None, :], 0.0)
        weights = jnp.where(causal, scores * jnp.exp(spread_log), 0.0).astype(jnp.bfloat16)
        inside = jnp.dot(weights, v_block, preferred_element_type=jnp.float32)
        lead_query = q_block.astype(jnp.float32) * (scaling * jnp.exp(a_block - prior_log))[:, None]
        carried = jnp.dot(
            lead_query, memory, precision=lax.Precision.HIGHEST, preferred_element_type=jnp.float32
        )
        last_log = a_block[-1]
        faded_keys = k_block.astype(jnp.float32) * jnp.exp(last_log - a_block)[:, None]
        memory = jnp.exp(last_log - prior_log) * memory + jnp.dot(
            faded_keys.T,
            v_block.astype(jnp.float32),
            precision=lax.Precision.HIGHEST,
            preferred_element_type=jnp.float32,
        )
        return ((memory, last_log), inside + carried)

    start_carry = (
        jnp.zeros((query.shape[1], values.shape[1]), jnp.float32),
        jnp.zeros((), jnp.float32),
    )
    _, outputs = lax.scan(advance, start_carry, (q_blocks, k_blocks, v_blocks, a_blocks))
    return outputs.reshape(length, values.shape[1])


def local(tokens, w_query, w_key, w_value, decay_log, group_gain):
    whole = lax.all_gather(tokens, "ctx", axis=1, tiled=True)[0]
    segments = (
        lax.all_gather(w_query, "dp", axis=0, tiled=True),
        lax.all_gather(w_key, "dp", axis=0, tiled=True),
        lax.all_gather(w_value, "dp", axis=0, tiled=True),
    )
    query_half, key_half, value_half = tuple(
        (jnp.dot(whole, segment, preferred_element_type=jnp.float32) for segment in segments)
    )
    query_mine = query_half.astype(jnp.bfloat16)
    key_mine = key_half.astype(jnp.bfloat16)
    values = value_half.astype(jnp.bfloat16)
    query_other, key_other = swapped((query_mine, key_mine), "ctx", 0)
    parity = lax.axis_index("ctx") % 2
    head_index = lax.axis_index("ctx") // 2
    query = jnp.where(
        parity == 0,
        jnp.concatenate([query_mine, query_other], axis=1),
        jnp.concatenate([query_other, query_mine], axis=1),
    )
    keys = jnp.where(
        parity == 0,
        jnp.concatenate([key_mine, key_other], axis=1),
        jnp.concatenate([key_other, key_mine], axis=1),
    )
    rates = lax.dynamic_index_in_dim(decay_log[0], head_index, 0, keepdims=False)
    outputs = retain(query, keys, values, rates)
    own_sums = jnp.sum(outputs, axis=1)
    other_sums = swapped(own_sums, "ctx", 0)
    average = (own_sums + other_sums) / VAL
    centered = outputs - average[:, None]
    own_squares = jnp.sum(centered * centered, axis=1)
    other_squares = swapped(own_squares, "ctx", 0)
    spread = (own_squares + other_squares) / VAL
    normed = (centered * lax.rsqrt(spread + norm_eps)[:, None] * group_gain[None, :]).astype(
        jnp.bfloat16
    )
    returned = lax.all_to_all(normed, "ctx", split_axis=0, concat_axis=1, tiled=True)
    return returned[None]


def solution(mesh):
    in_specs = (
        P("dp", "ctx", None),
        P("dp", "ctx"),
        P("dp", "ctx"),
        P("dp", "ctx"),
        P("dp", None, None),
        P("ctx"),
    )
    out_specs = P("dp", "ctx", None)
    return jax.shard_map(local, mesh=mesh, in_specs=in_specs, out_specs=out_specs, check_vma=False)
```

profile of v0, /device:TPU:0, one launch (start us, length us, event | category | flops | bytes accessed | tf_op | source)
XLA Modules:
  0.0 204.4 jit_solution(4157865813284658062)
XLA Ops:
  6.5 0.0 copy-start
  6.5 0.0 all-gather.9.cloned.1.call-start
  6.5 0.7 all-gather.9.cloned.1.call-update
  7.3 0.0 all-gather.5.cloned.1.call-start
  7.3 0.7 all-gather.5.cloned.1.call-update
  8.0 0.0 all-gather.7.cloned.1.call-start
  8.1 0.7 all-gather.7.cloned.1.call-update
  8.7 0.0 all-gather.11.cloned.1.call-start
  8.8 0.5 all-gather.11.cloned.1.call-update
  9.3 0.0 copy-done
  9.4 0.3 reduce-window.9
  9.7 0.1 slice.9
  9.8 0.1 slice_reduce_fusion
  9.9 0.1 exponential_multiply_fusion
  10.0 42.5 %all-gather.9.cloned.1.call-done = bf16[4096,128]{1,0:T(8,128)(2,1)} async-done(((bf16[512,128]{1,0:T(8,128)(2,1)}), bf16[4096,128]{1,0:T(8,128)(2,1)}) %all-gather.9.cloned.1.call-update) | async-done | bytes 1048592 | tf_op jit(solution)/shard_map/all_gather | solution.py:65
  52.5 34.8 %all-gather.5.cloned.1.call-done = bf16[1,512,4096]{2,1,0:T(8,128)(2,1)} async-done(((bf16[1,128,4096]{2,1,0:T(8,128)(2,1)}), bf16[1,512,4096]{2,1,0:T(8,128)(2,1)}) %all-gather.5.cloned.1.call-update) | async-done | bytes 4194320 | tf_op jit(solution)/shard_map/all_gather | solution.py:62
  87.3 4.0 %fusion.17 = bf16[512,128]{0,1:T(8,128)(2,1)S(1)} fusion(bf16[4096,128]{1,0:T(8,128)(2,1)} %all-gather.9.cloned.1.call-done, bf16[1,512,4096]{2,1,0:T(8,128)(2,1)} %all-gather.5.cloned.1.call-done), kind=kOutput, calls=%fused_computation.14 | convolution fusion | flops 536936448 | bytes 5373952 | tf_op jit(solution)/shard_map/dot_general | solution.py:69
  91.3 0.3 collective-permute-start.1
  91.6 38.1 %all-gather.7.cloned.1.call-done = bf16[4096,128]{1,0:T(8,128)(2,1)} async-done(((bf16[512,128]{1,0:T(8,128)(2,1)}), bf16[4096,128]{1,0:T(8,128)(2,1)}) %all-gather.7.cloned.1.call-update) | async-done | bytes 1048592 | tf_op jit(solution)/shard_map/all_gather | solution.py:64
  129.7 4.0 %fusion.14 = bf16[512,128]{0,1:T(8,128)(2,1)S(1)} fusion(bf16[4096,128]{1,0:T(8,128)(2,1)} %all-gather.7.cloned.1.call-done, bf16[1,512,4096]{2,1,0:T(8,128)(2,1)} %all-gather.5.cloned.1.call-done), kind=kOutput, calls=%fused_computation.13 | convolution fusion | flops 536936448 | bytes 5373952 | tf_op jit(solution)/shard_map/dot_general | solution.py:69
  133.7 0.1 collective-permute-start
  133.8 45.7 %all-gather.11.cloned.1.call-done = bf16[4096,256]{1,0:T(8,128)(2,1)} async-done(((bf16[512,256]{1,0:T(8,128)(2,1)}), bf16[4096,256]{1,0:T(8,128)(2,1)}) %all-gather.11.cloned.1.call-update) | async-done | bytes 2097168 | tf_op jit(solution)/shard_map/all_gather | solution.py:66
  179.5 4.1 %fusion.11 = bf16[512,256]{1,0:T(8,128)(2,1)S(1)} fusion(bf16[4096,256]{1,0:T(8,128)(2,1)} %all-gather.11.cloned.1.call-done, bf16[1,512,4096]{2,1,0:T(8,128)(2,1)} %all-gather.5.cloned.1.call-done), kind=kOutput, calls=%fused_computation.12 | convolution fusion | flops 1073872896 | bytes 6553600 | tf_op jit(solution)/shard_map/dot_general | solution.py:69
  183.6 0.0 copy-start.1
  183.6 0.0 collective-permute-done
  183.6 1.0 fusion.23
  184.7 0.0 collective-permute-done.1
  184.7 0.7 fusion.50
  185.3 0.1 collective-permute-start.2
  185.4 1.1 collective-permute-done.2
  186.6 0.2 multiply_reduce_fusion
  186.8 0.2 collective-permute-start.3
  187.0 1.0 collective-permute-done.3
  188.0 0.0 copy-done.1
  188.0 0.2 multiply_convert_fusion
  188.2 8.5 %all_to_all.16 = bf16[4,128,256]{2,1,0:T(8,128)(2,1)S(1)} all-to-all(bf16[4,128,256]{2,1,0:T(8,128)(2,1)S(1)} %bitcast.23), channel_id=1, replica_groups=mesh['dp'=8,'ctx'=4] {'ctx'}, dimensions={0} | all-to-all | bytes 524288 | tf_op jit(solution)/shard_map/all_to_all | solution.py:99
  196.8 0.2 copy.8
  197.0 0.9 broadcast_in_dim.28
  (4 shorter events, 0.1 us)
Async XLA Ops:
  6.5 2.8 %copy-start = (f32[1,2,512]{2,1,0:T(2,128)S(1)}, f32[1,2,512]{2,1,0:T(2,128)}, u32[]{:S(2)}) copy-start(f32[1,2,512]{2,1,0:T(2,128)} %param.10) | copy-start | bytes 12292
  6.5 46.0 %all-gather.9.cloned.1.call-start = ((), (), s32[]{:S(2)}) async-start(), calls=%async_computation.3 | async-start | bytes 1179648 | tf_op jit(solution)/shard_map/all_gather | solution.py:65
  7.3 80.0 %all-gather.5.cloned.1.call-start = ((), (), s32[]{:S(2)}) async-start(), calls=%async_computation.1 | async-start | bytes 5242880 | tf_op jit(solution)/shard_map/all_gather | solution.py:62
  8.0 121.7 %all-gather.7.cloned.1.call-start = ((), (), s32[]{:S(2)}) async-start(), calls=%async_computation.2 | async-start | bytes 1179648 | tf_op jit(solution)/shard_map/all_gather | solution.py:64
  8.7 170.8 %all-gather.11.cloned.1.call-start = ((), (), s32[]{:S(2)}) async-start(), calls=%async_computation.4 | async-start | bytes 2359296 | tf_op jit(solution)/shard_map/all_gather | solution.py:66
  91.3 93.4 %collective-permute-start.1 = (bf16[512,128]{0,1:T(8,128)(2,1)S(1)}, bf16[512,128]{0,1:T(8,128)(2,1)S(1)}, u32[]{:S(2)}, u32[]{:S(2)}) collective-permute-start(bf16[512,128]{0,1:T(8,128)(2,1)S(1)} %fusion.17), channel_id=1, source_target_pairs={{0,1},{1,0},{2,3},{3,2},{4,5},{5,4},{6,7},{7,6},{8,9},{9,8},{10,11... | collective-permute-start | bytes 393224 | tf_op jit(solution)/shard_map/ppermute | solution.py:16
  133.7 50.0 %collective-permute-start = (bf16[512,128]{0,1:T(8,128)(2,1)S(1)}, bf16[512,128]{0,1:T(8,128)(2,1)S(1)}, u32[]{:S(2)}, u32[]{:S(2)}) collective-permute-start(bf16[512,128]{0,1:T(8,128)(2,1)S(1)} %fusion.14), channel_id=1, source_target_pairs={{0,1},{1,0},{2,3},{3,2},{4,5},{5,4},{6,7},{7,6},{8,9},{9,8},{10,11... | collective-permute-start | bytes 393224 | tf_op jit(solution)/shard_map/ppermute | solution.py:16
  183.6 4.4 %copy-start.1 = (f32[256]{0:T(256)S(1)}, f32[256]{0:T(256)}, u32[]{:S(2)}) copy-start(f32[256]{0:T(256)} %param.11) | copy-start | bytes 3076
  185.3 1.2 collective-permute-start.2
  186.8 1.2 collective-permute-start.3
Sparse Core Ops, SparseCore 0:
  9.5 42.9 all-gather.8
  54.0 33.1 all-gather.4
  89.4 40.2 all-gather.6
  131.7 47.7 all-gather.10
where the time goes:
time: 205 us; the launch traced here: 204 us
  waiting for transfers between devices  166 us (81%)
  matrix products  13.8 us (7%)
  between operations  13.3 us (6%)
  blocking collectives  8.54 us (4%)
    all_gather x1, waiting for transfers between devices, local(): lax.all_gather(w_value, 'dp', axis=0, tiled=True)  45.7 us
    all_gather x1, waiting for transfers between devices, local(): lax.all_gather(w_key, 'dp', axis=0, tiled=True)  42.5 us
    all_gather x1, waiting for transfers between devices, local(): lax.all_gather(w_query, 'dp', axis=0, tiled=True)  38.1 us
    all_gather x1, waiting for transfers between devices, local(): whole = lax.all_gather(tokens, 'ctx', axis=1, tiled=True)[0]  34.8 us
    dot_general x3, matrix products, local(): jnp.dot(whole, segment, preferred_element_type=jnp.float32)  12.1 us
    all_to_all x1, blocking collectives, local(): lax.all_to_all(normed, 'ctx', split_axis=0, concat_axis=1, tiled=True)  8.54 us
  transfers between devices with their start and end apart: 8, of which 6 were waited for; matrix products, arithmetic and copies ran while one was open for 7% of the time, Pallas kernels for 0%

commit v1 on v0

v1 whole, which is shorter than its diff:
```python
import math

import jax
import jax.numpy as jnp
from jax import lax
from jax.sharding import PartitionSpec as P


BLOCK = 512
norm_eps = 1e-05
TOKEN_MOST = 6.0
WEIGHT_MOST = 0.09375


def flipped(value, axis, mask):
    pairs = [(source, source ^ mask) for source in range(lax.axis_size(axis))]
    return lax.ppermute(value, axis, pairs)


def flipped_both(value, mask_dp, mask_ctx):
    ctx = lax.axis_size("ctx")
    pairs = [
        (source, ((source // ctx) ^ mask_dp) * ctx + ((source % ctx) ^ mask_ctx))
        for source in range(lax.axis_size("dp") * ctx)
    ]
    return lax.ppermute(value, ("dp", "ctx"), pairs)


def place_at(turn, count):
    return jnp.where(turn <= count // 2, jnp.maximum(2 * turn - 1, 0), 2 * (count - turn))


def turn_of(place, count):
    half = (place + 1) // 2
    return jnp.where(place % 2 == 1, half, jnp.where(place == 0, 0, count - half))


def loop_order(count):
    return [0] + list(range(1, count, 2)) + list(range(2, count, 2))[::-1]


def columns_of(tokens, outer, width, parity):
    return jnp.concatenate(
        [
            lax.dynamic_slice_in_dim(tokens, (2 * step + parity) * width, width, axis=1)
            for step in range(outer)
        ],
        axis=1,
    )


def dot32(left, right):
    return jnp.dot(left, right, preferred_element_type=jnp.float32)


def dot_exact(left, right):
    return jnp.dot(
        left, right, precision=lax.Precision.HIGHEST, preferred_element_type=jnp.float32
    )


def retain(query, keys, values, summed, me, chunk):
    length = query.shape[0]
    blocks = length // BLOCK
    per_block = BLOCK // chunk
    scaling = query.shape[1] ** (-0.5)
    low = me % per_block
    high = me // per_block
    places = jnp.arange(per_block) ^ low
    pos = (places[:, None] * chunk + jnp.arange(chunk)[None, :]).reshape(BLOCK)
    causal = pos[:, None] >= pos[None, :]
    memory = jnp.zeros((query.shape[1], values.shape[1]), jnp.float32)
    prior_log = jnp.zeros((), jnp.float32)
    outputs = jnp.zeros((length, values.shape[1]), jnp.float32)
    for block in range(blocks):
        natural = summed[block * BLOCK : (block + 1) * BLOCK]
        if blocks == 1:
            q_block, k_block, v_block = query, keys, values
        else:
            start = (block ^ high) * BLOCK
            q_block = lax.dynamic_slice_in_dim(query, start, BLOCK, axis=0)
            k_block = lax.dynamic_slice_in_dim(keys, start, BLOCK, axis=0)
            v_block = lax.dynamic_slice_in_dim(values, start, BLOCK, axis=0)
        pieces = natural.reshape(per_block, chunk)
        a_block = jnp.concatenate(
            [
                lax.dynamic_index_in_dim(pieces, low ^ m, 0, keepdims=False)
                for m in range(per_block)
            ]
        )
        scores = dot32(q_block, k_block.T) * scaling
        spread_log = jnp.where(causal, a_block[:, None] - a_block[None, :], 0.0)
        weights = jnp.where(causal, scores * jnp.exp(spread_log), 0.0).astype(jnp.bfloat16)
        inside = dot32(weights, v_block)
        lead_query = q_block.astype(jnp.float32) * (scaling * jnp.exp(a_block - prior_log))[:, None]
        carried = dot_exact(lead_query, memory)
        last_log = natural[-1]
        faded_keys = k_block.astype(jnp.float32) * jnp.exp(last_log - a_block)[:, None]
        memory = jnp.exp(last_log - prior_log) * memory + dot_exact(
            faded_keys.T, v_block.astype(jnp.float32)
        )
        prior_log = last_log
        result = inside + carried
        if blocks == 1:
            outputs = result
        else:
            outputs = lax.dynamic_update_slice_in_dim(outputs, result, start, axis=0)
    return outputs


def whole(tokens, w_query, w_key, w_value, decay_log, group_gain):
    dp = lax.axis_size("dp")
    ctx = lax.axis_size("ctx")
    outer = dp // 2
    chunk = tokens.shape[1]
    width = w_query.shape[0]
    key_part = w_query.shape[1]
    rank = lax.axis_index("dp")
    me = lax.axis_index("ctx")
    parity = rank % 2
    turn = turn_of(rank // 2, outer)
    mine = tokens[0]

    order = loop_order(outer)
    ring = [
        (order[i] * 2 + p, order[(i + 1) % outer] * 2 + p) for i in range(outer) for p in range(2)
    ]
    held = [jnp.concatenate([w_query, w_key], axis=1), w_value]
    stages = [held]
    for _ in range(1, outer):
        sent = []
        for piece in held:
            sent.append(lax.ppermute(piece, "dp", ring))
        held = sent
        stages.append(held)
    sources = [place_at((turn + outer - step) % outer, outer) for step in range(outer)]

    own_tokens = columns_of(mine, outer, width, parity)
    away_tokens = columns_of(mine, outer, width, 1 - parity)

    def rows_of(piece, mask_dp):
        pieces = {}
        for m in range(0, ctx, 2):
            if m == 0 and mask_dp == 0:
                pieces[m] = piece
            else:
                pieces[m] = flipped_both(piece, mask_dp, m)
        for m in range(0, ctx, 2):
            pieces[m + 1] = flipped(pieces[m], "ctx", 1)
        rows = jnp.zeros((ctx * chunk, outer * width), piece.dtype)
        for m in range(ctx):
            rows = lax.dynamic_update_slice_in_dim(rows, pieces[m], m * chunk, axis=0)
        return rows

    own_rows = rows_of(own_tokens, 0)
    other_rows = rows_of(away_tokens, 1)

    def project(rows, part):
        total = None
        for step in range(outer):
            piece = lax.dynamic_slice_in_dim(rows, sources[step] * width, width, axis=1)
            product = dot32(piece, stages[step][part])
            total = product if total is None else total + product
        return total

    limit = TOKEN_MOST * WEIGHT_MOST * outer * width
    scale = 2.0 ** math.floor(math.log2(65504.0 / limit))

    def summed_over_pair(part):
        away = (project(other_rows, part) * scale).astype(jnp.float16)
        kept = project(own_rows, part)
        came = flipped(away, "dp", 1)
        return (kept + came.astype(jnp.float32) * (1.0 / scale)).astype(jnp.bfloat16)

    pair_mine = summed_over_pair(0)
    values = summed_over_pair(1)

    chunks = [pair_mine[m * chunk : (m + 1) * chunk] for m in range(ctx)]
    pair_other = flipped(jnp.concatenate([chunks[m ^ 1] for m in range(ctx)]), "ctx", 1)
    query = jnp.concatenate([pair_mine[:, :key_part], pair_other[:, :key_part]], axis=1)
    keys = jnp.concatenate([pair_mine[:, key_part:], pair_other[:, key_part:]], axis=1)

    rates = lax.dynamic_index_in_dim(decay_log[0], me // 2, 0, keepdims=False)
    outputs = retain(query, keys, values, jnp.cumsum(rates), me, chunk)

    count = outputs.shape[1]
    own_mean = jnp.mean(outputs, axis=1)
    own_squares = jnp.sum((outputs - own_mean[:, None]) ** 2, axis=1)
    stats = jnp.stack([own_mean, own_squares]).reshape(2, ctx // 2, 2, chunk)
    other = flipped(stats[:, :, ::-1], "ctx", 1).reshape(2, -1)
    average = 0.5 * (own_mean + other[0])
    squares = own_squares + other[1]
    squares = squares + count * ((own_mean - average) ** 2 + (other[0] - average) ** 2)
    spread = squares / (2 * count)
    centered = outputs - average[:, None]
    normed = (centered * lax.rsqrt(spread + norm_eps)[:, None] * group_gain[None, :]).astype(
        jnp.bfloat16
    )

    back = [normed[:chunk]]
    for m in range(1, ctx):
        back.append(flipped(normed[m * chunk : (m + 1) * chunk], "ctx", m))
    for bit in [1 << b for b in range(ctx.bit_length() - 1)]:
        swap = (me & bit) != 0
        back = [jnp.where(swap, back[m ^ bit], back[m]) for m in range(ctx)]
    return jnp.concatenate(back, axis=1)[None]


def solution(mesh):
    in_specs = (
        P("dp", "ctx", None),
        P("dp", "ctx"),
        P("dp", "ctx"),
        P("dp", "ctx"),
        P("dp", None, None),
        P("ctx"),
    )
    out_specs = P("dp", "ctx", None)
    return jax.shard_map(whole, mesh=mesh, in_specs=in_specs, out_specs=out_specs, check_vma=False)
```

time: 205 us -> 75.4 us (0.37)
  waiting for transfers between devices: 166 us -> 32.9 us
  starting transfers between devices: 0.79 us -> 20.1 us
  between operations: 13.3 us -> 0.6 us
  blocking collectives: 8.54 us -> 0 us
  local copies, waits for them, and re-layouts: 1.29 us -> 8.64 us
  matrix products: 13.8 us -> 10.6 us
    all_gather x4 -> x0, waiting for transfers between devices: 161 us -> none  [the longest x1 45.7 us: local(): lax.all_gather(w_value, 'dp', axis=0, tiled=True)]
    ppermute x4 -> x20, waiting for transfers between devices: 2.15 us -> 32.9 us  [the longest x3 12.3 us: flipped_both(): return lax.ppermute(value, ('dp', 'ctx'), pairs)]
    ppermute x4 -> x20, starting transfers between devices: 0.67 us -> 20.1 us  [the longest x6 10.1 us: whole(): sent.append(lax.ppermute(piece, 'dp', ring))]
    all_to_all x1 -> x0, blocking collectives: 8.54 us -> none  [local(): lax.all_to_all(normed, 'ctx', split_axis=0, concat_axis=1, tiled=True)]
    dynamic_update_slice x0 -> x8, local copies, waits for them, and re-layouts: none -> 5.91 us  [rows_of(): rows = lax.dynamic_update_slice_in_dim(rows, pieces[m], m * chunk, axis=0)]
    dot_general x5 -> x18, matrix products: 13.8 us -> 10.6 us  [the longest x17 9.88 us: dot32(): return jnp.dot(left, right, preferred_element_type=jnp.float32)]
    unnamed x4 -> x0, waiting for transfers between devices: 2.61 us -> none
  transfers between devices with their start and end apart: 8 -> 20, of which waited for: 6 -> 10; matrix products, arithmetic and copies ran while one was open for 7% -> 20% of each run, Pallas kernels for 0% -> 0%
where the time goes in v1:
time: 75.4 us; the launch traced here: 74.6 us
  waiting for transfers between devices  32.9 us (44%)
  starting transfers between devices  20.1 us (27%)
  matrix products  10.6 us (14%)
  local copies, waits for them, and re-layouts  8.64 us (11%)
  other arithmetic  1.72 us (2%)
    ppermute x3, waiting for transfers between devices, flipped_both(): return lax.ppermute(value, ('dp', 'ctx'), pairs)  12.3 us
    ppermute x6, waiting for transfers between devices, whole(): sent.append(lax.ppermute(piece, 'dp', ring))  10.3 us
    ppermute x11, waiting for transfers between devices, flipped(): return lax.ppermute(value, axis, pairs)  10.3 us
    ppermute x6, starting transfers between devices, whole(): sent.append(lax.ppermute(piece, 'dp', ring))  10.1 us
    dot_general x17, matrix products, dot32(): return jnp.dot(left, right, preferred_element_type=jnp.float32)  9.88 us
    dynamic_update_slice x8, local copies, waits for them, and re-layouts, rows_of(): rows = lax.dynamic_update_slice_in_dim(rows, pieces[m], m * chunk, axis=0)  5.91 us
    ppermute x11, starting transfers between devices, flipped(): return lax.ppermute(value, axis, pairs)  5.45 us
    ppermute x3, starting transfers between devices, flipped_both(): return lax.ppermute(value, ('dp', 'ctx'), pairs)  4.63 us
  transfers between devices with their start and end apart: 20, of which 10 were waited for; matrix products, arithmetic and copies ran while one was open for 20% of the time, Pallas kernels for 0%

profile of v1, /device:TPU:0, one launch (start us, length us, event | category | flops | bytes accessed | tf_op | source)
XLA Modules:
  0.0 74.6 jit_solution(2078504429012800793)
XLA Ops:
  0.0 1.4 %dynamic-slice_bitcast_fusion.3 = (bf16[128,512]{1,0:T(8,128)(2,1)S(1)}, bf16[128,512]{1,0:T(8,128)(2,1)S(1)}, bf16[128,512]{1,0:T(8,128)(2,1)S(1)}, bf16[128,51...) fusion(bf16[1,128,4096]{2,1,0:T(8,128)(2,1)} %param.6, ...), kind=kLoop, calls=%fused_computation.77 | loop fusion | bytes 2097184 | tf_op jit(solution)/shard_map/dynamic_slice | solution.py:45
  1.4 0.9 %pad_maximum_fusion.1 = bf16[128,2048]{1,0:T(8,128)(2,1)} fusion(bf16[128,512]{1,0:T(8,128)(2,1)S(1)} %get-tuple-element.11, bf16[128,512]{1,0:T(8,128)(2,1)S(1)} %get-tuple-element.12, bf16[128,512]{1,0:T(8,128)(2,1)S(1)} %get-tuple-element.6, bf16[128,512]{1,0:T(8,128)(2,1)S(1)} %get-tuple-element.5), kind=kLoop, calls=%fused_computation.30 | loop fusion | flops 2097152 | bytes 1048576 | tf_op jit(solution)/shard_map/concatenate | solution.py:43
  2.3 3.0 %collective-permute-start.6 = (bf16[128,2048]{1,0:T(8,128)(2,1)}, bf16[128,2048]{1,0:T(8,128)(2,1)}, u32[]{:S(2)}, u32[]{:S(2)}) collective-permute-start(bf16[128,2048]{1,0:T(8,128)(2,1)} %pad_maximum_fusion.1), channel_id=1, source_target_pairs={{0,4},{1,5},{2,6},{3,7},{4,0},{5,1},{6,2},{7,3},{8,12},{9,13},{10,... | collective-permute-start | bytes 1572872 | tf_op jit(solution)/shard_map/ppermute | solution.py:26
  5.3 1.5 %collective-permute-start.8 = (bf16[128,2048]{1,0:T(8,128)(2,1)}, bf16[128,2048]{1,0:T(8,128)(2,1)}, u32[]{:S(2)}, u32[]{:S(2)}) collective-permute-start(bf16[128,2048]{1,0:T(8,128)(2,1)} %pad_maximum_fusion.1), channel_id=1, source_target_pairs={{0,6},{1,7},{2,4},{3,5},{4,2},{5,3},{6,0},{7,1},{8,14},{9,15},{10,... | collective-permute-start | bytes 1572872 | tf_op jit(solution)/shard_map/ppermute | solution.py:26
  6.8 1.6 %collective-permute-start.12 = (bf16[512,256]{1,0:T(8,128)(2,1)S(1)}, bf16[512,256]{1,0:T(8,128)(2,1)S(1)}, u32[]{:S(2)}, u32[]{:S(2)}) collective-permute-start(bf16[512,256]{1,0:T(8,128)(2,1)S(1)} %copy-done.1), channel_id=1, source_target_pairs={{0,8},{4,12},{8,24},{12,28},{24,16},{28,20},{16,0},{20,4},{1,9},{5... | collective-permute-start | bytes 786440 | tf_op jit(solution)/shard_map/ppermute | solution.py:133
  8.4 0.1 collective-permute-start
  8.6 2.6 %collective-permute-start.3 = (bf16[512,256]{1,0:T(8,128)(2,1)S(1)}, bf16[512,256]{1,0:T(8,128)(2,1)S(1)}, u32[]{:S(2)}, u32[]{:S(2)}) collective-permute-start(bf16[512,256]{1,0:T(8,128)(2,1)S(1)} %constant_dynamic-update-slice_fusion.6), channel_id=1, source_target_pairs={{0,8},{4,12},{8,24},{12,28},{24,16},{28,20},{16,0},{20,4},{1,9},{5... | collective-permute-start | bytes 786440 | tf_op jit(solution)/shard_map/ppermute | solution.py:133
  11.2 0.3 reduce-window.9
  11.5 0.1 slice.60
  11.6 0.1 slice_reduce_fusion
  11.8 0.1 broadcast_add_fusion
  11.8 5.0 %collective-permute-done.12 = bf16[512,256]{1,0:T(8,128)(2,1)S(1)} collective-permute-done((bf16[512,256]{1,0:T(8,128)(2,1)S(1)}, bf16[512,256]{1,0:T(8,128)(2,1)S(1)}, u32[]{:S(2)}, u32[]{:S(2)}) %collective-permute-start.12) | collective-permute-done | bytes 262176 | tf_op jit(solution)/shard_map/ppermute | solution.py:133
  16.9 0.2 collective-permute-start.1
  17.0 3.7 %collective-permute-done.3 = bf16[512,256]{1,0:T(8,128)(2,1)S(1)} collective-permute-done((bf16[512,256]{1,0:T(8,128)(2,1)S(1)}, bf16[512,256]{1,0:T(8,128)(2,1)S(1)}, u32[]{:S(2)}, u32[]{:S(2)}) %collective-permute-start.3) | collective-permute-done | bytes 262176 | tf_op jit(solution)/shard_map/ppermute | solution.py:133
  20.8 0.8 %collective-permute-start.13 = (bf16[512,256]{1,0:T(8,128)(2,1)S(1)}, bf16[512,256]{1,0:T(8,128)(2,1)}, u32[]{:S(2)}, u32[]{:S(2)}) collective-permute-start(bf16[512,256]{1,0:T(8,128)(2,1)S(1)} %collective-permute-done.12), channel_id=1, source_target_pairs={{0,8},{4,12},{8,24},{12,28},{24,16},{28,20},{16,0},{20,4},{1,9},{5... | collective-permute-start | bytes 786440 | tf_op jit(solution)/shard_map/ppermute | solution.py:133
  21.6 0.1 add_bitcast_fusion
  21.7 0.1 collective-permute-start.7
  21.9 0.2 dynamic_update_slice.24
  22.2 7.9 %collective-permute-done.8 = bf16[128,2048]{1,0:T(8,128)(2,1)} collective-permute-done((bf16[128,2048]{1,0:T(8,128)(2,1)}, bf16[128,2048]{1,0:T(8,128)(2,1)}, u32[]{:S(2)}, u32[]{:S(2)}) %collective-permute-start.8) | collective-permute-done | bytes 524320 | tf_op jit(solution)/shard_map/ppermute | solution.py:26
  30.1 1.6 %collective-permute-start.4 = (bf16[512,256]{1,0:T(8,128)(2,1)}, bf16[512,256]{1,0:T(8,128)(2,1)S(1)}, u32[]{:S(2)}, u32[]{:S(2)}) collective-permute-start(bf16[512,256]{1,0:T(8,128)(2,1)} %copy-done.2), channel_id=1, source_target_pairs={{0,8},{4,12},{8,24},{12,28},{24,16},{28,20},{16,0},{20,4},{1,9},{5... | collective-permute-start | bytes 786440 | tf_op jit(solution)/shard_map/ppermute | solution.py:133
  31.6 2.6 %collective-permute-start.14 = (bf16[512,256]{1,0:T(8,128)(2,1)}, bf16[512,256]{1,0:T(8,128)(2,1)S(1)}, u32[]{:S(2)}, u32[]{:S(2)}) collective-permute-start(bf16[512,256]{1,0:T(8,128)(2,1)} %collective-permute-done.13), channel_id=1, source_target_pairs={{0,8},{4,12},{8,24},{12,28},{24,16},{28,20},{16,0},{20,4},{1,9},{5... | collective-permute-start | bytes 786440 | tf_op jit(solution)/shard_map/ppermute | solution.py:133
  34.3 4.5 %collective-permute-done.1 = bf16[128,2048]{1,0:T(8,128)(2,1)} collective-permute-done((bf16[128,2048]{1,0:T(8,128)(2,1)S(1)}, bf16[128,2048]{1,0:T(8,128)(2,1)}, u32[]{:S(2)}, u32[]{:S(2)}) %collective-permute-start.1) | collective-permute-done | bytes 524320 | tf_op jit(solution)/shard_map/ppermute | solution.py:26
  38.7 1.1 %constant_dynamic-update-slice_fusion.5 = bf16[512,2048]{1,0:T(8,128)(2,1)S(1)} fusion(bf16[512,2048]{1,0:T(8,128)(2,1)S(1)} %dynamic_update_slice.24, bf16[128,2048]{1,0:T(8,128)(2,1)} %collective-permute-done), kind=kLoop, calls=%fused_computation.116 | loop fusion | bytes 1048576 | tf_op jit(solution)/shard_map/dynamic_update_slice | solution.py:152
  39.8 1.1 %constant_dynamic-update-slice_fusion.4 = bf16[512,2048]{1,0:T(8,128)(2,1)S(1)} fusion(bf16[512,2048]{1,0:T(8,128)(2,1)S(1)} %constant_dynamic-update-slice_fusion.5, bf16[128,2048]{1,0:T(8,128)(2,1)} %collective-permute-done.1), kind=kLoop, calls=%fused_computation.115 | loop fusion | bytes 1048576 | tf_op jit(solution)/shard_map/dynamic_update_slice | solution.py:152
  40.9 1.3 %dynamic_update_slice.28 = bf16[512,2048]{1,0:T(8,128)(2,1)S(1)} pad(bf16[128,2048]{1,0:T(8,128)(2,1)} %collective-permute-done.6, bf16[]{:T(256)} %constant.144.clone.1), padding=0_384x0_0 | pad | bytes 2621442 | tf_op jit(solution)/shard_map/dynamic_update_slice | solution.py:152
  42.2 0.8 %collective-permute-start.5 = (bf16[512,256]{1,0:T(8,128)(2,1)S(1)}, bf16[512,256]{1,0:T(8,128)(2,1)S(1)}, u32[]{:S(2)}, u32[]{:S(2)}) collective-permute-start(bf16[512,256]{1,0:T(8,128)(2,1)S(1)} %collective-permute-done.4), channel_id=1, source_target_pairs={{0,8},{4,12},{8,24},{12,28},{24,16},{28,20},{16,0},{20,4},{1,9},{5... | collective-permute-start | bytes 786440 | tf_op jit(solution)/shard_map/ppermute | solution.py:133
  43.1 1.1 %constant_dynamic-update-slice_fusion.2 = bf16[512,2048]{1,0:T(8,128)(2,1)S(1)} fusion(bf16[512,2048]{1,0:T(8,128)(2,1)S(1)} %dynamic_update_slice.28, bf16[128,2048]{1,0:T(8,128)(2,1)} %collective-permute-done.7), kind=kLoop, calls=%fused_computation.109 | loop fusion | bytes 1048576 | tf_op jit(solution)/shard_map/dynamic_update_slice | solution.py:152
  44.1 1.1 %constant_dynamic-update-slice_fusion.1 = bf16[512,2048]{1,0:T(8,128)(2,1)S(1)} fusion(bf16[512,2048]{1,0:T(8,128)(2,1)S(1)} %constant_dynamic-update-slice_fusion.2, bf16[128,2048]{1,0:T(8,128)(2,1)} %collective-permute-done.8), kind=kLoop, calls=%fused_computation.108 | loop fusion | bytes 1048576 | tf_op jit(solution)/shard_map/dynamic_update_slice | solution.py:152
  45.3 0.3 fusion.35
  45.6 1.3 %fusion.31 = f32[512,256]{0,1:T(8,128)S(1)} fusion(bf16[512,256]{1,0:T(8,128)(2,1)} %collective-permute-done.13, bf16[512,2048]{1,0:T(8,128)(2,1)S(1)} %constant_dynamic-update-slice_fusion, s32[]{:T(128)S(6)} %select_n.191), kind=kOutput, calls=%fused_computation.44 | convolution fusion | flops 134217728 | bytes 1310724 | tf_op jit(solution)/shard_map/dot_general | solution.py:53
  46.9 0.0 copy-start.3
  47.0 0.3 fusion.6
  47.3 0.4 fusion.16
  47.7 1.6 %collective-permute-start.15 = (f16[512,256]{0,1:T(8,128)(2,1)S(1)}, f16[512,256]{0,1:T(8,128)(2,1)S(1)}, u32[]{:S(2)}, u32[]{:S(2)}) collective-permute-start(f16[512,256]{0,1:T(8,128)(2,1)S(1)} %fusion.16), channel_id=1, source_target_pairs={{0,4},{4,0},{8,12},{12,8},{16,20},{20,16},{24,28},{28,24},{1,5},{5... | collective-permute-start | bytes 786440 | tf_op jit(solution)/shard_map/ppermute | solution.py:17
  49.2 0.3 fusion.37
  49.6 0.4 fusion.33
  50.0 0.3 fusion.10
  50.3 1.6 %collective-permute-done.5 = bf16[512,256]{1,0:T(8,128)(2,1)S(1)} collective-permute-done((bf16[512,256]{1,0:T(8,128)(2,1)S(1)}, bf16[512,256]{1,0:T(8,128)(2,1)S(1)}, u32[]{:S(2)}, u32[]{:S(2)}) %collective-permute-start.5) | collective-permute-done | bytes 262176 | tf_op jit(solution)/shard_map/ppermute | solution.py:133
  51.9 0.3 fusion.14
  52.2 1.6 %collective-permute-start.10 = (f16[512,256]{0,1:T(8,128)(2,1)S(1)}, f16[512,256]{0,1:T(8,128)(2,1)S(1)}, u32[]{:S(2)}, u32[]{:S(2)}) collective-permute-start(f16[512,256]{0,1:T(8,128)(2,1)S(1)} %fusion.14), channel_id=1, source_target_pairs={{0,4},{4,0},{8,12},{12,8},{16,20},{20,16},{24,28},{28,24},{1,5},{5... | collective-permute-start | bytes 786440 | tf_op jit(solution)/shard_map/ppermute | solution.py:17
  53.8 0.3 fusion.47
  54.2 1.3 %fusion.43 = f32[512,256]{0,1:T(8,128)S(1)} fusion(bf16[512,256]{1,0:T(8,128)(2,1)} %collective-permute-done.13, bf16[512,2048]{1,0:T(8,128)(2,1)S(1)} %constant_dynamic-update-slice_fusion.3, s32[]{:T(128)S(6)} %select_n.191), kind=kOutput, calls=%fused_computation.56 | convolution fusion | flops 134217728 | bytes 1310724 | tf_op jit(solution)/shard_map/dot_general | solution.py:53
  55.5 0.3 fusion.8
  55.9 0.3 fusion.49
  56.2 0.3 fusion.45
  56.6 0.3 fusion.12
  56.9 4.9 %collective-permute-done.10 = f16[512,256]{0,1:T(8,128)(2,1)S(1)} collective-permute-done((f16[512,256]{0,1:T(8,128)(2,1)S(1)}, f16[512,256]{0,1:T(8,128)(2,1)S(1)}, u32[]{:S(2)}, u32[]{:S(2)}) %collective-permute-start.10) | collective-permute-done | bytes 262176 | tf_op jit(solution)/shard_map/ppermute | solution.py:17
  61.8 0.4 fusion.13
  62.3 0.1 collective-permute-start.11
  62.4 1.1 %fusion.15 = bf16[512,256]{0,1:T(8,128)(2,1)} fusion(f32[512,256]{0,1:T(8,128)S(1)} %fusion.8, bf16[512,256]{1,0:T(8,128)(2,1)S(1)} %collective-permute-done.14, f16[512,256]{0,1:T(8,128)(2,1)S(1)} %collective-permute-done.15, bf16[512,2048]{1,0:T(8,128)(2,1)S(1)} %constant_dynamic-update-slice_fusion.3, s32[]{:T(128)S(6)} %select_n.194), kind=kOutput, calls=%fused_computation.25 | convolution fusion | flops 134873088 | bytes 1835012 | tf_op jit(solution)/shard_map/dot_general | solution.py:53
  63.4 0.4 collective-permute-done.11
  63.9 0.7 fusion.20
  64.6 0.0 copy-start.6
  64.6 1.7 %fusion.92 = (f32[512]{0:T(512)S(1)}, f32[512,256]{0,1:T(8,128)S(1)}) fusion(f32[512,256]{0,1:T(8,128)S(1)} %fusion.20, bf16[512,256]{0,1:T(8,128)(2,1)} %fusion.15, f32[512]{0:T(512)S(1)} %get-tuple-element.32, s32[512]{0:T(512)S(1)} %add_bitcast_fusion, bf16[512,128]{0,1:T(8,128)(2,1)S(1)} %get-tuple-element.22, ...), kind=kOutput, calls=%fused_computation.143 | convolution fusion | flops 271580672 | bytes 1841152 | tf_op jit(solution)/shard_map/dot_general | solution.py:53
  66.3 0.1 multiply_reduce_fusion
  66.4 0.2 collective-permute-start.16
  66.6 1.0 %collective-permute-done.16 = f32[2,2,2,128]{3,2,1,0:T(2,128)S(1)} collective-permute-done((f32[2,2,2,128]{3,2,1,0:T(2,128)S(1)}, f32[2,2,2,128]{3,2,1,0:T(2,128)S(1)}, u32[]{:S(2)}, u32[]{:S(2)}) %collective-permute-start.16) | collective-permute-done | bytes 4128 | tf_op jit(solution)/shard_map/ppermute | solution.py:17
  67.6 0.1 multiply_convert_fusion
  67.8 0.3 collective-permute-start.17
  68.1 1.5 %collective-permute-start.18 = (bf16[128,256]{0,1:T(8,128)(2,1)S(1)}, bf16[128,256]{0,1:T(8,128)(2,1)S(1)}, u32[]{:S(2)}, u32[]{:S(2)}) collective-permute-start(bf16[128,256]{0,1:T(8,128)(2,1)S(1)} %get-tuple-element.18), channel_id=1, source_target_pairs={{0,2},{1,3},{2,0},{3,1},{4,6},{5,7},{6,4},{7,5},{8,10},{9,11},{10,... | collective-permute-start | bytes 196616 | tf_op jit(solution)/shard_map/ppermute | solution.py:17
  69.7 0.1 collective-permute-start.19
  69.7 2.2 %collective-permute-done.17 = bf16[128,256]{0,1:T(8,128)(2,1)S(1)} collective-permute-done((bf16[128,256]{0,1:T(8,128)(2,1)S(1)}, bf16[128,256]{0,1:T(8,128)(2,1)S(1)}, u32[]{:S(2)}, u32[]{:S(2)}) %collective-permute-start.17) | collective-permute-done | bytes 65568 | tf_op jit(solution)/shard_map/ppermute | solution.py:17
  71.9 1.8 %collective-permute-done.18 = bf16[128,256]{0,1:T(8,128)(2,1)S(1)} collective-permute-done((bf16[128,256]{0,1:T(8,128)(2,1)S(1)}, bf16[128,256]{0,1:T(8,128)(2,1)S(1)}, u32[]{:S(2)}, u32[]{:S(2)}) %collective-permute-start.18) | collective-permute-done | bytes 65568 | tf_op jit(solution)/shard_map/ppermute | solution.py:17
  73.7 0.9 %copy.16 = bf16[1,128,1024]{2,1,0:T(8,128)(2,1)} copy(bf16[1,128,1024]{1,2,0:T(8,128)(2,1)S(1)} %maximum_bitcast_fusion) | data formatting | bytes 524288 | tf_op jit(solution)/shard_map/broadcast_in_dim | solution.py:206
  (46 shorter events, 0.6 us)
Async XLA Ops:
  0.0 11.2 %copy-start = (f32[1,2,512]{2,1,0:T(2,128)S(1)}, f32[1,2,512]{2,1,0:T(2,128)}, u32[]{:S(2)}) copy-start(f32[1,2,512]{2,1,0:T(2,128)} %param.10) | copy-start | bytes 12292
  0.0 6.8 %copy-start.1 = (bf16[512,256]{1,0:T(8,128)(2,1)S(1)}, bf16[512,256]{1,0:T(8,128)(2,1)}, u32[]{:S(2)}) copy-start(bf16[512,256]{1,0:T(8,128)(2,1)} %param.9) | copy-start | bytes 786436
  0.0 8.5 %copy-start.4 = (bf16[512,128]{1,0:T(8,128)(2,1)S(1)}, bf16[512,128]{1,0:T(8,128)(2,1)}, u32[]{:S(2)}) copy-start(bf16[512,128]{1,0:T(8,128)(2,1)} %param.7) | copy-start | bytes 393220
  0.0 8.5 %copy-start.5 = (bf16[512,128]{1,0:T(8,128)(2,1)S(1)}, bf16[512,128]{1,0:T(8,128)(2,1)}, u32[]{:S(2)}) copy-start(bf16[512,128]{1,0:T(8,128)(2,1)} %param.8) | copy-start | bytes 393220
  2.3 19.3 %collective-permute-start.6 = (bf16[128,2048]{1,0:T(8,128)(2,1)}, bf16[128,2048]{1,0:T(8,128)(2,1)}, u32[]{:S(2)}, u32[]{:S(2)}) collective-permute-start(bf16[128,2048]{1,0:T(8,128)(2,1)} %pad_maximum_fusion.1), channel_id=1, source_target_pairs={{0,4},{1,5},{2,6},{3,7},{4,0},{5,1},{6,2},{7,3},{8,12},{9,13},{10,... | collective-permute-start | bytes 1572872 | tf_op jit(solution)/shard_map/ppermute | solution.py:26
  5.3 24.8 %collective-permute-start.8 = (bf16[128,2048]{1,0:T(8,128)(2,1)}, bf16[128,2048]{1,0:T(8,128)(2,1)}, u32[]{:S(2)}, u32[]{:S(2)}) collective-permute-start(bf16[128,2048]{1,0:T(8,128)(2,1)} %pad_maximum_fusion.1), channel_id=1, source_target_pairs={{0,6},{1,7},{2,4},{3,5},{4,2},{5,3},{6,0},{7,1},{8,14},{9,15},{10,... | collective-permute-start | bytes 1572872 | tf_op jit(solution)/shard_map/ppermute | solution.py:26
  6.8 10.1 %collective-permute-start.12 = (bf16[512,256]{1,0:T(8,128)(2,1)S(1)}, bf16[512,256]{1,0:T(8,128)(2,1)S(1)}, u32[]{:S(2)}, u32[]{:S(2)}) collective-permute-start(bf16[512,256]{1,0:T(8,128)(2,1)S(1)} %copy-done.1), channel_id=1, source_target_pairs={{0,8},{4,12},{8,24},{12,28},{24,16},{28,20},{16,0},{20,4},{1,9},{5... | collective-permute-start | bytes 786440 | tf_op jit(solution)/shard_map/ppermute | solution.py:133
  8.4 23.2 %collective-permute-start = (bf16[128,2048]{1,0:T(8,128)(2,1)S(1)}, bf16[128,2048]{1,0:T(8,128)(2,1)}, u32[]{:S(2)}, u32[]{:S(2)}) collective-permute-start(bf16[128,2048]{1,0:T(8,128)(2,1)S(1)} %pad_maximum_fusion), channel_id=1, source_target_pairs={{0,1},{1,0},{2,3},{3,2},{4,5},{5,4},{6,7},{7,6},{8,9},{9,8},{10,11... | collective-permute-start | bytes 1572872 | tf_op jit(solution)/shard_map/ppermute | solution.py:17
  8.6 12.2 %collective-permute-start.3 = (bf16[512,256]{1,0:T(8,128)(2,1)S(1)}, bf16[512,256]{1,0:T(8,128)(2,1)S(1)}, u32[]{:S(2)}, u32[]{:S(2)}) collective-permute-start(bf16[512,256]{1,0:T(8,128)(2,1)S(1)} %constant_dynamic-update-slice_fusion.6), channel_id=1, source_target_pairs={{0,8},{4,12},{8,24},{12,28},{24,16},{28,20},{16,0},{20,4},{1,9},{5... | collective-permute-start | bytes 786440 | tf_op jit(solution)/shard_map/ppermute | solution.py:133
  16.9 21.9 %collective-permute-start.1 = (bf16[128,2048]{1,0:T(8,128)(2,1)S(1)}, bf16[128,2048]{1,0:T(8,128)(2,1)}, u32[]{:S(2)}, u32[]{:S(2)}) collective-permute-start(bf16[128,2048]{1,0:T(8,128)(2,1)S(1)} %pad_maximum_fusion), channel_id=1, source_target_pairs={{0,2},{1,3},{2,0},{3,1},{4,6},{5,7},{6,4},{7,5},{8,10},{9,11},{10,... | collective-permute-start | bytes 1572872 | tf_op jit(solution)/shard_map/ppermute | solution.py:26
  20.8 1.1 %copy-start.2 = (bf16[512,256]{1,0:T(8,128)(2,1)}, bf16[512,256]{1,0:T(8,128)(2,1)S(1)}, u32[]{:S(2)}) copy-start(bf16[512,256]{1,0:T(8,128)(2,1)S(1)} %collective-permute-done.3) | copy-start | bytes 786436
  20.8 10.9 %collective-permute-start.13 = (bf16[512,256]{1,0:T(8,128)(2,1)S(1)}, bf16[512,256]{1,0:T(8,128)(2,1)}, u32[]{:S(2)}, u32[]{:S(2)}) collective-permute-start(bf16[512,256]{1,0:T(8,128)(2,1)S(1)} %collective-permute-done.12), channel_id=1, source_target_pairs={{0,8},{4,12},{8,24},{12,28},{24,16},{28,20},{16,0},{20,4},{1,9},{5... | collective-permute-start | bytes 786440 | tf_op jit(solution)/shard_map/ppermute | solution.py:133
  21.7 21.4 %collective-permute-start.7 = (bf16[128,2048]{1,0:T(8,128)(2,1)}, bf16[128,2048]{1,0:T(8,128)(2,1)}, u32[]{:S(2)}, u32[]{:S(2)}) collective-permute-start(bf16[128,2048]{1,0:T(8,128)(2,1)} %collective-permute-done.6), channel_id=1, source_target_pairs={{0,1},{1,0},{2,3},{3,2},{4,5},{5,4},{6,7},{7,6},{8,9},{9,8},{10,11... | collective-permute-start | bytes 1572872 | tf_op jit(solution)/shard_map/ppermute | solution.py:17
  30.1 12.1 %collective-permute-start.4 = (bf16[512,256]{1,0:T(8,128)(2,1)}, bf16[512,256]{1,0:T(8,128)(2,1)S(1)}, u32[]{:S(2)}, u32[]{:S(2)}) collective-permute-start(bf16[512,256]{1,0:T(8,128)(2,1)} %copy-done.2), channel_id=1, source_target_pairs={{0,8},{4,12},{8,24},{12,28},{24,16},{28,20},{16,0},{20,4},{1,9},{5... | collective-permute-start | bytes 786440 | tf_op jit(solution)/shard_map/ppermute | solution.py:133
  31.6 13.6 %collective-permute-start.9 = (bf16[128,2048]{1,0:T(8,128)(2,1)}, bf16[128,2048]{1,0:T(8,128)(2,1)S(1)}, u32[]{:S(2)}, u32[]{:S(2)}) collective-permute-start(bf16[128,2048]{1,0:T(8,128)(2,1)} %collective-permute-done.8), channel_id=1, source_target_pairs={{0,1},{1,0},{2,3},{3,2},{4,5},{5,4},{6,7},{7,6},{8,9},{9,8},{10,11... | collective-permute-start | bytes 1572872 | tf_op jit(solution)/shard_map/ppermute | solution.py:17
  31.6 15.7 %collective-permute-start.14 = (bf16[512,256]{1,0:T(8,128)(2,1)}, bf16[512,256]{1,0:T(8,128)(2,1)S(1)}, u32[]{:S(2)}, u32[]{:S(2)}) collective-permute-start(bf16[512,256]{1,0:T(8,128)(2,1)} %collective-permute-done.13), channel_id=1, source_target_pairs={{0,8},{4,12},{8,24},{12,28},{24,16},{28,20},{16,0},{20,4},{1,9},{5... | collective-permute-start | bytes 786440 | tf_op jit(solution)/shard_map/ppermute | solution.py:133
  38.7 15.1 %collective-permute-start.2 = (bf16[128,2048]{1,0:T(8,128)(2,1)}, bf16[128,2048]{1,0:T(8,128)(2,1)S(1)}, u32[]{:S(2)}, u32[]{:S(2)}) collective-permute-start(bf16[128,2048]{1,0:T(8,128)(2,1)} %collective-permute-done.1), channel_id=1, source_target_pairs={{0,1},{1,0},{2,3},{3,2},{4,5},{5,4},{6,7},{7,6},{8,9},{9,8},{10,11... | collective-permute-start | bytes 1572872 | tf_op jit(solution)/shard_map/ppermute | solution.py:17
  42.2 9.7 %collective-permute-start.5 = (bf16[512,256]{1,0:T(8,128)(2,1)S(1)}, bf16[512,256]{1,0:T(8,128)(2,1)S(1)}, u32[]{:S(2)}, u32[]{:S(2)}) collective-permute-start(bf16[512,256]{1,0:T(8,128)(2,1)S(1)} %collective-permute-done.4), channel_id=1, source_target_pairs={{0,8},{4,12},{8,24},{12,28},{24,16},{28,20},{16,0},{20,4},{1,9},{5... | collective-permute-start | bytes 786440 | tf_op jit(solution)/shard_map/ppermute | solution.py:133
  46.9 2.3 %copy-start.3 = (bf16[512,256]{1,0:T(8,128)(2,1)S(1)}, bf16[512,256]{1,0:T(8,128)(2,1)}, u32[]{:S(2)}) copy-start(bf16[512,256]{1,0:T(8,128)(2,1)} %copy-done.2) | copy-start | bytes 786436
  47.7 14.7 %collective-permute-start.15 = (f16[512,256]{0,1:T(8,128)(2,1)S(1)}, f16[512,256]{0,1:T(8,128)(2,1)S(1)}, u32[]{:S(2)}, u32[]{:S(2)}) collective-permute-start(f16[512,256]{0,1:T(8,128)(2,1)S(1)} %fusion.16), channel_id=1, source_target_pairs={{0,4},{4,0},{8,12},{12,8},{16,20},{20,16},{24,28},{28,24},{1,5},{5... | collective-permute-start | bytes 786440 | tf_op jit(solution)/shard_map/ppermute | solution.py:17
  52.2 9.6 %collective-permute-start.10 = (f16[512,256]{0,1:T(8,128)(2,1)S(1)}, f16[512,256]{0,1:T(8,128)(2,1)S(1)}, u32[]{:S(2)}, u32[]{:S(2)}) collective-permute-start(f16[512,256]{0,1:T(8,128)(2,1)S(1)} %fusion.14), channel_id=1, source_target_pairs={{0,4},{4,0},{8,12},{12,8},{16,20},{20,16},{24,28},{28,24},{1,5},{5... | collective-permute-start | bytes 786440 | tf_op jit(solution)/shard_map/ppermute | solution.py:17
  62.3 1.6 %collective-permute-start.11 = (bf16[512,256]{0,1:T(8,128)(2,1)S(1)}, bf16[512,256]{0,1:T(8,128)(2,1)S(1)}, u32[]{:S(2)}, u32[]{:S(2)}) collective-permute-start(bf16[512,256]{0,1:T(8,128)(2,1)S(1)} %pad_maximum_fusion.2), channel_id=1, source_target_pairs={{0,1},{1,0},{2,3},{3,2},{4,5},{5,4},{6,7},{7,6},{8,9},{9,8},{10,11... | collective-permute-start | bytes 786440 | tf_op jit(solution)/shard_map/ppermute | solution.py:17
  64.6 3.1 %copy-start.6 = (f32[256]{0:T(256)S(1)}, f32[256]{0:T(256)}, u32[]{:S(2)}) copy-start(f32[256]{0:T(256)} %param.11) | copy-start | bytes 3076
  66.4 1.2 %collective-permute-start.16 = (f32[2,2,2,128]{3,2,1,0:T(2,128)S(1)}, f32[2,2,2,128]{3,2,1,0:T(2,128)S(1)}, u32[]{:S(2)}, u32[]{:S(2)}) collective-permute-start(f32[2,2,2,128]{3,2,1,0:T(2,128)S(1)} %rev.3), channel_id=1, source_target_pairs={{0,1},{1,0},{2,3},{3,2},{4,5},{5,4},{6,7},{7,6},{8,9},{9,8},{10,11... | collective-permute-start | bytes 12296 | tf_op jit(solution)/shard_map/ppermute | solution.py:17
  67.8 4.1 %collective-permute-start.17 = (bf16[128,256]{0,1:T(8,128)(2,1)S(1)}, bf16[128,256]{0,1:T(8,128)(2,1)S(1)}, u32[]{:S(2)}, u32[]{:S(2)}) collective-permute-start(bf16[128,256]{0,1:T(8,128)(2,1)S(1)} %get-tuple-element.19), channel_id=1, source_target_pairs={{0,3},{1,2},{2,1},{3,0},{4,7},{5,6},{6,5},{7,4},{8,11},{9,10},{10,... | collective-permute-start | bytes 196616 | tf_op jit(solution)/shard_map/ppermute | solution.py:17
  68.1 5.5 %collective-permute-start.18 = (bf16[128,256]{0,1:T(8,128)(2,1)S(1)}, bf16[128,256]{0,1:T(8,128)(2,1)S(1)}, u32[]{:S(2)}, u32[]{:S(2)}) collective-permute-start(bf16[128,256]{0,1:T(8,128)(2,1)S(1)} %get-tuple-element.18), channel_id=1, source_target_pairs={{0,2},{1,3},{2,0},{3,1},{4,6},{5,7},{6,4},{7,5},{8,10},{9,11},{10,... | collective-permute-start | bytes 196616 | tf_op jit(solution)/shard_map/ppermute | solution.py:17
  69.7 4.0 %collective-permute-start.19 = (bf16[128,256]{0,1:T(8,128)(2,1)S(1)}, bf16[128,256]{0,1:T(8,128)(2,1)S(1)}, u32[]{:S(2)}, u32[]{:S(2)}) collective-permute-start(bf16[128,256]{0,1:T(8,128)(2,1)S(1)} %get-tuple-element.17), channel_id=1, source_target_pairs={{0,1},{1,0},{2,3},{3,2},{4,5},{5,4},{6,7},{7,6},{8,9},{9,8},{10,11... | collective-permute-start | bytes 196616 | tf_op jit(solution)/shard_map/ppermute | solution.py:17

commit v2 on v1

v2 whole, which is shorter than its diff:
```python
import math

import jax
import jax.numpy as jnp
from jax import lax
from jax.experimental import pallas as pl
from jax.experimental.pallas import tpu as pltpu
from jax.sharding import PartitionSpec as P


BLOCK = 512
norm_eps = 1e-05
TOKEN_MOST = 6.0
WEIGHT_MOST = 0.09375
GRANT = 16 * 2**20


def flipped(value, axis, mask):
    pairs = [(source, source ^ mask) for source in range(lax.axis_size(axis))]
    return lax.ppermute(value, axis, pairs)


def flipped_both(value, mask_dp, mask_ctx):
    ctx = lax.axis_size("ctx")
    pairs = [
        (source, ((source // ctx) ^ mask_dp) * ctx + ((source % ctx) ^ mask_ctx))
        for source in range(lax.axis_size("dp") * ctx)
    ]
    return lax.ppermute(value, ("dp", "ctx"), pairs)


def place_at(turn, count):
    return jnp.where(turn <= count // 2, jnp.maximum(2 * turn - 1, 0), 2 * (count - turn))


def turn_of(place, count):
    half = (place + 1) // 2
    return jnp.where(place % 2 == 1, half, jnp.where(place == 0, 0, count - half))


def loop_order(count):
    return [0] + list(range(1, count, 2)) + list(range(2, count, 2))[::-1]


def dot32(left, right):
    return jnp.dot(left, right, preferred_element_type=jnp.float32)


def dot_exact(left, right):
    return jnp.dot(
        left, right, precision=lax.Precision.HIGHEST, preferred_element_type=jnp.float32
    )


def near(operands):
    return [pltpu.with_memory_space_constraint(operand, pltpu.VMEM) for operand in operands]


def kernel(body, out, operands, scalars=None, scratch=(), far=()):
    vmem = pl.BlockSpec(memory_space=pltpu.VMEM)
    specs = [vmem] * len(operands) + [pl.BlockSpec(memory_space=pl.ANY)] * len(far)
    inputs = near(operands)
    inputs += [pltpu.with_memory_space_constraint(operand, pltpu.HBM) for operand in far]
    if scalars is not None:
        specs = [pl.BlockSpec(memory_space=pltpu.SMEM)] + specs
        inputs = [scalars] + inputs
    return pl.pallas_call(
        body,
        out_shape=out,
        in_specs=specs,
        out_specs=jax.tree.map(lambda _: vmem, out),
        scratch_shapes=list(scratch),
        compiler_params=pltpu.CompilerParams(vmem_limit_bytes=GRANT),
    )(*inputs)


def prepared(ids, tokens, w_query, w_key, outer):
    chunk = tokens.shape[0]
    width, part = w_query.shape

    def body(ids_ref, tokens_ref, query_ref, key_ref, pair_ref, own_ref, away_ref, arrivals):
        parity = ids_ref[0] % 2
        copies = [
            (query_ref, pair_ref.at[:, pl.ds(0, part)]),
            (key_ref, pair_ref.at[:, pl.ds(part, part)]),
        ]
        for step in range(outer):
            for side, out_ref in ((1 - parity, away_ref), (parity, own_ref)):
                start = pl.multiple_of((2 * step + side) * width, width)
                copies.append((tokens_ref.at[:, pl.ds(start, width)], out_ref.at[step]))
        copies = [
            pltpu.make_async_copy(source, target, arrivals.at[i])
            for i, (source, target) in enumerate(copies)
        ]
        for copy in copies:
            copy.start()
        for copy in copies:
            copy.wait()

    return kernel(
        body,
        [
            pltpu.VMEM((width, 2 * part), jnp.bfloat16),
            pltpu.VMEM((outer, chunk, width), jnp.bfloat16),
            pltpu.VMEM((outer, chunk, width), jnp.bfloat16),
        ],
        [],
        scalars=ids,
        scratch=[pltpu.SemaphoreType.DMA((2 + 2 * outer,))],
        far=[tokens, w_query, w_key],
    )


def decayed(ids, decay_log, chunk):
    _, length = decay_log.shape
    blocks = length // BLOCK
    per_block = BLOCK // chunk

    def body(ids_ref, rates_ref, row_ref, col_ref, end_ref, place_row, place_col, sums):
        head = ids_ref[1] // 2
        rates = rates_ref[pl.ds(head, 1), :]
        pieces = [rates[:, i * chunk : (i + 1) * chunk] for i in range(length // chunk)]
        before = lax.broadcasted_iota(jnp.int32, (chunk, chunk), 0)
        after = lax.broadcasted_iota(jnp.int32, (chunk, chunk), 1)
        inside = dot_exact(
            jnp.concatenate(pieces, axis=0), (before <= after).astype(jnp.float32)
        )
        carried = jnp.zeros((1, 1), jnp.float32)
        for i in range(length // chunk):
            sums[i : i + 1, :] = inside[i : i + 1, :] + carried
            carried = carried + inside[i : i + 1, chunk - 1 : chunk]
            if (i + 1) % per_block == 0:
                n = i // per_block
                end_ref[n : n + 1, :] = carried
        low = ids_ref[1] % per_block
        steps = lax.broadcasted_iota(jnp.int32, (1, chunk), 1)
        places = jnp.concatenate([(low ^ m) * chunk + steps for m in range(per_block)], axis=1)
        place_row[...] = places

        def column(row):
            return jnp.broadcast_to(row, (8, BLOCK)).T[:, :1]

        place_col[...] = column(places.astype(jnp.float32)).astype(jnp.int32)
        for n in range(blocks):
            row = jnp.concatenate(
                [sums[pl.ds(n * per_block + (low ^ m), 1), :] for m in range(per_block)], axis=1
            )
            row_ref[n] = row
            col_ref[n] = column(row)

    return kernel(
        body,
        [
            pltpu.VMEM((blocks, 1, BLOCK), jnp.float32),
            pltpu.VMEM((blocks, BLOCK, 1), jnp.float32),
            pltpu.VMEM((blocks, 1), jnp.float32),
            pltpu.VMEM((1, BLOCK), jnp.int32),
            pltpu.VMEM((BLOCK, 1), jnp.int32),
        ],
        [decay_log],
        scalars=ids,
        scratch=[pltpu.VMEM((length // chunk, chunk), jnp.float32)],
    )


def halved(weight):
    width, wide = weight.shape
    half = wide // 2

    def body(ref, first, second):
        first[...] = ref[:, :half]
        second[...] = ref[:, half:]

    return kernel(body, [pltpu.VMEM((width, half), weight.dtype)] * 2, [weight])


def mixed(ids, sides, stages):
    steps = len(stages)
    count = len(sides[0])
    _, chunk, width = sides[0][0].shape
    parts = [w.shape[1] for w in stages[0]]
    cuts = [sum(parts[:i]) for i in range(len(parts))]
    length = count * chunk

    def body(ids_ref, *refs):
        turn = turn_of(ids_ref[0] // 2, steps + 1)
        sources = [place_at((turn + steps + 1 - step) % (steps + 1), steps + 1) for step in range(steps + 1)]
        at = 0
        pieces = []
        for _ in sides:
            pieces.append(refs[at : at + count])
            at += count
        weights = []
        for _ in range(steps):
            weights.append(refs[at : at + len(parts)])
            at += len(parts)
        for side in pieces:
            total_ref, last = refs[at : at + 2]
            at += 2
            for m in range(0, count, 2):

                def rows(step):
                    return jnp.concatenate(
                        [side[m][sources[step]], side[m + 1][sources[step]]], axis=0
                    )

                span = pl.ds(m * chunk, 2 * chunk)
                for part, cut in zip(range(len(parts)), cuts):
                    total = None
                    for step in range(steps):
                        product = dot32(rows(step), weights[step][part][...])
                        total = product if total is None else total + product
                    total_ref[span, cut : cut + parts[part]] = total
                last[span, :] = rows(steps)

    outs = kernel(
        body,
        [
            pltpu.VMEM((length, sum(parts)), jnp.float32),
            pltpu.VMEM((length, width), jnp.bfloat16),
        ]
        * len(sides),
        [piece for side in sides for piece in side] + [w for step in stages for w in step],
        scalars=ids,
    )
    return outs[:2], outs[2:]


def projected(away, kept, weight, cut, scale):
    (length, _), part = away[0].shape, weight.shape[1]

    def body(away_total, away_last, kept_total, kept_last, w, away_out, kept_out):
        columns = w[...]
        span = slice(cut, cut + part)
        gone = away_total[:, span] + dot32(away_last[...], columns)
        away_out[...] = gone * scale
        kept_out[...] = kept_total[:, span] + dot32(kept_last[...], columns)

    return kernel(body, [pltpu.VMEM((length, part), jnp.float32)] * 2, [*away, *kept, weight])


def joined(kept, came, scale):
    return (kept + came.astype(jnp.float32) * (1.0 / scale)).astype(jnp.bfloat16)


def weighed(pair_mine, pair_other, decays, prior, memories):
    log_row, log_col, place_row, place_col = decays
    length, wide = pair_mine.shape
    part = wide // 2
    scaling = (2 * part) ** (-0.5)

    def body(mine, other, log_row, log_col, place_row, place_col, prior, *refs):
        states = refs[: len(memories)]
        out = refs[len(memories)]
        reads = refs[len(memories) + 1 :]

        def scored(ref, rows):
            return lax.dot_general(
                ref[rows, :part],
                ref[:, part:],
                (((1,), (1,)), ((), ())),
                preferred_element_type=jnp.float32,
            )

        tile = min(256, length)
        for start in range(0, length, tile):
            rows = pl.ds(start, tile)
            scores = (scored(mine, rows) + scored(other, rows)) * scaling
            causal = place_col[rows, :] >= place_row[...]
            spread_log = jnp.where(causal, log_col[rows, :] - log_row[...], 0.0)
            out[rows, :] = jnp.where(causal, scores * jnp.exp(spread_log), 0.0).astype(
                jnp.bfloat16
            )
            fade = scaling * jnp.exp(log_col[rows, :] - prior[...])
            for state, read in zip(states, reads):
                total = jnp.zeros((tile, state.shape[1]), jnp.float32)
                for i, ref in enumerate((mine, other)):
                    lead = ref[rows, :part].astype(jnp.float32) * fade
                    total = total + dot_exact(lead, state[i * part : (i + 1) * part, :])
                read[rows, :] = total

    outs = kernel(
        body,
        [pltpu.VMEM((length, length), jnp.bfloat16)]
        + [pltpu.VMEM((length, state.shape[1]), jnp.float32) for state in memories],
        [pair_mine, pair_other, log_row, log_col, place_row, place_col, prior, *memories],
    )
    return outs[0], outs[1:]


def applied(weights, values, carried, chunk):
    length, part = values.shape

    def body(weights_ref, values_ref, carried_ref, *outs):
        for m, out in enumerate(outs):
            rows = pl.ds(m * chunk, chunk)
            out[...] = dot32(weights_ref[rows, :], values_ref[...]) + carried_ref[rows, :]

    return kernel(
        body,
        [pltpu.VMEM((chunk, part), jnp.float32)] * (length // chunk),
        [weights, values, carried],
    )


def finished(ids, pieces, gains):
    count = len(pieces)
    groups = len(pieces[0])
    chunk, part = pieces[0][0].shape
    wide = groups * part

    def body(ids_ref, *refs):
        out = refs[-1]
        gain_refs = refs[count * groups : count * groups + count]
        for m in range(0, count, 2):
            mine = [refs[i] for i in range(m * groups, (m + 2) * groups)]
            total = sum(jnp.sum(ref[...], axis=1, keepdims=True) for ref in mine)
            average = total / (2 * wide)
            centered = [ref[...] - average for ref in mine]
            squares = sum(jnp.sum(c * c, axis=1, keepdims=True) for c in centered)
            rate = lax.rsqrt(squares / (2 * wide) + norm_eps)
            for i, c in enumerate(centered):
                which = m + i // groups
                group = i % groups
                gain = gain_refs[which][:, group * part : (group + 1) * part]
                start = pl.multiple_of((ids_ref[1] ^ which) * wide + group * part, part)
                out[:, pl.ds(start, part)] = (c * rate * gain).astype(jnp.bfloat16)

    return kernel(
        body,
        jax.ShapeDtypeStruct((chunk, count * wide), jnp.bfloat16),
        [ref for piece in pieces for ref in piece] + list(gains),
        scalars=ids,
    )


def whole(tokens, w_query, w_key, w_value, decay_log, group_gain):
    dp = lax.axis_size("dp")
    ctx = lax.axis_size("ctx")
    outer = dp // 2
    chunk = tokens.shape[1]
    width = w_query.shape[0]
    key_part = w_query.shape[1]
    half = w_value.shape[1] // 2
    rank = lax.axis_index("dp")
    me = lax.axis_index("ctx")
    ids = jnp.stack([rank, me]).astype(jnp.int32)
    length = ctx * chunk
    blocks = length // BLOCK
    high = me // (BLOCK // chunk)

    pair, own_tokens, away_tokens = prepared(ids, tokens[0], w_query, w_key, outer)
    log_rows, log_cols, ends, place_row, place_col = decayed(ids, decay_log[0], chunk)

    order = loop_order(outer)
    ring = [
        (order[i] * 2 + p, order[(i + 1) % outer] * 2 + p) for i in range(outer) for p in range(2)
    ]
    held = [pair, w_value]
    stages = []
    for step in range(1, outer):
        stages.append(held)
        if step == outer - 1:
            held = [held[0], *halved(held[1])]
        sent = []
        for piece in held:
            sent.append(lax.ppermute(piece, "dp", ring))
        held = sent

    def rows_of(piece, mask_dp):
        pieces = {}
        for m in range(0, ctx, 2):
            if m == 0 and mask_dp == 0:
                pieces[m] = piece
            else:
                pieces[m] = flipped_both(piece, mask_dp, m)
        for m in range(0, ctx, 2):
            pieces[m + 1] = flipped(pieces[m], "ctx", 1)
        return [pieces[m] for m in range(ctx)]

    own_rows = rows_of(own_tokens, 0)
    away_rows = rows_of(away_tokens, 1)
    gains = [group_gain[None]]
    for m in range(1, ctx):
        gains.append(flipped(group_gain[None], "ctx", m))

    away, kept = mixed(ids, (away_rows, own_rows), stages)

    limit = TOKEN_MOST * WEIGHT_MOST * outer * width
    scale = 2.0 ** math.floor(math.log2(65504.0 / limit))
    stays = []
    cut = 0
    for weight in held:
        gone, stay = projected(away, kept, weight, cut, scale)
        cut += weight.shape[1]
        stays.append((stay, flipped(gone.astype(jnp.float16), "dp", 1)))

    pair_mine = joined(*stays[0], scale)
    chunks = [pair_mine[m * chunk : (m + 1) * chunk] for m in range(ctx)]
    pair_other = flipped(jnp.concatenate([chunks[m ^ 1] for m in range(ctx)]), "ctx", 1)

    def cut_rows(array, block):
        if blocks == 1:
            return array
        return lax.dynamic_slice_in_dim(array, (block ^ high) * BLOCK, BLOCK, axis=0)

    memories = [jnp.zeros((2 * key_part, half), jnp.float32) for _ in stays[1:]]
    prior = jnp.zeros((1, 1), jnp.float32)
    outputs = [jnp.zeros((length, half), jnp.float32) for _ in stays[1:]]
    arrived = [[] for _ in range(ctx)]
    values = []
    for stay in stays[1:]:
        values.append(joined(*stay, scale))
    for n in range(blocks):
        mine, other = cut_rows(pair_mine, n), cut_rows(pair_other, n)
        decays = (log_rows[n], log_cols[n], place_row, place_col)
        weights, carried = weighed(mine, other, decays, prior, memories)
        k_block = jnp.concatenate([mine[:, key_part:], other[:, key_part:]], axis=1)
        end = ends[n : n + 1]
        faded = k_block.astype(jnp.float32) * jnp.exp(end - log_cols[n])
        for group in range(len(values)):
            v_block = cut_rows(values[group], n)
            results = applied(weights, v_block, carried[group], chunk)
            memories[group] = jnp.exp(end - prior) * memories[group] + dot_exact(
                faded.T, v_block.astype(jnp.float32)
            )
            if blocks > 1:
                outputs[group] = lax.dynamic_update_slice_in_dim(
                    outputs[group], jnp.concatenate(results), (n ^ high) * BLOCK, axis=0
                )
            else:
                outputs[group] = results
        prior = end
    for results in outputs:
        if blocks > 1:
            results = [results[m * chunk : (m + 1) * chunk] for m in range(ctx)]
        arrived[0].append(results[0])
        for m in range(1, ctx):
            arrived[m].append(flipped(results[m], "ctx", m))
    return finished(ids, arrived, gains)[None]


def solution(mesh):
    in_specs = (
        P("dp", "ctx", None),
        P("dp", "ctx"),
        P("dp", "ctx"),
        P("dp", "ctx"),
        P("dp", None, None),
        P("ctx"),
    )
    out_specs = P("dp", "ctx", None)
    return jax.shard_map(whole, mesh=mesh, in_specs=in_specs, out_specs=out_specs, check_vma=False)
```

time: 75.4 us -> 76 us (level)
  Pallas kernels: 0 us -> 10.8 us
  matrix products: 10.6 us -> 0 us
  starting transfers between devices: 20.1 us -> 28.6 us
  local copies, waits for them, and re-layouts: 8.64 us -> 0.64 us
  waiting for transfers between devices: 32.9 us -> 35.2 us
  other arithmetic: 1.72 us -> 0.36 us
    pallas_call x0 -> x11, Pallas kernels: none -> 10.8 us  [kernel(): pl.pallas_call(body, out_shape=out, in_specs=specs, out_specs=jax.tree.ma...]
    ppermute x6 -> x7, waiting for transfers between devices: 10.3 us -> 21 us  [whole(): sent.append(lax.ppermute(piece, 'dp', ring))]
    dot_general x18 -> x0, matrix products: 10.6 us -> none  [the longest x17 9.88 us: dot32(): return jnp.dot(left, right, preferred_element_type=jnp.float32)]
    dynamic_update_slice x8 -> x0, local copies, waits for them, and re-layouts: 5.91 us -> none  [rows_of(): rows = lax.dynamic_update_slice_in_dim(rows, pieces[m], m * chunk, axis=0)]
    ppermute x3, waiting for transfers between devices: 12.3 us -> 7.42 us  [flipped_both(): return lax.ppermute(value, ('dp', 'ctx'), pairs)]
    ppermute x11 -> x17, starting transfers between devices: 5.45 us -> 10 us  [flipped(): return lax.ppermute(value, axis, pairs)]
    ppermute x6 -> x7, starting transfers between devices: 10.1 us -> 14 us  [whole(): sent.append(lax.ppermute(piece, 'dp', ring))]
    ppermute x11 -> x17, waiting for transfers between devices: 10.3 us -> 6.72 us  [flipped(): return lax.ppermute(value, axis, pairs)]
  transfers between devices with their start and end apart: 20 -> 27, of which waited for: 10 -> 11; matrix products, arithmetic and copies ran while one was open for 20% -> 0% of each run, Pallas kernels for 0% -> 9%
where the time goes in v2:
time: 76 us; the launch traced here: 75.8 us
  waiting for transfers between devices  35.2 us (46%)
  starting transfers between devices  28.6 us (38%)
  Pallas kernels  10.8 us (14%)
    ppermute x7, waiting for transfers between devices, whole(): sent.append(lax.ppermute(piece, 'dp', ring))  21 us
    ppermute x7, starting transfers between devices, whole(): sent.append(lax.ppermute(piece, 'dp', ring))  14 us
    pallas_call x11, Pallas kernels, kernel(): pl.pallas_call(body, out_shape=out, in_specs=specs, out_specs=jax.tree.ma...  10.8 us
    ppermute x17, starting transfers between devices, flipped(): return lax.ppermute(value, axis, pairs)  10 us
    ppermute x3, waiting for transfers between devices, flipped_both(): return lax.ppermute(value, ('dp', 'ctx'), pairs)  7.42 us
    ppermute x17, waiting for transfers between devices, flipped(): return lax.ppermute(value, axis, pairs)  6.72 us
    ppermute x3, starting transfers between devices, flipped_both(): return lax.ppermute(value, ('dp', 'ctx'), pairs)  4.6 us
  transfers between devices with their start and end apart: 27, of which 11 were waited for; matrix products, arithmetic and copies ran while one was open for 0% of the time, Pallas kernels for 9%

profile of v2, /device:TPU:0, one launch (start us, length us, event | category | flops | bytes accessed | tf_op | source)
XLA Modules:
  0.0 75.8 jit_solution(336727450671918063)
XLA Ops:
  0.0 0.1 pad_add_fusion.ids_ref
  0.1 2.0 %shard_map.64 = (bf16[512,256]{1,0:T(8,128)(2,1)S(1)}, bf16[4,128,512]{2,1,0:T(8,128)(2,1)S(1)}, bf16[4,128,512]{2,1,0:T(8,128)(2,1)S(1)}) custom-call(s32[2]{0:T(128)S(1)} %pad_add_fusion.ids_ref, bf16[128,4096]{1,0:T(8,128)(2,1)} %bitcast.15, bf16[512,128]{1,0:T(8,128)(2,1)} %query_ref.1, bf16[512,128]{1,0:T(8,128)(2,1)} %key_ref.1), custom_call_target="tpu_custom_call" | custom-call | tf_op jit(solution)/shard_map/pallas_call | solution.py:67
  2.1 3.1 %collective-permute-start.5 = (bf16[4,128,512]{2,1,0:T(8,128)(2,1)S(1)}, bf16[4,128,512]{2,1,0:T(8,128)(2,1)S(1)}, u32[]{:S(2)}, u32[]{:S(2)}) collective-permute-start(bf16[4,128,512]{2,1,0:T(8,128)(2,1)S(1)} %get-tuple-element.36.refs_4_), channel_id=1, source_target_pairs={{0,2},{1,3},{2,0},{3,1},{4,6},{5,7},{6,4},{7,5},{8,10},{9,11},{10,... | collective-permute-start | bytes 1572872 | tf_op jit(solution)/shard_map/ppermute | solution.py:29
  5.1 1.5 %collective-permute-start = (bf16[4,128,512]{2,1,0:T(8,128)(2,1)S(1)}, bf16[4,128,512]{2,1,0:T(8,128)(2,1)S(1)}, u32[]{:S(2)}, u32[]{:S(2)}) collective-permute-start(bf16[4,128,512]{2,1,0:T(8,128)(2,1)S(1)} %get-tuple-element.35), channel_id=1, source_target_pairs={{0,4},{1,5},{2,6},{3,7},{4,0},{5,1},{6,2},{7,3},{8,12},{9,13},{10,... | collective-permute-start | bytes 1572872 | tf_op jit(solution)/shard_map/ppermute | solution.py:29
  6.6 0.0 collective-permute-start.2
  6.7 2.0 %collective-permute-start.7 = (bf16[512,256]{1,0:T(8,128)(2,1)S(1)}, bf16[512,256]{1,0:T(8,128)(2,1)S(1)}, u32[]{:S(2)}, u32[]{:S(2)}) collective-permute-start(bf16[512,256]{1,0:T(8,128)(2,1)S(1)} %get-tuple-element.37.refs_8_), channel_id=1, source_target_pairs={{0,8},{4,12},{8,24},{12,28},{24,16},{28,20},{16,0},{20,4},{1,9},{5... | collective-permute-start | bytes 786440 | tf_op jit(solution)/shard_map/ppermute | solution.py:367
  8.7 2.6 %collective-permute-start.8 = (bf16[512,256]{1,0:T(8,128)(2,1)S(1)}, bf16[512,256]{1,0:T(8,128)(2,1)S(1)}, u32[]{:S(2)}, u32[]{:S(2)}) collective-permute-start(bf16[512,256]{1,0:T(8,128)(2,1)S(1)} %copy-done), channel_id=1, source_target_pairs={{0,8},{4,12},{8,24},{12,28},{24,16},{28,20},{16,0},{20,4},{1,9},{5... | collective-permute-start | bytes 786440 | tf_op jit(solution)/shard_map/ppermute | solution.py:367
  11.3 5.6 %collective-permute-done.7.refs_10_ = bf16[512,256]{1,0:T(8,128)(2,1)S(1)} collective-permute-done((bf16[512,256]{1,0:T(8,128)(2,1)S(1)}, bf16[512,256]{1,0:T(8,128)(2,1)S(1)}, u32[]{:S(2)}, u32[]{:S(2)}) %collective-permute-start.7) | collective-permute-done | bytes 262176 | tf_op jit(solution)/shard_map/ppermute | solution.py:367
  16.9 0.0 collective-permute-start.4
  16.9 3.9 %collective-permute-done.8.refs_11_ = bf16[512,256]{1,0:T(8,128)(2,1)S(1)} collective-permute-done((bf16[512,256]{1,0:T(8,128)(2,1)S(1)}, bf16[512,256]{1,0:T(8,128)(2,1)S(1)}, u32[]{:S(2)}, u32[]{:S(2)}) %collective-permute-start.8) | collective-permute-done | bytes 262176 | tf_op jit(solution)/shard_map/ppermute | solution.py:367
  20.8 0.8 %collective-permute-start.9 = (bf16[512,256]{1,0:T(8,128)(2,1)S(1)}, bf16[512,256]{1,0:T(8,128)(2,1)S(1)}, u32[]{:S(2)}, u32[]{:S(2)}) collective-permute-start(bf16[512,256]{1,0:T(8,128)(2,1)S(1)} %collective-permute-done.7.refs_10_), channel_id=1, source_target_pairs={{0,8},{4,12},{8,24},{12,28},{24,16},{28,20},{16,0},{20,4},{1,9},{5... | collective-permute-start | bytes 786440 | tf_op jit(solution)/shard_map/ppermute | solution.py:367
  21.6 0.0 collective-permute-done.5.refs_6_
  21.6 0.0 collective-permute-start.6
  21.6 0.0 collective-permute-done.refs_0_
  21.6 0.5 collective-permute-start.1
  22.1 7.4 %collective-permute-done.2.refs_2_ = bf16[4,128,512]{2,1,0:T(8,128)(2,1)S(1)} collective-permute-done((bf16[4,128,512]{2,1,0:T(8,128)(2,1)S(1)}, bf16[4,128,512]{2,1,0:T(8,128)(2,1)S(1)}, u32[]{:S(2)}, u32[]{:S(2)}) %collective-permute-start.2) | collective-permute-done | bytes 524320 | tf_op jit(solution)/shard_map/ppermute | solution.py:29
  29.6 1.7 %collective-permute-start.10 = (bf16[512,256]{1,0:T(8,128)(2,1)S(1)}, bf16[512,256]{1,0:T(8,128)(2,1)S(1)}, u32[]{:S(2)}, u32[]{:S(2)}) collective-permute-start(bf16[512,256]{1,0:T(8,128)(2,1)S(1)} %collective-permute-done.8.refs_11_), channel_id=1, source_target_pairs={{0,8},{4,12},{8,24},{12,28},{24,16},{28,20},{16,0},{20,4},{1,9},{5... | collective-permute-start | bytes 786440 | tf_op jit(solution)/shard_map/ppermute | solution.py:367
  31.3 0.0 collective-permute-done.4.refs_5_
  31.3 2.6 %collective-permute-start.11 = (bf16[512,256]{1,0:T(8,128)(2,1)S(1)}, bf16[512,256]{1,0:T(8,128)(2,1)S(1)}, u32[]{:S(2)}, u32[]{:S(2)}) collective-permute-start(bf16[512,256]{1,0:T(8,128)(2,1)S(1)} %collective-permute-done.9.refs_12_), channel_id=1, source_target_pairs={{0,8},{4,12},{8,24},{12,28},{24,16},{28,20},{16,0},{20,4},{1,9},{5... | collective-permute-start | bytes 786440 | tf_op jit(solution)/shard_map/ppermute | solution.py:367
  33.9 5.8 %collective-permute-done.10.refs_13_.ref = bf16[512,256]{1,0:T(8,128)(2,1)S(1)} collective-permute-done((bf16[512,256]{1,0:T(8,128)(2,1)S(1)}, bf16[512,256]{1,0:T(8,128)(2,1)S(1)}, u32[]{:S(2)}, u32[]{:S(2)}) %collective-permute-start.10) | collective-permute-done | bytes 262176 | tf_op jit(solution)/shard_map/ppermute | solution.py:367
  39.6 0.0 collective-permute-done.6.refs_7_
  39.6 0.0 collective-permute-done.1.refs_1_
  39.7 0.0 collective-permute-done.3.refs_3_
  39.7 2.4 %shard_map.65 = (f32[512,512]{1,0:T(8,128)S(1)}, bf16[512,512]{1,0:T(8,128)(2,1)S(1)}, f32[512,512]{1,0:T(8,128)S(1)}, bf16[512,512]{1,0:T(8,128)(2,1)S(1)}) custom-call(s32[2]{0:T(128)S(1)} %pad_add_fusion.ids_ref, bf16[4,128,512]{2,1,0:T(8,128)(2,1)S(1)} %collective-permute-done.refs_0_, bf16[4,128,512]{2,1,0:T(8,128)(2,1)S(1)} %collective-permute-done.1.refs_1_, ...), custom_call_target="tpu_custom_call" | custom-call | tf_op jit(solution)/shard_map/pallas_call | solution.py:67
  42.1 2.8 %collective-permute-done.11.w = bf16[512,256]{1,0:T(8,128)(2,1)S(1)} collective-permute-done((bf16[512,256]{1,0:T(8,128)(2,1)S(1)}, bf16[512,256]{1,0:T(8,128)(2,1)S(1)}, u32[]{:S(2)}, u32[]{:S(2)}) %collective-permute-start.11) | collective-permute-done | bytes 262176 | tf_op jit(solution)/shard_map/ppermute | solution.py:367
  44.9 0.4 shard_map.66
  45.4 1.6 %collective-permute-start.12 = (f16[512,256]{1,0:T(8,128)(2,1)S(1)}, f16[512,256]{1,0:T(8,128)(2,1)S(1)}, u32[]{:S(2)}, u32[]{:S(2)}) collective-permute-start(f16[512,256]{1,0:T(8,128)(2,1)S(1)} %convert_element_type.27), channel_id=1, source_target_pairs={{0,4},{4,0},{8,12},{12,8},{16,20},{20,16},{24,28},{28,24},{1,5},{5... | collective-permute-start | bytes 786440 | tf_op jit(solution)/shard_map/ppermute | solution.py:20
  47.0 0.8 %collective-permute-start.16 = (bf16[512,128]{1,0:T(8,128)(2,1)S(1)}, bf16[512,128]{1,0:T(8,128)(2,1)S(1)}, u32[]{:S(2)}, u32[]{:S(2)}) collective-permute-start(bf16[512,128]{1,0:T(8,128)(2,1)S(1)} %get-tuple-element.54), channel_id=1, source_target_pairs={{0,8},{4,12},{8,24},{12,28},{24,16},{28,20},{16,0},{20,4},{1,9},{5... | collective-permute-start | bytes 393224 | tf_op jit(solution)/shard_map/ppermute | solution.py:367
  47.9 3.4 %collective-permute-start.14 = (bf16[512,128]{1,0:T(8,128)(2,1)S(1)}, bf16[512,128]{1,0:T(8,128)(2,1)S(1)}, u32[]{:S(2)}, u32[]{:S(2)}) collective-permute-start(bf16[512,128]{1,0:T(8,128)(2,1)S(1)} %get-tuple-element.49), channel_id=1, source_target_pairs={{0,8},{4,12},{8,24},{12,28},{24,16},{28,20},{16,0},{20,4},{1,9},{5... | collective-permute-start | bytes 393224 | tf_op jit(solution)/shard_map/ppermute | solution.py:367
  51.3 2.9 %collective-permute-done.16.w = bf16[512,128]{1,0:T(8,128)(2,1)S(1)} collective-permute-done((bf16[512,128]{1,0:T(8,128)(2,1)S(1)}, bf16[512,128]{1,0:T(8,128)(2,1)S(1)}, u32[]{:S(2)}, u32[]{:S(2)}) %collective-permute-start.16) | collective-permute-done | bytes 131104 | tf_op jit(solution)/shard_map/ppermute | solution.py:367
  54.2 0.4 shard_map.72
  54.6 0.6 collective-permute-start.17
  55.3 0.1 add_convert_fusion.mine
  55.4 0.0 copy-start.1
  55.4 0.0 copy-start.2
  55.5 0.1 collective-permute-start.13
  55.5 0.6 copy-done.2
  56.1 0.0 collective-permute-start.24
  56.1 1.5 %collective-permute-start.25 = (f32[1,256]{1,0:T(1,128)S(1)}, f32[1,256]{1,0:T(1,128)S(1)}, u32[]{:S(2)}, u32[]{:S(2)}) collective-permute-start(f32[1,256]{1,0:T(1,128)S(1)} %bitcast.12), channel_id=1, source_target_pairs={{0,2},{1,3},{2,0},{3,1},{4,6},{5,7},{6,4},{7,5},{8,10},{9,11},{10,... | collective-permute-start | bytes 3080 | tf_op jit(solution)/shard_map/ppermute | solution.py:20
  57.6 1.3 %shard_map.67 = (f32[1,1,512]{2,1,0:T(1,128)S(1)}, f32[1,512,1]{2,1,0:T(8,128)S(1)}, f32[1,1]{1,0:T(1,128)}, s32[1,512]{1,0:T(1,128)S(1)}, s32[512,1]{1,0:T(8,128)S(1)}) custom-call(s32[2]{0:T(128)S(1)} %pad_add_fusion.ids_ref, f32[2,512]{1,0:T(2,128)S(1)} %bitcast.9), custom_call_target="tpu_custom_call" | custom-call | tf_op jit(solution)/shard_map/pallas_call | solution.py:67
  58.9 0.0 collective-permute-done.14.w
  58.9 0.4 collective-permute-start.26
  59.3 0.4 shard_map.70
  59.8 0.0 collective-permute-done.17
  59.8 1.5 %collective-permute-start.15 = (f16[512,128]{1,0:T(8,128)(2,1)S(1)}, f16[512,128]{1,0:T(8,128)(2,1)S(1)}, u32[]{:S(2)}, u32[]{:S(2)}) collective-permute-start(f16[512,128]{1,0:T(8,128)(2,1)S(1)} %convert_element_type.30), channel_id=1, source_target_pairs={{0,4},{4,0},{8,12},{12,8},{16,20},{20,16},{24,28},{28,24},{1,5},{5... | collective-permute-start | bytes 393224 | tf_op jit(solution)/shard_map/ppermute | solution.py:20
  61.4 0.0 collective-permute-done.13.other
  61.4 1.5 %shard_map.68 = (bf16[512,512]{1,0:T(8,128)(2,1)S(1)}, f32[512,128]{1,0:T(8,128)S(1)}, f32[512,128]{1,0:T(8,128)S(1)}) custom-call(bf16[512,256]{1,0:T(8,128)(2,1)S(1)} %add_convert_fusion.mine, bf16[512,256]{1,0:T(8,128)(2,1)S(1)} %collective-permute-done.13.other, f32[1,512]{1,0:T(1,128)S(1)} %bitcast.10, f32[512,1]{1,0:T(8,128)S(1)} %bitcast.8, ...), custom_call_target="tpu_custom_call" | custom-call | tf_op jit(solution)/shard_map/pallas_call | solution.py:67
  62.9 0.3 shard_map.73
  63.1 0.1 collective-permute-start.19
  63.2 2.3 %collective-permute-done.15 = f16[512,128]{1,0:T(8,128)(2,1)S(1)} collective-permute-done((f16[512,128]{1,0:T(8,128)(2,1)S(1)}, f16[512,128]{1,0:T(8,128)(2,1)S(1)}, u32[]{:S(2)}, u32[]{:S(2)}) %collective-permute-start.15) | collective-permute-done | bytes 131104 | tf_op jit(solution)/shard_map/ppermute | solution.py:20
  65.6 1.5 %collective-permute-start.21 = (f32[128,128]{1,0:T(8,128)S(1)}, f32[128,128]{1,0:T(8,128)S(1)}, u32[]{:S(2)}, u32[]{:S(2)}) collective-permute-start(f32[128,128]{1,0:T(8,128)S(1)} %get-tuple-element.62), channel_id=1, source_target_pairs={{0,2},{1,3},{2,0},{3,1},{4,6},{5,7},{6,4},{7,5},{8,10},{9,11},{10,... | collective-permute-start | bytes 196616 | tf_op jit(solution)/shard_map/ppermute | solution.py:20
  67.1 0.3 shard_map.71
  67.4 0.0 collective-permute-done.24.refs_9_
  67.4 0.1 collective-permute-start.23
  67.5 0.6 collective-permute-start.18
  68.2 0.0 collective-permute-done.26.refs_11_
  68.2 1.5 %collective-permute-start.20 = (f32[128,128]{1,0:T(8,128)S(1)}, f32[128,128]{1,0:T(8,128)S(1)}, u32[]{:S(2)}, u32[]{:S(2)}) collective-permute-start(f32[128,128]{1,0:T(8,128)S(1)} %get-tuple-element.61), channel_id=1, source_target_pairs={{0,2},{1,3},{2,0},{3,1},{4,6},{5,7},{6,4},{7,5},{8,10},{9,11},{10,... | collective-permute-start | bytes 196616 | tf_op jit(solution)/shard_map/ppermute | solution.py:20
  69.7 0.0 collective-permute-start.22
  69.7 0.3 collective-permute-done.21.refs_5_
  69.9 1.4 %collective-permute-done.23.refs_7_ = f32[128,128]{1,0:T(8,128)S(1)} collective-permute-done((f32[128,128]{1,0:T(8,128)S(1)}, f32[128,128]{1,0:T(8,128)S(1)}, u32[]{:S(2)}, u32[]{:S(2)}) %collective-permute-start.23) | collective-permute-done | bytes 65568 | tf_op jit(solution)/shard_map/ppermute | solution.py:20
  71.3 0.0 collective-permute-done.18.refs_2_
  71.3 1.5 %collective-permute-done.20.refs_4_ = f32[128,128]{1,0:T(8,128)S(1)} collective-permute-done((f32[128,128]{1,0:T(8,128)S(1)}, f32[128,128]{1,0:T(8,128)S(1)}, u32[]{:S(2)}, u32[]{:S(2)}) %collective-permute-start.20) | collective-permute-done | bytes 65568 | tf_op jit(solution)/shard_map/ppermute | solution.py:20
  72.8 1.2 %collective-permute-done.22.refs_6_ = f32[128,128]{1,0:T(8,128)S(1)} collective-permute-done((f32[128,128]{1,0:T(8,128)S(1)}, f32[128,128]{1,0:T(8,128)S(1)}, u32[]{:S(2)}, u32[]{:S(2)}) %collective-permute-start.22) | collective-permute-done | bytes 65568 | tf_op jit(solution)/shard_map/ppermute | solution.py:20
  74.0 1.8 %shard_map.74 = bf16[128,1024]{1,0:T(8,128)(2,1)} custom-call(s32[2]{0:T(128)S(1)} %pad_add_fusion.ids_ref, f32[128,128]{1,0:T(8,128)S(1)} %get-tuple-element.53.refs_0_, f32[128,128]{1,0:T(8,128)S(1)} %get-tuple-element.58.refs_1_, f32[128,128]{1,0:T(8,128)S(1)} %collective-permute-done.18.refs_2_, f32[128,128]{1,0:T(8,128)S(1)} %collective-permute-done.19.refs_3_, ...), custom_call_target="tpu_custom_call" | custom-call | tf_op jit(solution)/shard_map/pallas_call | solution.py:67
  (17 shorter events, 0.3 us)
Async XLA Ops:
  0.1 8.6 %copy-start = (bf16[512,256]{1,0:T(8,128)(2,1)S(1)}, bf16[512,256]{1,0:T(8,128)(2,1)}, u32[]{:S(2)}) copy-start(bf16[512,256]{1,0:T(8,128)(2,1)} %refs_9_.1) | copy-start | bytes 786436
  2.1 19.5 %collective-permute-start.5 = (bf16[4,128,512]{2,1,0:T(8,128)(2,1)S(1)}, bf16[4,128,512]{2,1,0:T(8,128)(2,1)S(1)}, u32[]{:S(2)}, u32[]{:S(2)}) collective-permute-start(bf16[4,128,512]{2,1,0:T(8,128)(2,1)S(1)} %get-tuple-element.36.refs_4_), channel_id=1, source_target_pairs={{0,2},{1,3},{2,0},{3,1},{4,6},{5,7},{6,4},{7,5},{8,10},{9,11},{10,... | collective-permute-start | bytes 1572872 | tf_op jit(solution)/shard_map/ppermute | solution.py:29
  5.1 16.5 %collective-permute-start = (bf16[4,128,512]{2,1,0:T(8,128)(2,1)S(1)}, bf16[4,128,512]{2,1,0:T(8,128)(2,1)S(1)}, u32[]{:S(2)}, u32[]{:S(2)}) collective-permute-start(bf16[4,128,512]{2,1,0:T(8,128)(2,1)S(1)} %get-tuple-element.35), channel_id=1, source_target_pairs={{0,4},{1,5},{2,6},{3,7},{4,0},{5,1},{6,2},{7,3},{8,12},{9,13},{10,... | collective-permute-start | bytes 1572872 | tf_op jit(solution)/shard_map/ppermute | solution.py:29
  6.6 22.9 %collective-permute-start.2 = (bf16[4,128,512]{2,1,0:T(8,128)(2,1)S(1)}, bf16[4,128,512]{2,1,0:T(8,128)(2,1)S(1)}, u32[]{:S(2)}, u32[]{:S(2)}) collective-permute-start(bf16[4,128,512]{2,1,0:T(8,128)(2,1)S(1)} %get-tuple-element.35), channel_id=1, source_target_pairs={{0,6},{1,7},{2,4},{3,5},{4,2},{5,3},{6,0},{7,1},{8,14},{9,15},{10,... | collective-permute-start | bytes 1572872 | tf_op jit(solution)/shard_map/ppermute | solution.py:29
  6.7 10.2 %collective-permute-start.7 = (bf16[512,256]{1,0:T(8,128)(2,1)S(1)}, bf16[512,256]{1,0:T(8,128)(2,1)S(1)}, u32[]{:S(2)}, u32[]{:S(2)}) collective-permute-start(bf16[512,256]{1,0:T(8,128)(2,1)S(1)} %get-tuple-element.37.refs_8_), channel_id=1, source_target_pairs={{0,8},{4,12},{8,24},{12,28},{24,16},{28,20},{16,0},{20,4},{1,9},{5... | collective-permute-start | bytes 786440 | tf_op jit(solution)/shard_map/ppermute | solution.py:367
  8.7 12.1 %collective-permute-start.8 = (bf16[512,256]{1,0:T(8,128)(2,1)S(1)}, bf16[512,256]{1,0:T(8,128)(2,1)S(1)}, u32[]{:S(2)}, u32[]{:S(2)}) collective-permute-start(bf16[512,256]{1,0:T(8,128)(2,1)S(1)} %copy-done), channel_id=1, source_target_pairs={{0,8},{4,12},{8,24},{12,28},{24,16},{28,20},{16,0},{20,4},{1,9},{5... | collective-permute-start | bytes 786440 | tf_op jit(solution)/shard_map/ppermute | solution.py:367
  16.9 14.4 %collective-permute-start.4 = (bf16[4,128,512]{2,1,0:T(8,128)(2,1)S(1)}, bf16[4,128,512]{2,1,0:T(8,128)(2,1)S(1)}, u32[]{:S(2)}, u32[]{:S(2)}) collective-permute-start(bf16[4,128,512]{2,1,0:T(8,128)(2,1)S(1)} %get-tuple-element.36.refs_4_), channel_id=1, source_target_pairs={{0,1},{1,0},{2,3},{3,2},{4,5},{5,4},{6,7},{7,6},{8,9},{9,8},{10,11... | collective-permute-start | bytes 1572872 | tf_op jit(solution)/shard_map/ppermute | solution.py:20
  20.8 8.8 %collective-permute-start.9 = (bf16[512,256]{1,0:T(8,128)(2,1)S(1)}, bf16[512,256]{1,0:T(8,128)(2,1)S(1)}, u32[]{:S(2)}, u32[]{:S(2)}) collective-permute-start(bf16[512,256]{1,0:T(8,128)(2,1)S(1)} %collective-permute-done.7.refs_10_), channel_id=1, source_target_pairs={{0,8},{4,12},{8,24},{12,28},{24,16},{28,20},{16,0},{20,4},{1,9},{5... | collective-permute-start | bytes 786440 | tf_op jit(solution)/shard_map/ppermute | solution.py:367
  21.6 18.0 %collective-permute-start.6 = (bf16[4,128,512]{2,1,0:T(8,128)(2,1)S(1)}, bf16[4,128,512]{2,1,0:T(8,128)(2,1)S(1)}, u32[]{:S(2)}, u32[]{:S(2)}) collective-permute-start(bf16[4,128,512]{2,1,0:T(8,128)(2,1)S(1)} %collective-permute-done.5.refs_6_), channel_id=1, source_target_pairs={{0,1},{1,0},{2,3},{3,2},{4,5},{5,4},{6,7},{7,6},{8,9},{9,8},{10,11... | collective-permute-start | bytes 1572872 | tf_op jit(solution)/shard_map/ppermute | solution.py:20
  21.6 18.0 %collective-permute-start.1 = (bf16[4,128,512]{2,1,0:T(8,128)(2,1)S(1)}, bf16[4,128,512]{2,1,0:T(8,128)(2,1)S(1)}, u32[]{:S(2)}, u32[]{:S(2)}) collective-permute-start(bf16[4,128,512]{2,1,0:T(8,128)(2,1)S(1)} %collective-permute-done.refs_0_), channel_id=1, source_target_pairs={{0,1},{1,0},{2,3},{3,2},{4,5},{5,4},{6,7},{7,6},{8,9},{9,8},{10,11... | collective-permute-start | bytes 1572872 | tf_op jit(solution)/shard_map/ppermute | solution.py:20
  29.6 10.1 %collective-permute-start.3 = (bf16[4,128,512]{2,1,0:T(8,128)(2,1)S(1)}, bf16[4,128,512]{2,1,0:T(8,128)(2,1)S(1)}, u32[]{:S(2)}, u32[]{:S(2)}) collective-permute-start(bf16[4,128,512]{2,1,0:T(8,128)(2,1)S(1)} %collective-permute-done.2.refs_2_), channel_id=1, source_target_pairs={{0,1},{1,0},{2,3},{3,2},{4,5},{5,4},{6,7},{7,6},{8,9},{9,8},{10,11... | collective-permute-start | bytes 1572872 | tf_op jit(solution)/shard_map/ppermute | solution.py:20
  29.6 10.1 %collective-permute-start.10 = (bf16[512,256]{1,0:T(8,128)(2,1)S(1)}, bf16[512,256]{1,0:T(8,128)(2,1)S(1)}, u32[]{:S(2)}, u32[]{:S(2)}) collective-permute-start(bf16[512,256]{1,0:T(8,128)(2,1)S(1)} %collective-permute-done.8.refs_11_), channel_id=1, source_target_pairs={{0,8},{4,12},{8,24},{12,28},{24,16},{28,20},{16,0},{20,4},{1,9},{5... | collective-permute-start | bytes 786440 | tf_op jit(solution)/shard_map/ppermute | solution.py:367
  31.3 13.6 %collective-permute-start.11 = (bf16[512,256]{1,0:T(8,128)(2,1)S(1)}, bf16[512,256]{1,0:T(8,128)(2,1)S(1)}, u32[]{:S(2)}, u32[]{:S(2)}) collective-permute-start(bf16[512,256]{1,0:T(8,128)(2,1)S(1)} %collective-permute-done.9.refs_12_), channel_id=1, source_target_pairs={{0,8},{4,12},{8,24},{12,28},{24,16},{28,20},{16,0},{20,4},{1,9},{5... | collective-permute-start | bytes 786440 | tf_op jit(solution)/shard_map/ppermute | solution.py:367
  45.4 9.9 %collective-permute-start.12 = (f16[512,256]{1,0:T(8,128)(2,1)S(1)}, f16[512,256]{1,0:T(8,128)(2,1)S(1)}, u32[]{:S(2)}, u32[]{:S(2)}) collective-permute-start(f16[512,256]{1,0:T(8,128)(2,1)S(1)} %convert_element_type.27), channel_id=1, source_target_pairs={{0,4},{4,0},{8,12},{12,8},{16,20},{20,16},{24,28},{28,24},{1,5},{5... | collective-permute-start | bytes 786440 | tf_op jit(solution)/shard_map/ppermute | solution.py:20
  47.0 7.1 %collective-permute-start.16 = (bf16[512,128]{1,0:T(8,128)(2,1)S(1)}, bf16[512,128]{1,0:T(8,128)(2,1)S(1)}, u32[]{:S(2)}, u32[]{:S(2)}) collective-permute-start(bf16[512,128]{1,0:T(8,128)(2,1)S(1)} %get-tuple-element.54), channel_id=1, source_target_pairs={{0,8},{4,12},{8,24},{12,28},{24,16},{28,20},{16,0},{20,4},{1,9},{5... | collective-permute-start | bytes 393224 | tf_op jit(solution)/shard_map/ppermute | solution.py:367
  47.9 11.0 %collective-permute-start.14 = (bf16[512,128]{1,0:T(8,128)(2,1)S(1)}, bf16[512,128]{1,0:T(8,128)(2,1)S(1)}, u32[]{:S(2)}, u32[]{:S(2)}) collective-permute-start(bf16[512,128]{1,0:T(8,128)(2,1)S(1)} %get-tuple-element.49), channel_id=1, source_target_pairs={{0,8},{4,12},{8,24},{12,28},{24,16},{28,20},{16,0},{20,4},{1,9},{5... | collective-permute-start | bytes 393224 | tf_op jit(solution)/shard_map/ppermute | solution.py:367
  54.6 5.1 %collective-permute-start.17 = (f16[512,128]{1,0:T(8,128)(2,1)S(1)}, f16[512,128]{1,0:T(8,128)(2,1)S(1)}, u32[]{:S(2)}, u32[]{:S(2)}) collective-permute-start(f16[512,128]{1,0:T(8,128)(2,1)S(1)} %convert_element_type.33), channel_id=1, source_target_pairs={{0,4},{4,0},{8,12},{12,8},{16,20},{20,16},{24,28},{28,24},{1,5},{5... | collective-permute-start | bytes 393224 | tf_op jit(solution)/shard_map/ppermute | solution.py:20
  55.4 2.2 %copy-start.1 = (f32[1,2,512]{2,1,0:T(2,128)S(1)}, f32[1,2,512]{2,1,0:T(2,128)}, u32[]{:S(2)}) copy-start(f32[1,2,512]{2,1,0:T(2,128)} %param.10) | copy-start | bytes 12292
  55.4 0.7 copy-start.2
  55.5 5.9 %collective-permute-start.13 = (bf16[512,256]{1,0:T(8,128)(2,1)S(1)}, bf16[512,256]{1,0:T(8,128)(2,1)S(1)}, u32[]{:S(2)}, u32[]{:S(2)}) collective-permute-start(bf16[512,256]{1,0:T(8,128)(2,1)S(1)} %pad_maximum_fusion), channel_id=1, source_target_pairs={{0,1},{1,0},{2,3},{3,2},{4,5},{5,4},{6,7},{7,6},{8,9},{9,8},{10,11... | collective-permute-start | bytes 786440 | tf_op jit(solution)/shard_map/ppermute | solution.py:20
  56.1 11.3 %collective-permute-start.24 = (f32[1,256]{1,0:T(1,128)S(1)}, f32[1,256]{1,0:T(1,128)S(1)}, u32[]{:S(2)}, u32[]{:S(2)}) collective-permute-start(f32[1,256]{1,0:T(1,128)S(1)} %bitcast.11), channel_id=1, source_target_pairs={{0,1},{1,0},{2,3},{3,2},{4,5},{5,4},{6,7},{7,6},{8,9},{9,8},{10,11... | collective-permute-start | bytes 3080 | tf_op jit(solution)/shard_map/ppermute | solution.py:20
  56.1 11.4 %collective-permute-start.25 = (f32[1,256]{1,0:T(1,128)S(1)}, f32[1,256]{1,0:T(1,128)S(1)}, u32[]{:S(2)}, u32[]{:S(2)}) collective-permute-start(f32[1,256]{1,0:T(1,128)S(1)} %bitcast.12), channel_id=1, source_target_pairs={{0,2},{1,3},{2,0},{3,1},{4,6},{5,7},{6,4},{7,5},{8,10},{9,11},{10,... | collective-permute-start | bytes 3080 | tf_op jit(solution)/shard_map/ppermute | solution.py:20
  58.9 9.2 %collective-permute-start.26 = (f32[1,256]{1,0:T(1,128)S(1)}, f32[1,256]{1,0:T(1,128)S(1)}, u32[]{:S(2)}, u32[]{:S(2)}) collective-permute-start(f32[1,256]{1,0:T(1,128)S(1)} %bitcast.13), channel_id=1, source_target_pairs={{0,3},{1,2},{2,1},{3,0},{4,7},{5,6},{6,5},{7,4},{8,11},{9,10},{10,... | collective-permute-start | bytes 3080 | tf_op jit(solution)/shard_map/ppermute | solution.py:20
  59.8 5.8 %collective-permute-start.15 = (f16[512,128]{1,0:T(8,128)(2,1)S(1)}, f16[512,128]{1,0:T(8,128)(2,1)S(1)}, u32[]{:S(2)}, u32[]{:S(2)}) collective-permute-start(f16[512,128]{1,0:T(8,128)(2,1)S(1)} %convert_element_type.30), channel_id=1, source_target_pairs={{0,4},{4,0},{8,12},{12,8},{16,20},{20,16},{24,28},{28,24},{1,5},{5... | collective-permute-start | bytes 393224 | tf_op jit(solution)/shard_map/ppermute | solution.py:20
  63.1 6.5 %collective-permute-start.19 = (f32[128,128]{1,0:T(8,128)S(1)}, f32[128,128]{1,0:T(8,128)S(1)}, u32[]{:S(2)}, u32[]{:S(2)}) collective-permute-start(f32[128,128]{1,0:T(8,128)S(1)} %get-tuple-element.60), channel_id=1, source_target_pairs={{0,1},{1,0},{2,3},{3,2},{4,5},{5,4},{6,7},{7,6},{8,9},{9,8},{10,11... | collective-permute-start | bytes 196616 | tf_op jit(solution)/shard_map/ppermute | solution.py:20
  65.6 4.3 %collective-permute-start.21 = (f32[128,128]{1,0:T(8,128)S(1)}, f32[128,128]{1,0:T(8,128)S(1)}, u32[]{:S(2)}, u32[]{:S(2)}) collective-permute-start(f32[128,128]{1,0:T(8,128)S(1)} %get-tuple-element.62), channel_id=1, source_target_pairs={{0,2},{1,3},{2,0},{3,1},{4,6},{5,7},{6,4},{7,5},{8,10},{9,11},{10,... | collective-permute-start | bytes 196616 | tf_op jit(solution)/shard_map/ppermute | solution.py:20
  67.4 3.9 %collective-permute-start.23 = (f32[128,128]{1,0:T(8,128)S(1)}, f32[128,128]{1,0:T(8,128)S(1)}, u32[]{:S(2)}, u32[]{:S(2)}) collective-permute-start(f32[128,128]{1,0:T(8,128)S(1)} %get-tuple-element.64), channel_id=1, source_target_pairs={{0,3},{1,2},{2,1},{3,0},{4,7},{5,6},{6,5},{7,4},{8,11},{9,10},{10,... | collective-permute-start | bytes 196616 | tf_op jit(solution)/shard_map/ppermute | solution.py:20
  67.5 3.8 %collective-permute-start.18 = (f32[128,128]{1,0:T(8,128)S(1)}, f32[128,128]{1,0:T(8,128)S(1)}, u32[]{:S(2)}, u32[]{:S(2)}) collective-permute-start(f32[128,128]{1,0:T(8,128)S(1)} %get-tuple-element.59), channel_id=1, source_target_pairs={{0,1},{1,0},{2,3},{3,2},{4,5},{5,4},{6,7},{7,6},{8,9},{9,8},{10,11... | collective-permute-start | bytes 196616 | tf_op jit(solution)/shard_map/ppermute | solution.py:20
  68.2 4.6 %collective-permute-start.20 = (f32[128,128]{1,0:T(8,128)S(1)}, f32[128,128]{1,0:T(8,128)S(1)}, u32[]{:S(2)}, u32[]{:S(2)}) collective-permute-start(f32[128,128]{1,0:T(8,128)S(1)} %get-tuple-element.61), channel_id=1, source_target_pairs={{0,2},{1,3},{2,0},{3,1},{4,6},{5,7},{6,4},{7,5},{8,10},{9,11},{10,... | collective-permute-start | bytes 196616 | tf_op jit(solution)/shard_map/ppermute | solution.py:20
  69.7 4.4 %collective-permute-start.22 = (f32[128,128]{1,0:T(8,128)S(1)}, f32[128,128]{1,0:T(8,128)S(1)}, u32[]{:S(2)}, u32[]{:S(2)}) collective-permute-start(f32[128,128]{1,0:T(8,128)S(1)} %get-tuple-element.63), channel_id=1, source_target_pairs={{0,3},{1,2},{2,1},{3,0},{4,7},{5,6},{6,5},{7,4},{8,11},{9,10},{10,... | collective-permute-start | bytes 196616 | tf_op jit(solution)/shard_map/ppermute | solution.py:20

commit v3 on v2

--- a/solution.py
+++ b/solution.py
@@ -174,10 +174,10 @@
     return kernel(body, [pltpu.VMEM((width, half), weight.dtype)] * 2, [weight])
 
 
-def mixed(ids, sides, stages):
+def mixed(ids, side, stages):
     steps = len(stages)
-    count = len(sides[0])
-    _, chunk, width = sides[0][0].shape
+    count = len(side)
+    _, chunk, width = side[0].shape
     parts = [w.shape[1] for w in stages[0]]
     cuts = [sum(parts[:i]) for i in range(len(parts))]
     length = count * chunk
@@ -185,58 +185,46 @@
     def body(ids_ref, *refs):
         turn = turn_of(ids_ref[0] // 2, steps + 1)
         sources = [place_at((turn + steps + 1 - step) % (steps + 1), steps + 1) for step in range(steps + 1)]
-        at = 0
-        pieces = []
-        for _ in sides:
-            pieces.append(refs[at : at + count])
-            at += count
-        weights = []
-        for _ in range(steps):
-            weights.append(refs[at : at + len(parts)])
-            at += len(parts)
-        for side in pieces:
-            total_ref, last = refs[at : at + 2]
-            at += 2
-            for m in range(0, count, 2):
-
-                def rows(step):
-                    return jnp.concatenate(
-                        [side[m][sources[step]], side[m + 1][sources[step]]], axis=0
-                    )
-
-                span = pl.ds(m * chunk, 2 * chunk)
-                for part, cut in zip(range(len(parts)), cuts):
-                    total = None
-                    for step in range(steps):
-                        product = dot32(rows(step), weights[step][part][...])
-                        total = product if total is None else total + product
-                    total_ref[span, cut : cut + parts[part]] = total
-                last[span, :] = rows(steps)
-
-    outs = kernel(
+        total_ref, last = refs[-2:]
+        pieces = refs[:count]
+        weights = [
+            refs[count + step * len(parts) : count + (step + 1) * len(parts)]
+            for step in range(steps)
+        ]
+        for m in range(0, count, 2):
+
+            def rows(step):
+                return jnp.concatenate(
+                    [pieces[m][sources[step]], pieces[m + 1][sources[step]]], axis=0
+                )
+
+            span = pl.ds(m * chunk, 2 * chunk)
+            for part, cut in enumerate(cuts):
+                total = None
+                for step in range(steps):
+                    product = dot32(rows(step), weights[step][part][...])
+                    total = product if total is None else total + product
+                total_ref[span, cut : cut + parts[part]] = total
+            last[span, :] = rows(steps)
+
+    return kernel(
         body,
         [
             pltpu.VMEM((length, sum(parts)), jnp.float32),
             pltpu.VMEM((length, width), jnp.bfloat16),
-        ]
-        * len(sides),
-        [piece for side in sides for piece in side] + [w for step in stages for w in step],
+        ],
+        list(side) + [w for step in stages for w in step],
         scalars=ids,
     )
-    return outs[:2], outs[2:]
-
-
-def projected(away, kept, weight, cut, scale):
-    (length, _), part = away[0].shape, weight.shape[1]
-
-    def body(away_total, away_last, kept_total, kept_last, w, away_out, kept_out):
-        columns = w[...]
-        span = slice(cut, cut + part)
-        gone = away_total[:, span] + dot32(away_last[...], columns)
-        away_out[...] = gone * scale
-        kept_out[...] = kept_total[:, span] + dot32(kept_last[...], columns)
-
-    return kernel(body, [pltpu.VMEM((length, part), jnp.float32)] * 2, [*away, *kept, weight])
+
+
+def projected(side, weight, cut, factor):
+    (length, _), part = side[0].shape, weight.shape[1]
+
+    def body(total, last, w, out):
+        out[...] = (total[:, cut : cut + part] + dot32(last[...], w[...])) * factor
+
+    return kernel(body, pltpu.VMEM((length, part), jnp.float32), [*side, weight])
 
 
 def joined(kept, came, scale):
@@ -314,10 +302,10 @@
         gain_refs = refs[count * groups : count * groups + count]
         for m in range(0, count, 2):
             mine = [refs[i] for i in range(m * groups, (m + 2) * groups)]
-            total = sum(jnp.sum(ref[...], axis=1, keepdims=True) for ref in mine)
+            total = jnp.sum(sum(ref[...] for ref in mine), axis=1, keepdims=True)
             average = total / (2 * wide)
             centered = [ref[...] - average for ref in mine]
-            squares = sum(jnp.sum(c * c, axis=1, keepdims=True) for c in centered)
+            squares = jnp.sum(sum(c * c for c in centered), axis=1, keepdims=True)
             rate = lax.rsqrt(squares / (2 * wide) + norm_eps)
             for i, c in enumerate(centered):
                 which = m + i // groups
@@ -384,14 +372,16 @@
     for m in range(1, ctx):
         gains.append(flipped(group_gain[None], "ctx", m))
 
-    away, kept = mixed(ids, (away_rows, own_rows), stages)
+    away = mixed(ids, away_rows, stages)
+    kept = mixed(ids, own_rows, stages)
 
     limit = TOKEN_MOST * WEIGHT_MOST * outer * width
     scale = 2.0 ** math.floor(math.log2(65504.0 / limit))
     stays = []
     cut = 0
     for weight in held:
-        gone, stay = projected(away, kept, weight, cut, scale)
+        gone = projected(away, weight, cut, scale)
+        stay = projected(kept, weight, cut, 1.0)
         cut += weight.shape[1]
         stays.append((stay, flipped(gone.astype(jnp.float16), "dp", 1)))
 

time: 76 us -> 70.5 us (0.928)
  waiting for transfers between devices: 35.2 us -> 31.7 us
  starting transfers between devices: 28.6 us -> 25.7 us
  Pallas kernels: 10.8 us -> 11.7 us
    ppermute x7, starting transfers between devices: 14 us -> 10.7 us  [whole(): sent.append(lax.ppermute(piece, 'dp', ring))]
    ppermute x7, waiting for transfers between devices: 21 us -> 18.9 us  [whole(): sent.append(lax.ppermute(piece, 'dp', ring))]
    ppermute x3, waiting for transfers between devices: 7.42 us -> 6.43 us  [flipped_both(): return lax.ppermute(value, ('dp', 'ctx'), pairs)]
    pallas_call x11 -> x15, Pallas kernels: 10.8 us -> 11.7 us  [kernel(): pl.pallas_call(body, out_shape=out, in_specs=specs, out_specs=jax.tree.ma...]
  transfers between devices with their start and end apart: 27 -> 27, of which waited for: 11 -> 11; matrix products, arithmetic and copies ran while one was open for 0% -> 0% of each run, Pallas kernels for 9% -> 12%
where the time goes in v3:
time: 70.5 us; the launch traced here: 70.3 us
  waiting for transfers between devices  31.7 us (45%)
  starting transfers between devices  25.7 us (36%)
  Pallas kernels  11.7 us (17%)
    ppermute x7, waiting for transfers between devices, whole(): sent.append(lax.ppermute(piece, 'dp', ring))  18.9 us
    pallas_call x15, Pallas kernels, kernel(): pl.pallas_call(body, out_shape=out, in_specs=specs, out_specs=jax.tree.ma...  11.7 us
    ppermute x7, starting transfers between devices, whole(): sent.append(lax.ppermute(piece, 'dp', ring))  10.7 us
    ppermute x17, starting transfers between devices, flipped(): return lax.ppermute(value, axis, pairs)  9.91 us
    ppermute x3, waiting for transfers between devices, flipped_both(): return lax.ppermute(value, ('dp', 'ctx'), pairs)  6.43 us
    ppermute x17, waiting for transfers between devices, flipped(): return lax.ppermute(value, axis, pairs)  6.35 us
    ppermute x3, starting transfers between devices, flipped_both(): return lax.ppermute(value, ('dp', 'ctx'), pairs)  5.03 us
  transfers between devices with their start and end apart: 27, of which 11 were waited for; matrix products, arithmetic and copies ran while one was open for 0% of the time, Pallas kernels for 12%

profile of v3, /device:TPU:0, one launch (start us, length us, event | category | flops | bytes accessed | tf_op | source)
XLA Modules:
  0.0 70.3 jit_solution(7099511115606907388)
XLA Ops:
  0.0 0.1 pad_add_fusion.ids_ref
  0.1 2.0 %shard_map.64 = (bf16[512,256]{1,0:T(8,128)(2,1)S(1)}, bf16[4,128,512]{2,1,0:T(8,128)(2,1)S(1)}, bf16[4,128,512]{2,1,0:T(8,128)(2,1)S(1)}) custom-call(s32[2]{0:T(128)S(1)} %pad_add_fusion.ids_ref, bf16[128,4096]{1,0:T(8,128)(2,1)} %bitcast.15, bf16[512,128]{1,0:T(8,128)(2,1)} %query_ref.1, bf16[512,128]{1,0:T(8,128)(2,1)} %key_ref.1), custom_call_target="tpu_custom_call" | custom-call | tf_op jit(solution)/shard_map/pallas_call | solution.py:67
  2.1 4.0 %collective-permute-start.10 = (bf16[4,128,512]{2,1,0:T(8,128)(2,1)S(1)}, bf16[4,128,512]{2,1,0:T(8,128)(2,1)S(1)}, u32[]{:S(2)}, u32[]{:S(2)}) collective-permute-start(bf16[4,128,512]{2,1,0:T(8,128)(2,1)S(1)} %get-tuple-element.33), channel_id=1, source_target_pairs={{0,6},{1,7},{2,4},{3,5},{4,2},{5,3},{6,0},{7,1},{8,14},{9,15},{10,... | collective-permute-start | bytes 1572872 | tf_op jit(solution)/shard_map/ppermute | solution.py:29
  6.1 0.5 collective-permute-start.8
  6.6 1.6 %collective-permute-start.4 = (bf16[512,256]{1,0:T(8,128)(2,1)S(1)}, bf16[512,256]{1,0:T(8,128)(2,1)S(1)}, u32[]{:S(2)}, u32[]{:S(2)}) collective-permute-start(bf16[512,256]{1,0:T(8,128)(2,1)S(1)} %copy-done), channel_id=1, source_target_pairs={{0,8},{4,12},{8,24},{12,28},{24,16},{28,20},{16,0},{20,4},{1,9},{5... | collective-permute-start | bytes 786440 | tf_op jit(solution)/shard_map/ppermute | solution.py:355
  8.2 2.6 %collective-permute-start.3 = (bf16[512,256]{1,0:T(8,128)(2,1)S(1)}, bf16[512,256]{1,0:T(8,128)(2,1)S(1)}, u32[]{:S(2)}, u32[]{:S(2)}) collective-permute-start(bf16[512,256]{1,0:T(8,128)(2,1)S(1)} %get-tuple-element.30.refs_4_), channel_id=1, source_target_pairs={{0,8},{4,12},{8,24},{12,28},{24,16},{28,20},{16,0},{20,4},{1,9},{5... | collective-permute-start | bytes 786440 | tf_op jit(solution)/shard_map/ppermute | solution.py:355
  10.8 0.5 collective-permute-start.1
  11.3 5.4 %collective-permute-done.4.refs_7_ = bf16[512,256]{1,0:T(8,128)(2,1)S(1)} collective-permute-done((bf16[512,256]{1,0:T(8,128)(2,1)S(1)}, bf16[512,256]{1,0:T(8,128)(2,1)S(1)}, u32[]{:S(2)}, u32[]{:S(2)}) %collective-permute-start.4) | collective-permute-done | bytes 262176 | tf_op jit(solution)/shard_map/ppermute | solution.py:355
  16.7 0.8 %collective-permute-start.6 = (bf16[512,256]{1,0:T(8,128)(2,1)S(1)}, bf16[512,256]{1,0:T(8,128)(2,1)S(1)}, u32[]{:S(2)}, u32[]{:S(2)}) collective-permute-start(bf16[512,256]{1,0:T(8,128)(2,1)S(1)} %collective-permute-done.4.refs_7_), channel_id=1, source_target_pairs={{0,8},{4,12},{8,24},{12,28},{24,16},{28,20},{16,0},{20,4},{1,9},{5... | collective-permute-start | bytes 786440 | tf_op jit(solution)/shard_map/ppermute | solution.py:355
  17.5 4.8 %collective-permute-done.3.refs_6_ = bf16[512,256]{1,0:T(8,128)(2,1)S(1)} collective-permute-done((bf16[512,256]{1,0:T(8,128)(2,1)S(1)}, bf16[512,256]{1,0:T(8,128)(2,1)S(1)}, u32[]{:S(2)}, u32[]{:S(2)}) %collective-permute-start.3) | collective-permute-done | bytes 262176 | tf_op jit(solution)/shard_map/ppermute | solution.py:355
  22.3 0.8 %collective-permute-start.5 = (bf16[512,256]{1,0:T(8,128)(2,1)S(1)}, bf16[512,256]{1,0:T(8,128)(2,1)S(1)}, u32[]{:S(2)}, u32[]{:S(2)}) collective-permute-start(bf16[512,256]{1,0:T(8,128)(2,1)S(1)} %collective-permute-done.3.refs_6_), channel_id=1, source_target_pairs={{0,8},{4,12},{8,24},{12,28},{24,16},{28,20},{16,0},{20,4},{1,9},{5... | collective-permute-start | bytes 786440 | tf_op jit(solution)/shard_map/ppermute | solution.py:355
  23.1 0.0 collective-permute-done.10.refs_2_
  23.1 0.0 collective-permute-start.11
  23.1 6.4 %collective-permute-done.8.refs_0_ = bf16[4,128,512]{2,1,0:T(8,128)(2,1)S(1)} collective-permute-done((bf16[4,128,512]{2,1,0:T(8,128)(2,1)S(1)}, bf16[4,128,512]{2,1,0:T(8,128)(2,1)S(1)}, u32[]{:S(2)}, u32[]{:S(2)}) %collective-permute-start.8) | collective-permute-done | bytes 524320 | tf_op jit(solution)/shard_map/ppermute | solution.py:29
  29.5 0.5 collective-permute-start
  30.0 1.8 %collective-permute-done.5.refs_8_ = bf16[512,256]{1,0:T(8,128)(2,1)S(1)} collective-permute-done((bf16[512,256]{1,0:T(8,128)(2,1)S(1)}, bf16[512,256]{1,0:T(8,128)(2,1)S(1)}, u32[]{:S(2)}, u32[]{:S(2)}) %collective-permute-start.5) | collective-permute-done | bytes 262176 | tf_op jit(solution)/shard_map/ppermute | solution.py:355
  31.8 0.8 %collective-permute-start.7 = (bf16[512,256]{1,0:T(8,128)(2,1)S(1)}, bf16[512,256]{1,0:T(8,128)(2,1)S(1)}, u32[]{:S(2)}, u32[]{:S(2)}) collective-permute-start(bf16[512,256]{1,0:T(8,128)(2,1)S(1)} %collective-permute-done.5.refs_8_), channel_id=1, source_target_pairs={{0,8},{4,12},{8,24},{12,28},{24,16},{28,20},{16,0},{20,4},{1,9},{5... | collective-permute-start | bytes 786440 | tf_op jit(solution)/shard_map/ppermute | solution.py:355
  32.6 0.0 collective-permute-done.1.refs_2_
  32.6 0.0 collective-permute-start.2
  32.6 0.0 collective-permute-done.11.refs_3_
  32.7 1.5 %shard_map.67 = (f32[512,512]{1,0:T(8,128)S(1)}, bf16[512,512]{1,0:T(8,128)(2,1)S(1)}) custom-call(s32[2]{0:T(128)S(1)} %pad_add_fusion.ids_ref, bf16[4,128,512]{2,1,0:T(8,128)(2,1)S(1)} %collective-permute-done.8.refs_0_, bf16[4,128,512]{2,1,0:T(8,128)(2,1)S(1)} %collective-permute-done.9.refs_1_, bf16[4,128,512]{2,1,0:T(8,128)(2,1)S(1)} %collective-permute-done.10.refs_2_, ...), custom_call_target="tpu_custom_call" | custom-call | tf_op jit(solution)/shard_map/pallas_call | solution.py:67
  34.2 5.2 %collective-permute-done.7.w = bf16[512,256]{1,0:T(8,128)(2,1)S(1)} collective-permute-done((bf16[512,256]{1,0:T(8,128)(2,1)S(1)}, bf16[512,256]{1,0:T(8,128)(2,1)S(1)}, u32[]{:S(2)}, u32[]{:S(2)}) %collective-permute-start.7) | collective-permute-done | bytes 262176 | tf_op jit(solution)/shard_map/ppermute | solution.py:355
  39.4 0.3 shard_map.68
  39.7 1.6 %collective-permute-start.12 = (f16[512,256]{1,0:T(8,128)(2,1)S(1)}, f16[512,256]{1,0:T(8,128)(2,1)S(1)}, u32[]{:S(2)}, u32[]{:S(2)}) collective-permute-start(f16[512,256]{1,0:T(8,128)(2,1)S(1)} %convert_element_type.27), channel_id=1, source_target_pairs={{0,4},{4,0},{8,12},{12,8},{16,20},{20,16},{24,28},{28,24},{1,5},{5... | collective-permute-start | bytes 786440 | tf_op jit(solution)/shard_map/ppermute | solution.py:20
  41.3 0.8 %collective-permute-start.14 = (bf16[512,128]{1,0:T(8,128)(2,1)S(1)}, bf16[512,128]{1,0:T(8,128)(2,1)S(1)}, u32[]{:S(2)}, u32[]{:S(2)}) collective-permute-start(bf16[512,128]{1,0:T(8,128)(2,1)S(1)} %get-tuple-element.41), channel_id=1, source_target_pairs={{0,8},{4,12},{8,24},{12,28},{24,16},{28,20},{16,0},{20,4},{1,9},{5... | collective-permute-start | bytes 393224 | tf_op jit(solution)/shard_map/ppermute | solution.py:355
  42.2 3.4 %collective-permute-start.16 = (bf16[512,128]{1,0:T(8,128)(2,1)S(1)}, bf16[512,128]{1,0:T(8,128)(2,1)S(1)}, u32[]{:S(2)}, u32[]{:S(2)}) collective-permute-start(bf16[512,128]{1,0:T(8,128)(2,1)S(1)} %get-tuple-element.44), channel_id=1, source_target_pairs={{0,8},{4,12},{8,24},{12,28},{24,16},{28,20},{16,0},{20,4},{1,9},{5... | collective-permute-start | bytes 393224 | tf_op jit(solution)/shard_map/ppermute | solution.py:355
  45.5 1.7 %collective-permute-done.14.w = bf16[512,128]{1,0:T(8,128)(2,1)S(1)} collective-permute-done((bf16[512,128]{1,0:T(8,128)(2,1)S(1)}, bf16[512,128]{1,0:T(8,128)(2,1)S(1)}, u32[]{:S(2)}, u32[]{:S(2)}) %collective-permute-start.14) | collective-permute-done | bytes 131104 | tf_op jit(solution)/shard_map/ppermute | solution.py:355
  47.3 0.3 shard_map.73
  47.6 0.6 collective-permute-start.15
  48.2 0.0 collective-permute-done.refs_1_
  48.2 0.0 collective-permute-done.2.refs_3_
  48.2 1.5 %shard_map.65 = (f32[512,512]{1,0:T(8,128)S(1)}, bf16[512,512]{1,0:T(8,128)(2,1)S(1)}) custom-call(s32[2]{0:T(128)S(1)} %pad_add_fusion.ids_ref, bf16[4,128,512]{2,1,0:T(8,128)(2,1)S(1)} %get-tuple-element.29.refs_0_, bf16[4,128,512]{2,1,0:T(8,128)(2,1)S(1)} %collective-permute-done.refs_1_, bf16[4,128,512]{2,1,0:T(8,128)(2,1)S(1)} %collective-permute-done.1.refs_2_, ...), custom_call_target="tpu_custom_call" | custom-call | tf_op jit(solution)/shard_map/pallas_call | solution.py:67
  49.7 0.3 shard_map.66
  50.0 0.0 collective-permute-done.12
  50.0 0.1 add_convert_fusion.mine
  50.2 0.0 copy-start.1
  50.2 0.0 copy-start.2
  50.2 0.1 collective-permute-start.13
  50.3 0.6 copy-done.2
  50.9 0.2 collective-permute-start.26
  51.1 1.3 %collective-permute-start.25 = (f32[1,256]{1,0:T(1,128)S(1)}, f32[1,256]{1,0:T(1,128)S(1)}, u32[]{:S(2)}, u32[]{:S(2)}) collective-permute-start(f32[1,256]{1,0:T(1,128)S(1)} %bitcast.12), channel_id=1, source_target_pairs={{0,2},{1,3},{2,0},{3,1},{4,6},{5,7},{6,4},{7,5},{8,10},{9,11},{10,... | collective-permute-start | bytes 3080 | tf_op jit(solution)/shard_map/ppermute | solution.py:20
  52.4 1.3 %shard_map.69 = (f32[1,1,512]{2,1,0:T(1,128)S(1)}, f32[1,512,1]{2,1,0:T(8,128)S(1)}, f32[1,1]{1,0:T(1,128)}, s32[1,512]{1,0:T(1,128)S(1)}, s32[512,1]{1,0:T(8,128)S(1)}) custom-call(s32[2]{0:T(128)S(1)} %pad_add_fusion.ids_ref, f32[2,512]{1,0:T(2,128)S(1)} %bitcast.9), custom_call_target="tpu_custom_call" | custom-call | tf_op jit(solution)/shard_map/pallas_call | solution.py:67
  53.7 0.0 collective-permute-done.16.w
  53.7 0.3 collective-permute-start.24
  54.1 0.3 shard_map.76
  54.4 0.3 shard_map.75
  54.7 0.3 shard_map.72
  55.0 0.0 collective-permute-done.15
  55.0 1.6 %collective-permute-start.17 = (f16[512,128]{1,0:T(8,128)(2,1)S(1)}, f16[512,128]{1,0:T(8,128)(2,1)S(1)}, u32[]{:S(2)}, u32[]{:S(2)}) collective-permute-start(f16[512,128]{1,0:T(8,128)(2,1)S(1)} %convert_element_type.33), channel_id=1, source_target_pairs={{0,4},{4,0},{8,12},{12,8},{16,20},{20,16},{24,28},{28,24},{1,5},{5... | collective-permute-start | bytes 393224 | tf_op jit(solution)/shard_map/ppermute | solution.py:20
  56.6 1.5 %shard_map.70 = (bf16[512,512]{1,0:T(8,128)(2,1)S(1)}, f32[512,128]{1,0:T(8,128)S(1)}, f32[512,128]{1,0:T(8,128)S(1)}) custom-call(bf16[512,256]{1,0:T(8,128)(2,1)S(1)} %add_convert_fusion.mine, bf16[512,256]{1,0:T(8,128)(2,1)S(1)} %collective-permute-done.13.other, f32[1,512]{1,0:T(1,128)S(1)} %bitcast.10, f32[512,1]{1,0:T(8,128)S(1)} %bitcast.8, ...), custom_call_target="tpu_custom_call" | custom-call | tf_op jit(solution)/shard_map/pallas_call | solution.py:67
  58.1 0.3 shard_map.74
  58.4 0.1 collective-permute-start.18
  58.5 2.2 %collective-permute-done.17 = f16[512,128]{1,0:T(8,128)(2,1)S(1)} collective-permute-done((f16[512,128]{1,0:T(8,128)(2,1)S(1)}, f16[512,128]{1,0:T(8,128)(2,1)S(1)}, u32[]{:S(2)}, u32[]{:S(2)}) %collective-permute-start.17) | collective-permute-done | bytes 131104 | tf_op jit(solution)/shard_map/ppermute | solution.py:20
  60.7 0.8 %collective-permute-start.20 = (f32[128,128]{1,0:T(8,128)S(1)}, f32[128,128]{1,0:T(8,128)S(1)}, u32[]{:S(2)}, u32[]{:S(2)}) collective-permute-start(f32[128,128]{1,0:T(8,128)S(1)} %get-tuple-element.49), channel_id=1, source_target_pairs={{0,2},{1,3},{2,0},{3,1},{4,6},{5,7},{6,4},{7,5},{8,10},{9,11},{10,... | collective-permute-start | bytes 196616 | tf_op jit(solution)/shard_map/ppermute | solution.py:20
  61.5 0.3 shard_map.77
  61.8 0.1 collective-permute-start.22
  61.9 1.4 %collective-permute-start.19 = (f32[128,128]{1,0:T(8,128)S(1)}, f32[128,128]{1,0:T(8,128)S(1)}, u32[]{:S(2)}, u32[]{:S(2)}) collective-permute-start(f32[128,128]{1,0:T(8,128)S(1)} %get-tuple-element.48), channel_id=1, source_target_pairs={{0,1},{1,0},{2,3},{3,2},{4,5},{5,4},{6,7},{7,6},{8,9},{9,8},{10,11... | collective-permute-start | bytes 196616 | tf_op jit(solution)/shard_map/ppermute | solution.py:20
  63.3 0.7 %collective-permute-start.21 = (f32[128,128]{1,0:T(8,128)S(1)}, f32[128,128]{1,0:T(8,128)S(1)}, u32[]{:S(2)}, u32[]{:S(2)}) collective-permute-start(f32[128,128]{1,0:T(8,128)S(1)} %get-tuple-element.50), channel_id=1, source_target_pairs={{0,2},{1,3},{2,0},{3,1},{4,6},{5,7},{6,4},{7,5},{8,10},{9,11},{10,... | collective-permute-start | bytes 196616 | tf_op jit(solution)/shard_map/ppermute | solution.py:20
  64.0 0.7 collective-permute-start.23
  64.7 0.5 collective-permute-done.20.refs_4_
  65.2 1.0 %collective-permute-done.22.refs_6_ = f32[128,128]{1,0:T(8,128)S(1)} collective-permute-done((f32[128,128]{1,0:T(8,128)S(1)}, f32[128,128]{1,0:T(8,128)S(1)}, u32[]{:S(2)}, u32[]{:S(2)}) %collective-permute-start.22) | collective-permute-done | bytes 65568 | tf_op jit(solution)/shard_map/ppermute | solution.py:20
  66.3 2.0 %collective-permute-done.21.refs_5_ = f32[128,128]{1,0:T(8,128)S(1)} collective-permute-done((f32[128,128]{1,0:T(8,128)S(1)}, f32[128,128]{1,0:T(8,128)S(1)}, u32[]{:S(2)}, u32[]{:S(2)}) %collective-permute-start.21) | collective-permute-done | bytes 65568 | tf_op jit(solution)/shard_map/ppermute | solution.py:20
  68.2 0.6 collective-permute-done.23.refs_7_
  68.8 1.5 %shard_map.78 = bf16[128,1024]{1,0:T(8,128)(2,1)} custom-call(s32[2]{0:T(128)S(1)} %pad_add_fusion.ids_ref, f32[128,128]{1,0:T(8,128)S(1)} %get-tuple-element.43.refs_0_, f32[128,128]{1,0:T(8,128)S(1)} %get-tuple-element.46.refs_1_, f32[128,128]{1,0:T(8,128)S(1)} %collective-permute-done.18.refs_2_, f32[128,128]{1,0:T(8,128)S(1)} %collective-permute-done.19.refs_3_, ...), custom_call_target="tpu_custom_call" | custom-call | tf_op jit(solution)/shard_map/pallas_call | solution.py:67
  (21 shorter events, 0.3 us)
Async XLA Ops:
  0.1 6.5 %copy-start = (bf16[512,256]{1,0:T(8,128)(2,1)S(1)}, bf16[512,256]{1,0:T(8,128)(2,1)}, u32[]{:S(2)}) copy-start(bf16[512,256]{1,0:T(8,128)(2,1)} %refs_5_.3) | copy-start | bytes 786436
  2.1 21.0 %collective-permute-start.10 = (bf16[4,128,512]{2,1,0:T(8,128)(2,1)S(1)}, bf16[4,128,512]{2,1,0:T(8,128)(2,1)S(1)}, u32[]{:S(2)}, u32[]{:S(2)}) collective-permute-start(bf16[4,128,512]{2,1,0:T(8,128)(2,1)S(1)} %get-tuple-element.33), channel_id=1, source_target_pairs={{0,6},{1,7},{2,4},{3,5},{4,2},{5,3},{6,0},{7,1},{8,14},{9,15},{10,... | collective-permute-start | bytes 1572872 | tf_op jit(solution)/shard_map/ppermute | solution.py:29
  6.1 23.5 %collective-permute-start.8 = (bf16[4,128,512]{2,1,0:T(8,128)(2,1)S(1)}, bf16[4,128,512]{2,1,0:T(8,128)(2,1)S(1)}, u32[]{:S(2)}, u32[]{:S(2)}) collective-permute-start(bf16[4,128,512]{2,1,0:T(8,128)(2,1)S(1)} %get-tuple-element.33), channel_id=1, source_target_pairs={{0,4},{1,5},{2,6},{3,7},{4,0},{5,1},{6,2},{7,3},{8,12},{9,13},{10,... | collective-permute-start | bytes 1572872 | tf_op jit(solution)/shard_map/ppermute | solution.py:29
  6.6 10.1 %collective-permute-start.4 = (bf16[512,256]{1,0:T(8,128)(2,1)S(1)}, bf16[512,256]{1,0:T(8,128)(2,1)S(1)}, u32[]{:S(2)}, u32[]{:S(2)}) collective-permute-start(bf16[512,256]{1,0:T(8,128)(2,1)S(1)} %copy-done), channel_id=1, source_target_pairs={{0,8},{4,12},{8,24},{12,28},{24,16},{28,20},{16,0},{20,4},{1,9},{5... | collective-permute-start | bytes 786440 | tf_op jit(solution)/shard_map/ppermute | solution.py:355
  8.2 14.1 %collective-permute-start.3 = (bf16[512,256]{1,0:T(8,128)(2,1)S(1)}, bf16[512,256]{1,0:T(8,128)(2,1)S(1)}, u32[]{:S(2)}, u32[]{:S(2)}) collective-permute-start(bf16[512,256]{1,0:T(8,128)(2,1)S(1)} %get-tuple-element.30.refs_4_), channel_id=1, source_target_pairs={{0,8},{4,12},{8,24},{12,28},{24,16},{28,20},{16,0},{20,4},{1,9},{5... | collective-permute-start | bytes 786440 | tf_op jit(solution)/shard_map/ppermute | solution.py:355
  10.8 21.9 %collective-permute-start.1 = (bf16[4,128,512]{2,1,0:T(8,128)(2,1)S(1)}, bf16[4,128,512]{2,1,0:T(8,128)(2,1)S(1)}, u32[]{:S(2)}, u32[]{:S(2)}) collective-permute-start(bf16[4,128,512]{2,1,0:T(8,128)(2,1)S(1)} %get-tuple-element.29.refs_0_), channel_id=1, source_target_pairs={{0,2},{1,3},{2,0},{3,1},{4,6},{5,7},{6,4},{7,5},{8,10},{9,11},{10,... | collective-permute-start | bytes 1572872 | tf_op jit(solution)/shard_map/ppermute | solution.py:29
  16.7 12.8 %collective-permute-start.6 = (bf16[512,256]{1,0:T(8,128)(2,1)S(1)}, bf16[512,256]{1,0:T(8,128)(2,1)S(1)}, u32[]{:S(2)}, u32[]{:S(2)}) collective-permute-start(bf16[512,256]{1,0:T(8,128)(2,1)S(1)} %collective-permute-done.4.refs_7_), channel_id=1, source_target_pairs={{0,8},{4,12},{8,24},{12,28},{24,16},{28,20},{16,0},{20,4},{1,9},{5... | collective-permute-start | bytes 786440 | tf_op jit(solution)/shard_map/ppermute | solution.py:355
  22.3 9.5 %collective-permute-start.5 = (bf16[512,256]{1,0:T(8,128)(2,1)S(1)}, bf16[512,256]{1,0:T(8,128)(2,1)S(1)}, u32[]{:S(2)}, u32[]{:S(2)}) collective-permute-start(bf16[512,256]{1,0:T(8,128)(2,1)S(1)} %collective-permute-done.3.refs_6_), channel_id=1, source_target_pairs={{0,8},{4,12},{8,24},{12,28},{24,16},{28,20},{16,0},{20,4},{1,9},{5... | collective-permute-start | bytes 786440 | tf_op jit(solution)/shard_map/ppermute | solution.py:355
  23.1 9.5 %collective-permute-start.11 = (bf16[4,128,512]{2,1,0:T(8,128)(2,1)S(1)}, bf16[4,128,512]{2,1,0:T(8,128)(2,1)S(1)}, u32[]{:S(2)}, u32[]{:S(2)}) collective-permute-start(bf16[4,128,512]{2,1,0:T(8,128)(2,1)S(1)} %collective-permute-done.10.refs_2_), channel_id=1, source_target_pairs={{0,1},{1,0},{2,3},{3,2},{4,5},{5,4},{6,7},{7,6},{8,9},{9,8},{10,11... | collective-permute-start | bytes 1572872 | tf_op jit(solution)/shard_map/ppermute | solution.py:20
  29.5 3.1 %collective-permute-start.9 = (bf16[4,128,512]{2,1,0:T(8,128)(2,1)S(1)}, bf16[4,128,512]{2,1,0:T(8,128)(2,1)S(1)}, u32[]{:S(2)}, u32[]{:S(2)}) collective-permute-start(bf16[4,128,512]{2,1,0:T(8,128)(2,1)S(1)} %collective-permute-done.8.refs_0_), channel_id=1, source_target_pairs={{0,1},{1,0},{2,3},{3,2},{4,5},{5,4},{6,7},{7,6},{8,9},{9,8},{10,11... | collective-permute-start | bytes 1572872 | tf_op jit(solution)/shard_map/ppermute | solution.py:20
  29.5 18.7 %collective-permute-start = (bf16[4,128,512]{2,1,0:T(8,128)(2,1)S(1)}, bf16[4,128,512]{2,1,0:T(8,128)(2,1)S(1)}, u32[]{:S(2)}, u32[]{:S(2)}) collective-permute-start(bf16[4,128,512]{2,1,0:T(8,128)(2,1)S(1)} %get-tuple-element.29.refs_0_), channel_id=1, source_target_pairs={{0,1},{1,0},{2,3},{3,2},{4,5},{5,4},{6,7},{7,6},{8,9},{9,8},{10,11... | collective-permute-start | bytes 1572872 | tf_op jit(solution)/shard_map/ppermute | solution.py:20
  31.8 7.5 %collective-permute-start.7 = (bf16[512,256]{1,0:T(8,128)(2,1)S(1)}, bf16[512,256]{1,0:T(8,128)(2,1)S(1)}, u32[]{:S(2)}, u32[]{:S(2)}) collective-permute-start(bf16[512,256]{1,0:T(8,128)(2,1)S(1)} %collective-permute-done.5.refs_8_), channel_id=1, source_target_pairs={{0,8},{4,12},{8,24},{12,28},{24,16},{28,20},{16,0},{20,4},{1,9},{5... | collective-permute-start | bytes 786440 | tf_op jit(solution)/shard_map/ppermute | solution.py:355
  32.6 15.5 %collective-permute-start.2 = (bf16[4,128,512]{2,1,0:T(8,128)(2,1)S(1)}, bf16[4,128,512]{2,1,0:T(8,128)(2,1)S(1)}, u32[]{:S(2)}, u32[]{:S(2)}) collective-permute-start(bf16[4,128,512]{2,1,0:T(8,128)(2,1)S(1)} %collective-permute-done.1.refs_2_), channel_id=1, source_target_pairs={{0,1},{1,0},{2,3},{3,2},{4,5},{5,4},{6,7},{7,6},{8,9},{9,8},{10,11... | collective-permute-start | bytes 1572872 | tf_op jit(solution)/shard_map/ppermute | solution.py:20
  39.7 10.3 %collective-permute-start.12 = (f16[512,256]{1,0:T(8,128)(2,1)S(1)}, f16[512,256]{1,0:T(8,128)(2,1)S(1)}, u32[]{:S(2)}, u32[]{:S(2)}) collective-permute-start(f16[512,256]{1,0:T(8,128)(2,1)S(1)} %convert_element_type.27), channel_id=1, source_target_pairs={{0,4},{4,0},{8,12},{12,8},{16,20},{20,16},{24,28},{28,24},{1,5},{5... | collective-permute-start | bytes 786440 | tf_op jit(solution)/shard_map/ppermute | solution.py:20
  41.3 5.9 %collective-permute-start.14 = (bf16[512,128]{1,0:T(8,128)(2,1)S(1)}, bf16[512,128]{1,0:T(8,128)(2,1)S(1)}, u32[]{:S(2)}, u32[]{:S(2)}) collective-permute-start(bf16[512,128]{1,0:T(8,128)(2,1)S(1)} %get-tuple-element.41), channel_id=1, source_target_pairs={{0,8},{4,12},{8,24},{12,28},{24,16},{28,20},{16,0},{20,4},{1,9},{5... | collective-permute-start | bytes 393224 | tf_op jit(solution)/shard_map/ppermute | solution.py:355
  42.2 11.6 %collective-permute-start.16 = (bf16[512,128]{1,0:T(8,128)(2,1)S(1)}, bf16[512,128]{1,0:T(8,128)(2,1)S(1)}, u32[]{:S(2)}, u32[]{:S(2)}) collective-permute-start(bf16[512,128]{1,0:T(8,128)(2,1)S(1)} %get-tuple-element.44), channel_id=1, source_target_pairs={{0,8},{4,12},{8,24},{12,28},{24,16},{28,20},{16,0},{20,4},{1,9},{5... | collective-permute-start | bytes 393224 | tf_op jit(solution)/shard_map/ppermute | solution.py:355
  47.6 7.4 %collective-permute-start.15 = (f16[512,128]{1,0:T(8,128)(2,1)S(1)}, f16[512,128]{1,0:T(8,128)(2,1)S(1)}, u32[]{:S(2)}, u32[]{:S(2)}) collective-permute-start(f16[512,128]{1,0:T(8,128)(2,1)S(1)} %convert_element_type.30), channel_id=1, source_target_pairs={{0,4},{4,0},{8,12},{12,8},{16,20},{20,16},{24,28},{28,24},{1,5},{5... | collective-permute-start | bytes 393224 | tf_op jit(solution)/shard_map/ppermute | solution.py:20
  50.2 2.3 %copy-start.1 = (f32[1,2,512]{2,1,0:T(2,128)S(1)}, f32[1,2,512]{2,1,0:T(2,128)}, u32[]{:S(2)}) copy-start(f32[1,2,512]{2,1,0:T(2,128)} %param.10) | copy-start | bytes 12292
  50.2 0.7 copy-start.2
  50.2 6.4 %collective-permute-start.13 = (bf16[512,256]{1,0:T(8,128)(2,1)S(1)}, bf16[512,256]{1,0:T(8,128)(2,1)S(1)}, u32[]{:S(2)}, u32[]{:S(2)}) collective-permute-start(bf16[512,256]{1,0:T(8,128)(2,1)S(1)} %pad_maximum_fusion), channel_id=1, source_target_pairs={{0,1},{1,0},{2,3},{3,2},{4,5},{5,4},{6,7},{7,6},{8,9},{9,8},{10,11... | collective-permute-start | bytes 786440 | tf_op jit(solution)/shard_map/ppermute | solution.py:20
  50.9 10.9 %collective-permute-start.26 = (f32[1,256]{1,0:T(1,128)S(1)}, f32[1,256]{1,0:T(1,128)S(1)}, u32[]{:S(2)}, u32[]{:S(2)}) collective-permute-start(f32[1,256]{1,0:T(1,128)S(1)} %bitcast.11), channel_id=1, source_target_pairs={{0,3},{1,2},{2,1},{3,0},{4,7},{5,6},{6,5},{7,4},{8,11},{9,10},{10,... | collective-permute-start | bytes 3080 | tf_op jit(solution)/shard_map/ppermute | solution.py:20
  51.1 10.7 %collective-permute-start.25 = (f32[1,256]{1,0:T(1,128)S(1)}, f32[1,256]{1,0:T(1,128)S(1)}, u32[]{:S(2)}, u32[]{:S(2)}) collective-permute-start(f32[1,256]{1,0:T(1,128)S(1)} %bitcast.12), channel_id=1, source_target_pairs={{0,2},{1,3},{2,0},{3,1},{4,6},{5,7},{6,4},{7,5},{8,10},{9,11},{10,... | collective-permute-start | bytes 3080 | tf_op jit(solution)/shard_map/ppermute | solution.py:20
  53.7 9.5 %collective-permute-start.24 = (f32[1,256]{1,0:T(1,128)S(1)}, f32[1,256]{1,0:T(1,128)S(1)}, u32[]{:S(2)}, u32[]{:S(2)}) collective-permute-start(f32[1,256]{1,0:T(1,128)S(1)} %bitcast.13), channel_id=1, source_target_pairs={{0,1},{1,0},{2,3},{3,2},{4,5},{5,4},{6,7},{7,6},{8,9},{9,8},{10,11... | collective-permute-start | bytes 3080 | tf_op jit(solution)/shard_map/ppermute | solution.py:20
  55.0 5.7 %collective-permute-start.17 = (f16[512,128]{1,0:T(8,128)(2,1)S(1)}, f16[512,128]{1,0:T(8,128)(2,1)S(1)}, u32[]{:S(2)}, u32[]{:S(2)}) collective-permute-start(f16[512,128]{1,0:T(8,128)(2,1)S(1)} %convert_element_type.33), channel_id=1, source_target_pairs={{0,4},{4,0},{8,12},{12,8},{16,20},{20,16},{24,28},{28,24},{1,5},{5... | collective-permute-start | bytes 393224 | tf_op jit(solution)/shard_map/ppermute | solution.py:20
  58.4 5.6 %collective-permute-start.18 = (f32[128,128]{1,0:T(8,128)S(1)}, f32[128,128]{1,0:T(8,128)S(1)}, u32[]{:S(2)}, u32[]{:S(2)}) collective-permute-start(f32[128,128]{1,0:T(8,128)S(1)} %get-tuple-element.47), channel_id=1, source_target_pairs={{0,1},{1,0},{2,3},{3,2},{4,5},{5,4},{6,7},{7,6},{8,9},{9,8},{10,11... | collective-permute-start | bytes 196616 | tf_op jit(solution)/shard_map/ppermute | solution.py:20
  60.7 4.5 %collective-permute-start.20 = (f32[128,128]{1,0:T(8,128)S(1)}, f32[128,128]{1,0:T(8,128)S(1)}, u32[]{:S(2)}, u32[]{:S(2)}) collective-permute-start(f32[128,128]{1,0:T(8,128)S(1)} %get-tuple-element.49), channel_id=1, source_target_pairs={{0,2},{1,3},{2,0},{3,1},{4,6},{5,7},{6,4},{7,5},{8,10},{9,11},{10,... | collective-permute-start | bytes 196616 | tf_op jit(solution)/shard_map/ppermute | solution.py:20
  61.8 4.5 %collective-permute-start.22 = (f32[128,128]{1,0:T(8,128)S(1)}, f32[128,128]{1,0:T(8,128)S(1)}, u32[]{:S(2)}, u32[]{:S(2)}) collective-permute-start(f32[128,128]{1,0:T(8,128)S(1)} %get-tuple-element.51), channel_id=1, source_target_pairs={{0,3},{1,2},{2,1},{3,0},{4,7},{5,6},{6,5},{7,4},{8,11},{9,10},{10,... | collective-permute-start | bytes 196616 | tf_op jit(solution)/shard_map/ppermute | solution.py:20
  61.9 4.4 %collective-permute-start.19 = (f32[128,128]{1,0:T(8,128)S(1)}, f32[128,128]{1,0:T(8,128)S(1)}, u32[]{:S(2)}, u32[]{:S(2)}) collective-permute-start(f32[128,128]{1,0:T(8,128)S(1)} %get-tuple-element.48), channel_id=1, source_target_pairs={{0,1},{1,0},{2,3},{3,2},{4,5},{5,4},{6,7},{7,6},{8,9},{9,8},{10,11... | collective-permute-start | bytes 196616 | tf_op jit(solution)/shard_map/ppermute | solution.py:20
  63.3 5.0 %collective-permute-start.21 = (f32[128,128]{1,0:T(8,128)S(1)}, f32[128,128]{1,0:T(8,128)S(1)}, u32[]{:S(2)}, u32[]{:S(2)}) collective-permute-start(f32[128,128]{1,0:T(8,128)S(1)} %get-tuple-element.50), channel_id=1, source_target_pairs={{0,2},{1,3},{2,0},{3,1},{4,6},{5,7},{6,4},{7,5},{8,10},{9,11},{10,... | collective-permute-start | bytes 196616 | tf_op jit(solution)/shard_map/ppermute | solution.py:20
  64.0 4.8 %collective-permute-start.23 = (f32[128,128]{1,0:T(8,128)S(1)}, f32[128,128]{1,0:T(8,128)S(1)}, u32[]{:S(2)}, u32[]{:S(2)}) collective-permute-start(f32[128,128]{1,0:T(8,128)S(1)} %get-tuple-element.52), channel_id=1, source_target_pairs={{0,3},{1,2},{2,1},{3,0},{4,7},{5,6},{6,5},{7,4},{8,11},{9,10},{10,... | collective-permute-start | bytes 196616 | tf_op jit(solution)/shard_map/ppermute | solution.py:20

commit v4 on v3

--- a/solution.py
+++ b/solution.py
@@ -13,20 +13,12 @@
 TOKEN_MOST = 6.0
 WEIGHT_MOST = 0.09375
 GRANT = 16 * 2**20
+TAIL = 8
 
 
 def flipped(value, axis, mask):
     pairs = [(source, source ^ mask) for source in range(lax.axis_size(axis))]
     return lax.ppermute(value, axis, pairs)
-
-
-def flipped_both(value, mask_dp, mask_ctx):
-    ctx = lax.axis_size("ctx")
-    pairs = [
-        (source, ((source // ctx) ^ mask_dp) * ctx + ((source % ctx) ^ mask_ctx))
-        for source in range(lax.axis_size("dp") * ctx)
-    ]
-    return lax.ppermute(value, ("dp", "ctx"), pairs)
 
 
 def place_at(turn, count):
@@ -74,20 +66,30 @@
     )(*inputs)
 
 
-def prepared(ids, tokens, w_query, w_key, outer):
-    chunk = tokens.shape[0]
+def prepared(ids, tokens, w_query, w_key, w_value, outer):
+    chunk = tokens.shape[0] // 2
     width, part = w_query.shape
-
-    def body(ids_ref, tokens_ref, query_ref, key_ref, pair_ref, own_ref, away_ref, arrivals):
+    half = w_value.shape[1] // 2
+
+    def body(ids_ref, tokens_ref, query_ref, key_ref, value_ref, *refs):
+        pair_ref, first_ref, second_ref = refs[:3]
+        sides = (refs[3:5], refs[5:7])
+        arrivals = refs[7]
         parity = ids_ref[0] % 2
         copies = [
             (query_ref, pair_ref.at[:, pl.ds(0, part)]),
             (key_ref, pair_ref.at[:, pl.ds(part, part)]),
         ]
-        for step in range(outer):
-            for side, out_ref in ((1 - parity, away_ref), (parity, own_ref)):
-                start = pl.multiple_of((2 * step + side) * width, width)
-                copies.append((tokens_ref.at[:, pl.ds(start, width)], out_ref.at[step]))
+        for side, outs in ((1 - parity, sides[0]), (parity, sides[1])):
+            for i, out_ref in enumerate(outs):
+                for step in range(outer):
+                    start = pl.multiple_of((2 * step + side) * width, width)
+                    source = tokens_ref.at[pl.ds(i * chunk, chunk), pl.ds(start, width)]
+                    copies.append((source, out_ref.at[step]))
+        copies += [
+            (value_ref.at[:, pl.ds(0, half)], first_ref),
+            (value_ref.at[:, pl.ds(half, half)], second_ref),
+        ]
         copies = [
             pltpu.make_async_copy(source, target, arrivals.at[i])
             for i, (source, target) in enumerate(copies)
@@ -97,18 +99,17 @@
         for copy in copies:
             copy.wait()
 
-    return kernel(
-        body,
-        [
-            pltpu.VMEM((width, 2 * part), jnp.bfloat16),
-            pltpu.VMEM((outer, chunk, width), jnp.bfloat16),
-            pltpu.VMEM((outer, chunk, width), jnp.bfloat16),
-        ],
+    outs = kernel(
+        body,
+        [pltpu.VMEM((width, 2 * part), jnp.bfloat16)]
+        + [pltpu.VMEM((width, half), jnp.bfloat16)] * 2
+        + [pltpu.VMEM((outer, chunk, width), jnp.bfloat16)] * 4,
         [],
         scalars=ids,
-        scratch=[pltpu.SemaphoreType.DMA((2 + 2 * outer,))],
-        far=[tokens, w_query, w_key],
-    )
+        scratch=[pltpu.SemaphoreType.DMA((4 + 4 * outer,))],
+        far=[tokens, w_query, w_key, w_value],
+    )
+    return outs[:3], outs[3:5], outs[5:]
 
 
 def decayed(ids, decay_log, chunk):
@@ -163,21 +164,12 @@
     )
 
 
-def halved(weight):
-    width, wide = weight.shape
-    half = wide // 2
-
-    def body(ref, first, second):
-        first[...] = ref[:, :half]
-        second[...] = ref[:, half:]
-
-    return kernel(body, [pltpu.VMEM((width, half), weight.dtype)] * 2, [weight])
-
-
-def mixed(ids, side, stages):
+def mixed(ids, side, stages, gather):
     steps = len(stages)
     count = len(side)
-    _, chunk, width = side[0].shape
+    split = len(side[0])
+    _, piece, width = side[0][0].shape
+    chunk = split * piece
     parts = [w.shape[1] for w in stages[0]]
     cuts = [sum(parts[:i]) for i in range(len(parts))]
     length = count * chunk
@@ -185,17 +177,17 @@
     def body(ids_ref, *refs):
         turn = turn_of(ids_ref[0] // 2, steps + 1)
         sources = [place_at((turn + steps + 1 - step) % (steps + 1), steps + 1) for step in range(steps + 1)]
-        total_ref, last = refs[-2:]
-        pieces = refs[:count]
+        outs = refs[-2:] if gather else refs[-1:]
+        first = count * split
         weights = [
-            refs[count + step * len(parts) : count + (step + 1) * len(parts)]
+            refs[first + step * len(parts) : first + (step + 1) * len(parts)]
             for step in range(steps)
         ]
         for m in range(0, count, 2):
 
             def rows(step):
                 return jnp.concatenate(
-                    [pieces[m][sources[step]], pieces[m + 1][sources[step]]], axis=0
+                    [ref[sources[step]] for ref in refs[m * split : (m + 2) * split]], axis=0
                 )
 
             span = pl.ds(m * chunk, 2 * chunk)
@@ -204,27 +196,28 @@
                 for step in range(steps):
                     product = dot32(rows(step), weights[step][part][...])
                     total = product if total is None else total + product
-                total_ref[span, cut : cut + parts[part]] = total
-            last[span, :] = rows(steps)
+                outs[0][span, cut : cut + parts[part]] = total
+            if gather:
+                outs[1][span, :] = rows(steps)
 
     return kernel(
         body,
         [
             pltpu.VMEM((length, sum(parts)), jnp.float32),
             pltpu.VMEM((length, width), jnp.bfloat16),
-        ],
-        list(side) + [w for step in stages for w in step],
+        ][: 2 if gather else 1],
+        [rows for pieces in side for rows in pieces] + [w for step in stages for w in step],
         scalars=ids,
     )
 
 
-def projected(side, weight, cut, factor):
-    (length, _), part = side[0].shape, weight.shape[1]
+def projected(total, last, weight, cut, factor):
+    (length, _), part = total.shape, weight.shape[1]
 
     def body(total, last, w, out):
         out[...] = (total[:, cut : cut + part] + dot32(last[...], w[...])) * factor
 
-    return kernel(body, pltpu.VMEM((length, part), jnp.float32), [*side, weight])
+    return kernel(body, pltpu.VMEM((length, part), jnp.float32), [total, last, weight])
 
 
 def joined(kept, came, scale):
@@ -276,48 +269,50 @@
     return outs[0], outs[1:]
 
 
-def applied(weights, values, carried, chunk):
+def applied(weights, values, carried, gain, chunk):
     length, part = values.shape
 
-    def body(weights_ref, values_ref, carried_ref, *outs):
+    def body(weights_ref, values_ref, carried_ref, gain_ref, *outs):
         for m, out in enumerate(outs):
             rows = pl.ds(m * chunk, chunk)
-            out[...] = dot32(weights_ref[rows, :], values_ref[...]) + carried_ref[rows, :]
+            out[pl.ds(0, chunk), :] = (
+                dot32(weights_ref[rows, :], values_ref[...]) + carried_ref[rows, :]
+            )
+            out[pl.ds(chunk, TAIL), :] = jnp.broadcast_to(gain_ref[...], (TAIL, part))
 
     return kernel(
         body,
-        [pltpu.VMEM((chunk, part), jnp.float32)] * (length // chunk),
-        [weights, values, carried],
-    )
-
-
-def finished(ids, pieces, gains):
+        [pltpu.VMEM((chunk + TAIL, part), jnp.float32)] * (length // chunk),
+        [weights, values, carried, gain],
+    )
+
+
+def finished(ids, pieces):
     count = len(pieces)
     groups = len(pieces[0])
-    chunk, part = pieces[0][0].shape
+    rows, part = pieces[0][0].shape
+    chunk = rows - TAIL
     wide = groups * part
 
     def body(ids_ref, *refs):
         out = refs[-1]
-        gain_refs = refs[count * groups : count * groups + count]
         for m in range(0, count, 2):
-            mine = [refs[i] for i in range(m * groups, (m + 2) * groups)]
-            total = jnp.sum(sum(ref[...] for ref in mine), axis=1, keepdims=True)
-            average = total / (2 * wide)
-            centered = [ref[...] - average for ref in mine]
+            mine = refs[m * groups : (m + 2) * groups]
+            heads = [ref[pl.ds(0, chunk), :] for ref in mine]
+            average = jnp.sum(sum(heads), axis=1, keepdims=True) / (2 * wide)
+            centered = [head - average for head in heads]
             squares = jnp.sum(sum(c * c for c in centered), axis=1, keepdims=True)
             rate = lax.rsqrt(squares / (2 * wide) + norm_eps)
             for i, c in enumerate(centered):
                 which = m + i // groups
-                group = i % groups
-                gain = gain_refs[which][:, group * part : (group + 1) * part]
-                start = pl.multiple_of((ids_ref[1] ^ which) * wide + group * part, part)
+                gain = mine[i][pl.ds(chunk, 1), :]
+                start = pl.multiple_of((ids_ref[1] ^ which) * wide + i % groups * part, part)
                 out[:, pl.ds(start, part)] = (c * rate * gain).astype(jnp.bfloat16)
 
     return kernel(
         body,
         jax.ShapeDtypeStruct((chunk, count * wide), jnp.bfloat16),
-        [ref for piece in pieces for ref in piece] + list(gains),
+        [ref for piece in pieces for ref in piece],
         scalars=ids,
     )
 
@@ -337,52 +332,54 @@
     blocks = length // BLOCK
     high = me // (BLOCK // chunk)
 
-    pair, own_tokens, away_tokens = prepared(ids, tokens[0], w_query, w_key, outer)
+    held, away_tokens, own_tokens = prepared(
+        ids, tokens[0], w_query, w_key, w_value, outer
+    )
     log_rows, log_cols, ends, place_row, place_col = decayed(ids, decay_log[0], chunk)
 
     order = loop_order(outer)
     ring = [
         (order[i] * 2 + p, order[(i + 1) % outer] * 2 + p) for i in range(outer) for p in range(2)
     ]
-    held = [pair, w_value]
     stages = []
-    for step in range(1, outer):
+    for _ in range(1, outer):
         stages.append(held)
-        if step == outer - 1:
-            held = [held[0], *halved(held[1])]
         sent = []
         for piece in held:
             sent.append(lax.ppermute(piece, "dp", ring))
         held = sent
 
-    def rows_of(piece, mask_dp):
-        pieces = {}
+    def rows_of(parts):
+        pieces = {0: parts}
+        for m in range(2, ctx, 2):
+            pieces[m] = []
+            for part in parts:
+                pieces[m].append(flipped(part, "ctx", m))
         for m in range(0, ctx, 2):
-            if m == 0 and mask_dp == 0:
-                pieces[m] = piece
-            else:
-                pieces[m] = flipped_both(piece, mask_dp, m)
-        for m in range(0, ctx, 2):
-            pieces[m + 1] = flipped(pieces[m], "ctx", 1)
+            pieces[m + 1] = []
+            for part in pieces[m]:
+                pieces[m + 1].append(flipped(part, "ctx", 1))
         return [pieces[m] for m in range(ctx)]
 
-    own_rows = rows_of(own_tokens, 0)
-    away_rows = rows_of(away_tokens, 1)
-    gains = [group_gain[None]]
-    for m in range(1, ctx):
-        gains.append(flipped(group_gain[None], "ctx", m))
-
-    away = mixed(ids, away_rows, stages)
-    kept = mixed(ids, own_rows, stages)
+    came = []
+    for part in away_tokens:
+        came.append(flipped(part, "dp", 1))
+    away_rows = rows_of(came)
+    own_rows = rows_of(own_tokens)
+    early = [[step[0]] for step in stages]
+    late = [step[1:] for step in stages]
+    away, away_last = mixed(ids, away_rows, early, True)
+    kept, kept_last = mixed(ids, own_rows, early, True)
+    away_late = mixed(ids, away_rows, late, False)[0]
+    kept_late = mixed(ids, own_rows, late, False)[0]
 
     limit = TOKEN_MOST * WEIGHT_MOST * outer * width
     scale = 2.0 ** math.floor(math.log2(65504.0 / limit))
     stays = []
-    cut = 0
-    for weight in held:
-        gone = projected(away, weight, cut, scale)
-        stay = projected(kept, weight, cut, 1.0)
-        cut += weight.shape[1]
+    for part, weight in enumerate(held):
+        cut = max(part - 1, 0) * half
+        gone = projected(away_late if part else away, away_last, weight, cut, scale)
+        stay = projected(kept_late if part else kept, kept_last, weight, cut, 1.0)
         stays.append((stay, flipped(gone.astype(jnp.float16), "dp", 1)))
 
     pair_mine = joined(*stays[0], scale)
@@ -398,6 +395,7 @@
     prior = jnp.zeros((1, 1), jnp.float32)
     outputs = [jnp.zeros((length, half), jnp.float32) for _ in stays[1:]]
     arrived = [[] for _ in range(ctx)]
+    gains = [group_gain[None, i * half : (i + 1) * half] for i in range(len(stays) - 1)]
     values = []
     for stay in stays[1:]:
         values.append(joined(*stay, scale))
@@ -410,24 +408,30 @@
         faded = k_block.astype(jnp.float32) * jnp.exp(end - log_cols[n])
         for group in range(len(values)):
             v_block = cut_rows(values[group], n)
-            results = applied(weights, v_block, carried[group], chunk)
+            results = applied(weights, v_block, carried[group], gains[group], chunk)
             memories[group] = jnp.exp(end - prior) * memories[group] + dot_exact(
                 faded.T, v_block.astype(jnp.float32)
             )
             if blocks > 1:
                 outputs[group] = lax.dynamic_update_slice_in_dim(
-                    outputs[group], jnp.concatenate(results), (n ^ high) * BLOCK, axis=0
+                    outputs[group],
+                    jnp.concatenate([rows[:chunk] for rows in results]),
+                    (n ^ high) * BLOCK,
+                    axis=0,
                 )
             else:
                 outputs[group] = results
         prior = end
-    for results in outputs:
+    for group, results in enumerate(outputs):
         if blocks > 1:
-            results = [results[m * chunk : (m + 1) * chunk] for m in range(ctx)]
+            below = jnp.broadcast_to(gains[group], (TAIL, half))
+            results = [
+                jnp.concatenate([results[m * chunk : (m + 1) * chunk], below]) for m in range(ctx)
+            ]
         arrived[0].append(results[0])
         for m in range(1, ctx):
             arrived[m].append(flipped(results[m], "ctx", m))
-    return finished(ids, arrived, gains)[None]
+    return finished(ids, arrived)[None]
 
 
 def solution(mesh):

time: 70.5 us -> 86.2 us (1.22)
  waiting for transfers between devices: 31.7 us -> 40.4 us
  starting transfers between devices: 25.7 us -> 30.3 us
  Pallas kernels: 11.7 us -> 14.1 us
    ppermute x17 -> x24, waiting for transfers between devices: 6.35 us -> 24.2 us  [flipped(): return lax.ppermute(value, axis, pairs)]
    ppermute x3 -> x0, waiting for transfers between devices: 6.43 us -> none  [flipped_both(): return lax.ppermute(value, ('dp', 'ctx'), pairs)]
    ppermute x17 -> x24, starting transfers between devices: 9.91 us -> 15.2 us  [flipped(): return lax.ppermute(value, axis, pairs)]
    ppermute x3 -> x0, starting transfers between devices: 5.03 us -> none  [flipped_both(): return lax.ppermute(value, ('dp', 'ctx'), pairs)]
    ppermute x7 -> x9, starting transfers between devices: 10.7 us -> 15.1 us  [whole(): sent.append(lax.ppermute(piece, 'dp', ring))]
    ppermute x7 -> x9, waiting for transfers between devices: 18.9 us -> 16.2 us  [whole(): sent.append(lax.ppermute(piece, 'dp', ring))]
    pallas_call x15 -> x16, Pallas kernels: 11.7 us -> 14.1 us  [kernel(): pl.pallas_call(body, out_shape=out, in_specs=specs, out_specs=jax.tree.ma...]
  transfers between devices with their start and end apart: 27 -> 33, of which waited for: 11 -> 14; matrix products, arithmetic and copies ran while one was open for 0% -> 0% of each run, Pallas kernels for 12% -> 12%
where the time goes in v4:
time: 86.2 us; the launch traced here: 86 us
  waiting for transfers between devices  40.4 us (47%)
  starting transfers between devices  30.3 us (35%)
  Pallas kernels  14.1 us (16%)
    ppermute x24, waiting for transfers between devices, flipped(): return lax.ppermute(value, axis, pairs)  24.2 us
    ppermute x9, waiting for transfers between devices, whole(): sent.append(lax.ppermute(piece, 'dp', ring))  16.2 us
    ppermute x24, starting transfers between devices, flipped(): return lax.ppermute(value, axis, pairs)  15.2 us
    ppermute x9, starting transfers between devices, whole(): sent.append(lax.ppermute(piece, 'dp', ring))  15.1 us
    pallas_call x16, Pallas kernels, kernel(): pl.pallas_call(body, out_shape=out, in_specs=specs, out_specs=jax.tree.ma...  14.1 us
  transfers between devices with their start and end apart: 33, of which 14 were waited for; matrix products, arithmetic and copies ran while one was open for 0% of the time, Pallas kernels for 12%

profile of v4, /device:TPU:0, one launch (start us, length us, event | category | flops | bytes accessed | tf_op | source)
XLA Modules:
  0.0 86.0 jit_solution(7473653651093692447)
XLA Ops:
  0.0 0.1 pad_add_fusion.ids_ref
  0.1 2.2 %shard_map.64 = (bf16[512,256]{1,0:T(8,128)(2,1)S(1)}, bf16[512,128]{1,0:T(8,128)(2,1)S(1)}, bf16[512,128]{1,0:T(8,128)(2,1)S(1)}, bf16[4,64,512]{2,1,0:T(8,128)...) custom-call(s32[2]{0:T(128)S(1)} %pad_add_fusion.ids_ref, ...), custom_call_target="tpu_custom_call" | custom-call | tf_op jit(solution)/shard_map/pallas_call | solution.py:59
  2.3 3.0 %collective-permute-start.9 = (bf16[4,64,512]{2,1,0:T(8,128)(2,1)S(1)}, bf16[4,64,512]{2,1,0:T(8,128)(2,1)S(1)}, u32[]{:S(2)}, u32[]{:S(2)}) collective-permute-start(bf16[4,64,512]{2,1,0:T(8,128)(2,1)S(1)} %get-tuple-element.36), channel_id=1, source_target_pairs={{0,4},{4,0},{8,12},{12,8},{16,20},{20,16},{24,28},{28,24},{1,5},{5... | collective-permute-start | bytes 786440 | tf_op jit(solution)/shard_map/ppermute | solution.py:21
  5.3 0.1 collective-permute-start.10
  5.4 2.0 %collective-permute-start.19 = (bf16[512,128]{1,0:T(8,128)(2,1)S(1)}, bf16[512,128]{1,0:T(8,128)(2,1)S(1)}, u32[]{:S(2)}, u32[]{:S(2)}) collective-permute-start(bf16[512,128]{1,0:T(8,128)(2,1)S(1)} %get-tuple-element.45.refs_8_), channel_id=1, source_target_pairs={{0,8},{4,12},{8,24},{12,28},{24,16},{28,20},{16,0},{20,4},{1,9},{5... | collective-permute-start | bytes 393224 | tf_op jit(solution)/shard_map/ppermute | solution.py:349
  7.4 2.6 %collective-permute-start.6 = (bf16[512,256]{1,0:T(8,128)(2,1)S(1)}, bf16[512,256]{1,0:T(8,128)(2,1)S(1)}, u32[]{:S(2)}, u32[]{:S(2)}) collective-permute-start(bf16[512,256]{1,0:T(8,128)(2,1)S(1)} %get-tuple-element.33.refs_8_), channel_id=1, source_target_pairs={{0,8},{4,12},{8,24},{12,28},{24,16},{28,20},{16,0},{20,4},{1,9},{5... | collective-permute-start | bytes 786440 | tf_op jit(solution)/shard_map/ppermute | solution.py:349
  10.0 0.4 collective-permute-start.20
  10.4 2.3 %collective-permute-done.19.refs_10_ = bf16[512,128]{1,0:T(8,128)(2,1)S(1)} collective-permute-done((bf16[512,128]{1,0:T(8,128)(2,1)S(1)}, bf16[512,128]{1,0:T(8,128)(2,1)S(1)}, u32[]{:S(2)}, u32[]{:S(2)}) %collective-permute-start.19) | collective-permute-done | bytes 131104 | tf_op jit(solution)/shard_map/ppermute | solution.py:349
  12.8 1.1 %collective-permute-start.21 = (bf16[512,128]{1,0:T(8,128)(2,1)S(1)}, bf16[512,128]{1,0:T(8,128)(2,1)S(1)}, u32[]{:S(2)}, u32[]{:S(2)}) collective-permute-start(bf16[512,128]{1,0:T(8,128)(2,1)S(1)} %collective-permute-done.19.refs_10_), channel_id=1, source_target_pairs={{0,8},{4,12},{8,24},{12,28},{24,16},{28,20},{16,0},{20,4},{1,9},{5... | collective-permute-start | bytes 393224 | tf_op jit(solution)/shard_map/ppermute | solution.py:349
  13.9 7.3 %collective-permute-done.20.refs_11_ = bf16[512,128]{1,0:T(8,128)(2,1)S(1)} collective-permute-done((bf16[512,128]{1,0:T(8,128)(2,1)S(1)}, bf16[512,128]{1,0:T(8,128)(2,1)S(1)}, u32[]{:S(2)}, u32[]{:S(2)}) %collective-permute-start.20) | collective-permute-done | bytes 131104 | tf_op jit(solution)/shard_map/ppermute | solution.py:349
  21.2 1.6 %collective-permute-start.2 = (bf16[4,64,512]{2,1,0:T(8,128)(2,1)S(1)}, bf16[4,64,512]{2,1,0:T(8,128)(2,1)S(1)}, u32[]{:S(2)}, u32[]{:S(2)}) collective-permute-start(bf16[4,64,512]{2,1,0:T(8,128)(2,1)S(1)} %get-tuple-element.31.refs_0_), channel_id=1, source_target_pairs={{0,2},{1,3},{2,0},{3,1},{4,6},{5,7},{6,4},{7,5},{8,10},{9,11},{10,... | collective-permute-start | bytes 786440 | tf_op jit(solution)/shard_map/ppermute | solution.py:21
  22.7 0.0 collective-permute-done.9.refs_0_
  22.8 0.5 collective-permute-start.3
  23.2 1.6 %collective-permute-start.13 = (bf16[4,64,512]{2,1,0:T(8,128)(2,1)S(1)}, bf16[4,64,512]{2,1,0:T(8,128)(2,1)S(1)}, u32[]{:S(2)}, u32[]{:S(2)}) collective-permute-start(bf16[4,64,512]{2,1,0:T(8,128)(2,1)S(1)} %collective-permute-done.9.refs_0_), channel_id=1, source_target_pairs={{0,2},{1,3},{2,0},{3,1},{4,6},{5,7},{6,4},{7,5},{8,10},{9,11},{10,... | collective-permute-start | bytes 786440 | tf_op jit(solution)/shard_map/ppermute | solution.py:21
  24.8 0.5 collective-permute-start.14
  25.2 0.8 collective-permute-start.7
  26.1 4.3 %collective-permute-done.2.refs_4_ = bf16[4,64,512]{2,1,0:T(8,128)(2,1)S(1)} collective-permute-done((bf16[4,64,512]{2,1,0:T(8,128)(2,1)S(1)}, bf16[4,64,512]{2,1,0:T(8,128)(2,1)S(1)}, u32[]{:S(2)}, u32[]{:S(2)}) %collective-permute-start.2) | collective-permute-done | bytes 262176 | tf_op jit(solution)/shard_map/ppermute | solution.py:21
  30.4 5.6 %collective-permute-done.3.refs_5_ = bf16[4,64,512]{2,1,0:T(8,128)(2,1)S(1)} collective-permute-done((bf16[4,64,512]{2,1,0:T(8,128)(2,1)S(1)}, bf16[4,64,512]{2,1,0:T(8,128)(2,1)S(1)}, u32[]{:S(2)}, u32[]{:S(2)}) %collective-permute-start.3) | collective-permute-done | bytes 262176 | tf_op jit(solution)/shard_map/ppermute | solution.py:21
  36.0 4.8 %collective-permute-done.13.refs_4_ = bf16[4,64,512]{2,1,0:T(8,128)(2,1)S(1)} collective-permute-done((bf16[4,64,512]{2,1,0:T(8,128)(2,1)S(1)}, bf16[4,64,512]{2,1,0:T(8,128)(2,1)S(1)}, u32[]{:S(2)}, u32[]{:S(2)}) %collective-permute-start.13) | collective-permute-done | bytes 262176 | tf_op jit(solution)/shard_map/ppermute | solution.py:21
  40.7 2.8 %collective-permute-done.14.refs_5_ = bf16[4,64,512]{2,1,0:T(8,128)(2,1)S(1)} collective-permute-done((bf16[4,64,512]{2,1,0:T(8,128)(2,1)S(1)}, bf16[4,64,512]{2,1,0:T(8,128)(2,1)S(1)}, u32[]{:S(2)}, u32[]{:S(2)}) %collective-permute-start.14) | collective-permute-done | bytes 262176 | tf_op jit(solution)/shard_map/ppermute | solution.py:21
  43.5 1.2 %collective-permute-start.8 = (bf16[512,256]{1,0:T(8,128)(2,1)S(1)}, bf16[512,256]{1,0:T(8,128)(2,1)S(1)}, u32[]{:S(2)}, u32[]{:S(2)}) collective-permute-start(bf16[512,256]{1,0:T(8,128)(2,1)S(1)} %collective-permute-done.7.refs_10_), channel_id=1, source_target_pairs={{0,8},{4,12},{8,24},{12,28},{24,16},{28,20},{16,0},{20,4},{1,9},{5... | collective-permute-start | bytes 786440 | tf_op jit(solution)/shard_map/ppermute | solution.py:349
  44.8 0.2 collective-permute-start
  45.0 2.7 %collective-permute-start.22 = (bf16[512,128]{1,0:T(8,128)(2,1)S(1)}, bf16[512,128]{1,0:T(8,128)(2,1)S(1)}, u32[]{:S(2)}, u32[]{:S(2)}) collective-permute-start(bf16[512,128]{1,0:T(8,128)(2,1)S(1)} %collective-permute-done.20.refs_11_), channel_id=1, source_target_pairs={{0,8},{4,12},{8,24},{12,28},{24,16},{28,20},{16,0},{20,4},{1,9},{5... | collective-permute-start | bytes 393224 | tf_op jit(solution)/shard_map/ppermute | solution.py:349
  47.7 0.0 collective-permute-start.1
  47.7 0.5 collective-permute-start.4
  48.2 5.4 %collective-permute-done.8.w = bf16[512,256]{1,0:T(8,128)(2,1)S(1)} collective-permute-done((bf16[512,256]{1,0:T(8,128)(2,1)S(1)}, bf16[512,256]{1,0:T(8,128)(2,1)S(1)}, u32[]{:S(2)}, u32[]{:S(2)}) %collective-permute-start.8) | collective-permute-done | bytes 262176 | tf_op jit(solution)/shard_map/ppermute | solution.py:349
  53.6 1.1 %shard_map.67 = (f32[512,256]{1,0:T(8,128)S(1)}, bf16[512,512]{1,0:T(8,128)(2,1)S(1)}) custom-call(s32[2]{0:T(128)S(1)} %pad_add_fusion.ids_ref, bf16[4,64,512]{2,1,0:T(8,128)(2,1)S(1)} %collective-permute-done.9.refs_0_, bf16[4,64,512]{2,1,0:T(8,128)(2,1)S(1)} %collective-permute-done.10.refs_1_, bf16[4,64,512]{2,1,0:T(8,128)(2,1)S(1)} %collective-permute-done.11.refs_2_, ...), custom_call_target="tpu_custom_call" | custom-call | tf_op jit(solution)/shard_map/pallas_call | solution.py:59
  54.8 0.3 shard_map.68
  55.1 0.9 collective-permute-done.22.refs_13_
  56.0 1.3 %collective-permute-start.17 = (f16[512,256]{1,0:T(8,128)(2,1)S(1)}, f16[512,256]{1,0:T(8,128)(2,1)S(1)}, u32[]{:S(2)}, u32[]{:S(2)}) collective-permute-start(f16[512,256]{1,0:T(8,128)(2,1)S(1)} %convert_element_type.27), channel_id=1, source_target_pairs={{0,4},{4,0},{8,12},{12,8},{16,20},{20,16},{24,28},{28,24},{1,5},{5... | collective-permute-start | bytes 786440 | tf_op jit(solution)/shard_map/ppermute | solution.py:21
  57.2 0.8 collective-permute-start.25
  58.0 3.4 %collective-permute-start.23 = (bf16[512,128]{1,0:T(8,128)(2,1)S(1)}, bf16[512,128]{1,0:T(8,128)(2,1)S(1)}, u32[]{:S(2)}, u32[]{:S(2)}) collective-permute-start(bf16[512,128]{1,0:T(8,128)(2,1)S(1)} %collective-permute-done.21.refs_12_), channel_id=1, source_target_pairs={{0,8},{4,12},{8,24},{12,28},{24,16},{28,20},{16,0},{20,4},{1,9},{5... | collective-permute-start | bytes 393224 | tf_op jit(solution)/shard_map/ppermute | solution.py:349
  61.4 1.1 %shard_map.65 = (f32[512,256]{1,0:T(8,128)S(1)}, bf16[512,512]{1,0:T(8,128)(2,1)S(1)}) custom-call(s32[2]{0:T(128)S(1)} %pad_add_fusion.ids_ref, bf16[4,64,512]{2,1,0:T(8,128)(2,1)S(1)} %get-tuple-element.31.refs_0_, bf16[4,64,512]{2,1,0:T(8,128)(2,1)S(1)} %get-tuple-element.32.refs_1_, bf16[4,64,512]{2,1,0:T(8,128)(2,1)S(1)} %collective-permute-done.refs_2_, ...), custom_call_target="tpu_custom_call" | custom-call | tf_op jit(solution)/shard_map/pallas_call | solution.py:59
  62.5 1.5 %shard_map.73.total = f32[512,256]{1,0:T(8,128)S(1)} custom-call(s32[2]{0:T(128)S(1)} %pad_add_fusion.ids_ref, bf16[4,64,512]{2,1,0:T(8,128)(2,1)S(1)} %collective-permute-done.9.refs_0_, bf16[4,64,512]{2,1,0:T(8,128)(2,1)S(1)} %collective-permute-done.10.refs_1_, bf16[4,64,512]{2,1,0:T(8,128)(2,1)S(1)} %collective-permute-done.11.refs_2_, ...), custom_call_target="tpu_custom_call" | custom-call | tf_op jit(solution)/shard_map/pallas_call | solution.py:59
  64.1 0.3 collective-permute-done.25.w
  64.4 0.3 shard_map.77
  64.7 0.8 collective-permute-start.26
  65.5 0.3 shard_map.66
  65.9 0.1 add_convert_fusion.mine
  66.0 0.0 copy-start.1
  66.0 0.0 copy-start
  66.0 0.1 collective-permute-start.18
  66.1 0.6 copy-done.1
  66.6 0.0 copy-done
  66.7 1.3 %shard_map.69 = (f32[1,1,512]{2,1,0:T(1,128)S(1)}, f32[1,512,1]{2,1,0:T(8,128)S(1)}, f32[1,1]{1,0:T(1,128)}, s32[1,512]{1,0:T(1,128)S(1)}, s32[512,1]{1,0:T(8,128)S(1)}) custom-call(s32[2]{0:T(128)S(1)} %pad_add_fusion.ids_ref, f32[2,512]{1,0:T(2,128)S(1)} %bitcast.12), custom_call_target="tpu_custom_call" | custom-call | tf_op jit(solution)/shard_map/pallas_call | solution.py:59
  68.0 1.5 %shard_map.71.total = f32[512,256]{1,0:T(8,128)S(1)} custom-call(s32[2]{0:T(128)S(1)} %pad_add_fusion.ids_ref, bf16[4,64,512]{2,1,0:T(8,128)(2,1)S(1)} %get-tuple-element.31.refs_0_, bf16[4,64,512]{2,1,0:T(8,128)(2,1)S(1)} %get-tuple-element.32.refs_1_, bf16[4,64,512]{2,1,0:T(8,128)(2,1)S(1)} %collective-permute-done.refs_2_, ...), custom_call_target="tpu_custom_call" | custom-call | tf_op jit(solution)/shard_map/pallas_call | solution.py:59
  69.5 0.3 shard_map.76
  69.8 0.3 shard_map.72
  70.1 0.3 shard_map.74
  70.4 1.3 %collective-permute-start.24 = (f16[512,128]{1,0:T(8,128)(2,1)S(1)}, f16[512,128]{1,0:T(8,128)(2,1)S(1)}, u32[]{:S(2)}, u32[]{:S(2)}) collective-permute-start(f16[512,128]{1,0:T(8,128)(2,1)S(1)} %convert_element_type.30), channel_id=1, source_target_pairs={{0,4},{4,0},{8,12},{12,8},{16,20},{20,16},{24,28},{28,24},{1,5},{5... | collective-permute-start | bytes 393224 | tf_op jit(solution)/shard_map/ppermute | solution.py:21
  71.8 1.5 %shard_map.70 = (bf16[512,512]{1,0:T(8,128)(2,1)S(1)}, f32[512,128]{1,0:T(8,128)S(1)}, f32[512,128]{1,0:T(8,128)S(1)}) custom-call(bf16[512,256]{1,0:T(8,128)(2,1)S(1)} %add_convert_fusion.mine, bf16[512,256]{1,0:T(8,128)(2,1)S(1)} %collective-permute-done.18.other, f32[1,512]{1,0:T(1,128)S(1)} %bitcast.13, f32[512,1]{1,0:T(8,128)S(1)} %bitcast.11, ...), custom_call_target="tpu_custom_call" | custom-call | tf_op jit(solution)/shard_map/pallas_call | solution.py:59
  73.3 0.3 shard_map.78
  73.6 0.1 collective-permute-start.28
  73.7 2.2 %collective-permute-done.24 = f16[512,128]{1,0:T(8,128)(2,1)S(1)} collective-permute-done((f16[512,128]{1,0:T(8,128)(2,1)S(1)}, f16[512,128]{1,0:T(8,128)(2,1)S(1)}, u32[]{:S(2)}, u32[]{:S(2)}) %collective-permute-start.24) | collective-permute-done | bytes 131104 | tf_op jit(solution)/shard_map/ppermute | solution.py:21
  75.9 1.3 %collective-permute-start.30 = (f32[136,128]{1,0:T(8,128)S(1)}, f32[136,128]{1,0:T(8,128)S(1)}, u32[]{:S(2)}, u32[]{:S(2)}) collective-permute-start(f32[136,128]{1,0:T(8,128)S(1)} %get-tuple-element.54), channel_id=1, source_target_pairs={{0,2},{1,3},{2,0},{3,1},{4,6},{5,7},{6,4},{7,5},{8,10},{9,11},{10,... | collective-permute-start | bytes 208904 | tf_op jit(solution)/shard_map/ppermute | solution.py:21
  77.2 0.3 shard_map.75
  77.5 0.9 %collective-permute-start.27 = (f32[136,128]{1,0:T(8,128)S(1)}, f32[136,128]{1,0:T(8,128)S(1)}, u32[]{:S(2)}, u32[]{:S(2)}) collective-permute-start(f32[136,128]{1,0:T(8,128)S(1)} %get-tuple-element.51), channel_id=1, source_target_pairs={{0,1},{1,0},{2,3},{3,2},{4,5},{5,4},{6,7},{7,6},{8,9},{9,8},{10,11... | collective-permute-start | bytes 208904 | tf_op jit(solution)/shard_map/ppermute | solution.py:21
  78.5 1.3 %collective-permute-start.29 = (f32[136,128]{1,0:T(8,128)S(1)}, f32[136,128]{1,0:T(8,128)S(1)}, u32[]{:S(2)}, u32[]{:S(2)}) collective-permute-start(f32[136,128]{1,0:T(8,128)S(1)} %get-tuple-element.53), channel_id=1, source_target_pairs={{0,2},{1,3},{2,0},{3,1},{4,6},{5,7},{6,4},{7,5},{8,10},{9,11},{10,... | collective-permute-start | bytes 208904 | tf_op jit(solution)/shard_map/ppermute | solution.py:21
  79.7 0.2 collective-permute-start.31
  79.9 0.4 collective-permute-done.30.refs_5_
  80.3 1.4 %collective-permute-done.32.refs_7_ = f32[136,128]{1,0:T(8,128)S(1)} collective-permute-done((f32[136,128]{1,0:T(8,128)S(1)}, f32[136,128]{1,0:T(8,128)S(1)}, u32[]{:S(2)}, u32[]{:S(2)}) %collective-permute-start.32) | collective-permute-done | bytes 69664 | tf_op jit(solution)/shard_map/ppermute | solution.py:21
  81.7 1.8 %collective-permute-done.29.refs_4_ = f32[136,128]{1,0:T(8,128)S(1)} collective-permute-done((f32[136,128]{1,0:T(8,128)S(1)}, f32[136,128]{1,0:T(8,128)S(1)}, u32[]{:S(2)}, u32[]{:S(2)}) %collective-permute-start.29) | collective-permute-done | bytes 69664 | tf_op jit(solution)/shard_map/ppermute | solution.py:21
  83.5 1.0 %collective-permute-done.31.refs_6_ = f32[136,128]{1,0:T(8,128)S(1)} collective-permute-done((f32[136,128]{1,0:T(8,128)S(1)}, f32[136,128]{1,0:T(8,128)S(1)}, u32[]{:S(2)}, u32[]{:S(2)}) %collective-permute-start.31) | collective-permute-done | bytes 69664 | tf_op jit(solution)/shard_map/ppermute | solution.py:21
  84.5 1.5 %shard_map.79 = bf16[128,1024]{1,0:T(8,128)(2,1)} custom-call(s32[2]{0:T(128)S(1)} %pad_add_fusion.ids_ref, f32[136,128]{1,0:T(8,128)S(1)} %get-tuple-element.48.refs_0_, f32[136,128]{1,0:T(8,128)S(1)} %get-tuple-element.50.refs_1_, f32[136,128]{1,0:T(8,128)S(1)} %collective-permute-done.27.refs_2_, f32[136,128]{1,0:T(8,128)S(1)} %collective-permute-done.28.refs_3_, ...), custom_call_target="tpu_custom_call" | custom-call | tf_op jit(solution)/shard_map/pallas_call | solution.py:59
  (33 shorter events, 0.3 us)
Async XLA Ops:
  2.3 20.5 %collective-permute-start.9 = (bf16[4,64,512]{2,1,0:T(8,128)(2,1)S(1)}, bf16[4,64,512]{2,1,0:T(8,128)(2,1)S(1)}, u32[]{:S(2)}, u32[]{:S(2)}) collective-permute-start(bf16[4,64,512]{2,1,0:T(8,128)(2,1)S(1)} %get-tuple-element.36), channel_id=1, source_target_pairs={{0,4},{4,0},{8,12},{12,8},{16,20},{20,16},{24,28},{28,24},{1,5},{5... | collective-permute-start | bytes 786440 | tf_op jit(solution)/shard_map/ppermute | solution.py:21
  5.3 17.9 %collective-permute-start.10 = (bf16[4,64,512]{2,1,0:T(8,128)(2,1)S(1)}, bf16[4,64,512]{2,1,0:T(8,128)(2,1)S(1)}, u32[]{:S(2)}, u32[]{:S(2)}) collective-permute-start(bf16[4,64,512]{2,1,0:T(8,128)(2,1)S(1)} %get-tuple-element.37), channel_id=1, source_target_pairs={{0,4},{4,0},{8,12},{12,8},{16,20},{20,16},{24,28},{28,24},{1,5},{5... | collective-permute-start | bytes 786440 | tf_op jit(solution)/shard_map/ppermute | solution.py:21
  5.4 7.4 %collective-permute-start.19 = (bf16[512,128]{1,0:T(8,128)(2,1)S(1)}, bf16[512,128]{1,0:T(8,128)(2,1)S(1)}, u32[]{:S(2)}, u32[]{:S(2)}) collective-permute-start(bf16[512,128]{1,0:T(8,128)(2,1)S(1)} %get-tuple-element.45.refs_8_), channel_id=1, source_target_pairs={{0,8},{4,12},{8,24},{12,28},{24,16},{28,20},{16,0},{20,4},{1,9},{5... | collective-permute-start | bytes 393224 | tf_op jit(solution)/shard_map/ppermute | solution.py:349
  7.4 17.8 %collective-permute-start.6 = (bf16[512,256]{1,0:T(8,128)(2,1)S(1)}, bf16[512,256]{1,0:T(8,128)(2,1)S(1)}, u32[]{:S(2)}, u32[]{:S(2)}) collective-permute-start(bf16[512,256]{1,0:T(8,128)(2,1)S(1)} %get-tuple-element.33.refs_8_), channel_id=1, source_target_pairs={{0,8},{4,12},{8,24},{12,28},{24,16},{28,20},{16,0},{20,4},{1,9},{5... | collective-permute-start | bytes 786440 | tf_op jit(solution)/shard_map/ppermute | solution.py:349
  10.0 11.2 %collective-permute-start.20 = (bf16[512,128]{1,0:T(8,128)(2,1)S(1)}, bf16[512,128]{1,0:T(8,128)(2,1)S(1)}, u32[]{:S(2)}, u32[]{:S(2)}) collective-permute-start(bf16[512,128]{1,0:T(8,128)(2,1)S(1)} %get-tuple-element.46.refs_9_), channel_id=1, source_target_pairs={{0,8},{4,12},{8,24},{12,28},{24,16},{28,20},{16,0},{20,4},{1,9},{5... | collective-permute-start | bytes 393224 | tf_op jit(solution)/shard_map/ppermute | solution.py:349
  12.8 12.0 %collective-permute-start.21 = (bf16[512,128]{1,0:T(8,128)(2,1)S(1)}, bf16[512,128]{1,0:T(8,128)(2,1)S(1)}, u32[]{:S(2)}, u32[]{:S(2)}) collective-permute-start(bf16[512,128]{1,0:T(8,128)(2,1)S(1)} %collective-permute-done.19.refs_10_), channel_id=1, source_target_pairs={{0,8},{4,12},{8,24},{12,28},{24,16},{28,20},{16,0},{20,4},{1,9},{5... | collective-permute-start | bytes 393224 | tf_op jit(solution)/shard_map/ppermute | solution.py:349
  21.2 9.2 %collective-permute-start.2 = (bf16[4,64,512]{2,1,0:T(8,128)(2,1)S(1)}, bf16[4,64,512]{2,1,0:T(8,128)(2,1)S(1)}, u32[]{:S(2)}, u32[]{:S(2)}) collective-permute-start(bf16[4,64,512]{2,1,0:T(8,128)(2,1)S(1)} %get-tuple-element.31.refs_0_), channel_id=1, source_target_pairs={{0,2},{1,3},{2,0},{3,1},{4,6},{5,7},{6,4},{7,5},{8,10},{9,11},{10,... | collective-permute-start | bytes 786440 | tf_op jit(solution)/shard_map/ppermute | solution.py:21
  22.8 13.2 %collective-permute-start.3 = (bf16[4,64,512]{2,1,0:T(8,128)(2,1)S(1)}, bf16[4,64,512]{2,1,0:T(8,128)(2,1)S(1)}, u32[]{:S(2)}, u32[]{:S(2)}) collective-permute-start(bf16[4,64,512]{2,1,0:T(8,128)(2,1)S(1)} %get-tuple-element.32.refs_1_), channel_id=1, source_target_pairs={{0,2},{1,3},{2,0},{3,1},{4,6},{5,7},{6,4},{7,5},{8,10},{9,11},{10,... | collective-permute-start | bytes 786440 | tf_op jit(solution)/shard_map/ppermute | solution.py:21
  23.2 17.5 %collective-permute-start.13 = (bf16[4,64,512]{2,1,0:T(8,128)(2,1)S(1)}, bf16[4,64,512]{2,1,0:T(8,128)(2,1)S(1)}, u32[]{:S(2)}, u32[]{:S(2)}) collective-permute-start(bf16[4,64,512]{2,1,0:T(8,128)(2,1)S(1)} %collective-permute-done.9.refs_0_), channel_id=1, source_target_pairs={{0,2},{1,3},{2,0},{3,1},{4,6},{5,7},{6,4},{7,5},{8,10},{9,11},{10,... | collective-permute-start | bytes 786440 | tf_op jit(solution)/shard_map/ppermute | solution.py:21
  24.8 18.7 %collective-permute-start.14 = (bf16[4,64,512]{2,1,0:T(8,128)(2,1)S(1)}, bf16[4,64,512]{2,1,0:T(8,128)(2,1)S(1)}, u32[]{:S(2)}, u32[]{:S(2)}) collective-permute-start(bf16[4,64,512]{2,1,0:T(8,128)(2,1)S(1)} %collective-permute-done.10.refs_1_), channel_id=1, source_target_pairs={{0,2},{1,3},{2,0},{3,1},{4,6},{5,7},{6,4},{7,5},{8,10},{9,11},{10,... | collective-permute-start | bytes 786440 | tf_op jit(solution)/shard_map/ppermute | solution.py:21
  25.2 18.3 %collective-permute-start.7 = (bf16[512,256]{1,0:T(8,128)(2,1)S(1)}, bf16[512,256]{1,0:T(8,128)(2,1)S(1)}, u32[]{:S(2)}, u32[]{:S(2)}) collective-permute-start(bf16[512,256]{1,0:T(8,128)(2,1)S(1)} %collective-permute-done.6.refs_9_), channel_id=1, source_target_pairs={{0,8},{4,12},{8,24},{12,28},{24,16},{28,20},{16,0},{20,4},{1,9},{5... | collective-permute-start | bytes 786440 | tf_op jit(solution)/shard_map/ppermute | solution.py:349
  30.4 14.4 %collective-permute-start.11 = (bf16[4,64,512]{2,1,0:T(8,128)(2,1)S(1)}, bf16[4,64,512]{2,1,0:T(8,128)(2,1)S(1)}, u32[]{:S(2)}, u32[]{:S(2)}) collective-permute-start(bf16[4,64,512]{2,1,0:T(8,128)(2,1)S(1)} %collective-permute-done.9.refs_0_), channel_id=1, source_target_pairs={{0,1},{1,0},{2,3},{3,2},{4,5},{5,4},{6,7},{7,6},{8,9},{9,8},{10,11... | collective-permute-start | bytes 786440 | tf_op jit(solution)/shard_map/ppermute | solution.py:21
  36.0 9.1 %collective-permute-start.12 = (bf16[4,64,512]{2,1,0:T(8,128)(2,1)S(1)}, bf16[4,64,512]{2,1,0:T(8,128)(2,1)S(1)}, u32[]{:S(2)}, u32[]{:S(2)}) collective-permute-start(bf16[4,64,512]{2,1,0:T(8,128)(2,1)S(1)} %collective-permute-done.10.refs_1_), channel_id=1, source_target_pairs={{0,1},{1,0},{2,3},{3,2},{4,5},{5,4},{6,7},{7,6},{8,9},{9,8},{10,11... | collective-permute-start | bytes 786440 | tf_op jit(solution)/shard_map/ppermute | solution.py:21
  40.7 7.0 %collective-permute-start.15 = (bf16[4,64,512]{2,1,0:T(8,128)(2,1)S(1)}, bf16[4,64,512]{2,1,0:T(8,128)(2,1)S(1)}, u32[]{:S(2)}, u32[]{:S(2)}) collective-permute-start(bf16[4,64,512]{2,1,0:T(8,128)(2,1)S(1)} %collective-permute-done.13.refs_4_), channel_id=1, source_target_pairs={{0,1},{1,0},{2,3},{3,2},{4,5},{5,4},{6,7},{7,6},{8,9},{9,8},{10,11... | collective-permute-start | bytes 786440 | tf_op jit(solution)/shard_map/ppermute | solution.py:21
  43.5 4.2 %collective-permute-start.16 = (bf16[4,64,512]{2,1,0:T(8,128)(2,1)S(1)}, bf16[4,64,512]{2,1,0:T(8,128)(2,1)S(1)}, u32[]{:S(2)}, u32[]{:S(2)}) collective-permute-start(bf16[4,64,512]{2,1,0:T(8,128)(2,1)S(1)} %collective-permute-done.14.refs_5_), channel_id=1, source_target_pairs={{0,1},{1,0},{2,3},{3,2},{4,5},{5,4},{6,7},{7,6},{8,9},{9,8},{10,11... | collective-permute-start | bytes 786440 | tf_op jit(solution)/shard_map/ppermute | solution.py:21
  43.5 10.1 %collective-permute-start.8 = (bf16[512,256]{1,0:T(8,128)(2,1)S(1)}, bf16[512,256]{1,0:T(8,128)(2,1)S(1)}, u32[]{:S(2)}, u32[]{:S(2)}) collective-permute-start(bf16[512,256]{1,0:T(8,128)(2,1)S(1)} %collective-permute-done.7.refs_10_), channel_id=1, source_target_pairs={{0,8},{4,12},{8,24},{12,28},{24,16},{28,20},{16,0},{20,4},{1,9},{5... | collective-permute-start | bytes 786440 | tf_op jit(solution)/shard_map/ppermute | solution.py:349
  44.8 12.4 %collective-permute-start = (bf16[4,64,512]{2,1,0:T(8,128)(2,1)S(1)}, bf16[4,64,512]{2,1,0:T(8,128)(2,1)S(1)}, u32[]{:S(2)}, u32[]{:S(2)}) collective-permute-start(bf16[4,64,512]{2,1,0:T(8,128)(2,1)S(1)} %get-tuple-element.31.refs_0_), channel_id=1, source_target_pairs={{0,1},{1,0},{2,3},{3,2},{4,5},{5,4},{6,7},{7,6},{8,9},{9,8},{10,11... | collective-permute-start | bytes 786440 | tf_op jit(solution)/shard_map/ppermute | solution.py:21
  45.0 10.9 %collective-permute-start.22 = (bf16[512,128]{1,0:T(8,128)(2,1)S(1)}, bf16[512,128]{1,0:T(8,128)(2,1)S(1)}, u32[]{:S(2)}, u32[]{:S(2)}) collective-permute-start(bf16[512,128]{1,0:T(8,128)(2,1)S(1)} %collective-permute-done.20.refs_11_), channel_id=1, source_target_pairs={{0,8},{4,12},{8,24},{12,28},{24,16},{28,20},{16,0},{20,4},{1,9},{5... | collective-permute-start | bytes 393224 | tf_op jit(solution)/shard_map/ppermute | solution.py:349
  47.7 10.3 %collective-permute-start.1 = (bf16[4,64,512]{2,1,0:T(8,128)(2,1)S(1)}, bf16[4,64,512]{2,1,0:T(8,128)(2,1)S(1)}, u32[]{:S(2)}, u32[]{:S(2)}) collective-permute-start(bf16[4,64,512]{2,1,0:T(8,128)(2,1)S(1)} %get-tuple-element.32.refs_1_), channel_id=1, source_target_pairs={{0,1},{1,0},{2,3},{3,2},{4,5},{5,4},{6,7},{7,6},{8,9},{9,8},{10,11... | collective-permute-start | bytes 786440 | tf_op jit(solution)/shard_map/ppermute | solution.py:21
  47.7 13.7 %collective-permute-start.4 = (bf16[4,64,512]{2,1,0:T(8,128)(2,1)S(1)}, bf16[4,64,512]{2,1,0:T(8,128)(2,1)S(1)}, u32[]{:S(2)}, u32[]{:S(2)}) collective-permute-start(bf16[4,64,512]{2,1,0:T(8,128)(2,1)S(1)} %collective-permute-done.2.refs_4_), channel_id=1, source_target_pairs={{0,1},{1,0},{2,3},{3,2},{4,5},{5,4},{6,7},{7,6},{8,9},{9,8},{10,11... | collective-permute-start | bytes 786440 | tf_op jit(solution)/shard_map/ppermute | solution.py:21
  53.6 7.8 %collective-permute-start.5 = (bf16[4,64,512]{2,1,0:T(8,128)(2,1)S(1)}, bf16[4,64,512]{2,1,0:T(8,128)(2,1)S(1)}, u32[]{:S(2)}, u32[]{:S(2)}) collective-permute-start(bf16[4,64,512]{2,1,0:T(8,128)(2,1)S(1)} %collective-permute-done.3.refs_5_), channel_id=1, source_target_pairs={{0,1},{1,0},{2,3},{3,2},{4,5},{5,4},{6,7},{7,6},{8,9},{9,8},{10,11... | collective-permute-start | bytes 786440 | tf_op jit(solution)/shard_map/ppermute | solution.py:21
  56.0 9.9 %collective-permute-start.17 = (f16[512,256]{1,0:T(8,128)(2,1)S(1)}, f16[512,256]{1,0:T(8,128)(2,1)S(1)}, u32[]{:S(2)}, u32[]{:S(2)}) collective-permute-start(f16[512,256]{1,0:T(8,128)(2,1)S(1)} %convert_element_type.27), channel_id=1, source_target_pairs={{0,4},{4,0},{8,12},{12,8},{16,20},{20,16},{24,28},{28,24},{1,5},{5... | collective-permute-start | bytes 786440 | tf_op jit(solution)/shard_map/ppermute | solution.py:21
  57.2 7.1 %collective-permute-start.25 = (bf16[512,128]{1,0:T(8,128)(2,1)S(1)}, bf16[512,128]{1,0:T(8,128)(2,1)S(1)}, u32[]{:S(2)}, u32[]{:S(2)}) collective-permute-start(bf16[512,128]{1,0:T(8,128)(2,1)S(1)} %collective-permute-done.22.refs_13_), channel_id=1, source_target_pairs={{0,8},{4,12},{8,24},{12,28},{24,16},{28,20},{16,0},{20,4},{1,9},{5... | collective-permute-start | bytes 393224 | tf_op jit(solution)/shard_map/ppermute | solution.py:349
  58.0 11.8 %collective-permute-start.23 = (bf16[512,128]{1,0:T(8,128)(2,1)S(1)}, bf16[512,128]{1,0:T(8,128)(2,1)S(1)}, u32[]{:S(2)}, u32[]{:S(2)}) collective-permute-start(bf16[512,128]{1,0:T(8,128)(2,1)S(1)} %collective-permute-done.21.refs_12_), channel_id=1, source_target_pairs={{0,8},{4,12},{8,24},{12,28},{24,16},{28,20},{16,0},{20,4},{1,9},{5... | collective-permute-start | bytes 393224 | tf_op jit(solution)/shard_map/ppermute | solution.py:349
  64.7 7.1 %collective-permute-start.26 = (f16[512,128]{1,0:T(8,128)(2,1)S(1)}, f16[512,128]{1,0:T(8,128)(2,1)S(1)}, u32[]{:S(2)}, u32[]{:S(2)}) collective-permute-start(f16[512,128]{1,0:T(8,128)(2,1)S(1)} %convert_element_type.33), channel_id=1, source_target_pairs={{0,4},{4,0},{8,12},{12,8},{16,20},{20,16},{24,28},{28,24},{1,5},{5... | collective-permute-start | bytes 393224 | tf_op jit(solution)/shard_map/ppermute | solution.py:21
  66.0 0.7 copy-start.1
  66.0 0.7 copy-start
  66.0 5.8 %collective-permute-start.18 = (bf16[512,256]{1,0:T(8,128)(2,1)S(1)}, bf16[512,256]{1,0:T(8,128)(2,1)S(1)}, u32[]{:S(2)}, u32[]{:S(2)}) collective-permute-start(bf16[512,256]{1,0:T(8,128)(2,1)S(1)} %pad_maximum_fusion), channel_id=1, source_target_pairs={{0,1},{1,0},{2,3},{3,2},{4,5},{5,4},{6,7},{7,6},{8,9},{9,8},{10,11... | collective-permute-start | bytes 786440 | tf_op jit(solution)/shard_map/ppermute | solution.py:21
  70.4 5.4 %collective-permute-start.24 = (f16[512,128]{1,0:T(8,128)(2,1)S(1)}, f16[512,128]{1,0:T(8,128)(2,1)S(1)}, u32[]{:S(2)}, u32[]{:S(2)}) collective-permute-start(f16[512,128]{1,0:T(8,128)(2,1)S(1)} %convert_element_type.30), channel_id=1, source_target_pairs={{0,4},{4,0},{8,12},{12,8},{16,20},{20,16},{24,28},{28,24},{1,5},{5... | collective-permute-start | bytes 393224 | tf_op jit(solution)/shard_map/ppermute | solution.py:21
  73.6 6.1 %collective-permute-start.28 = (f32[136,128]{1,0:T(8,128)S(1)}, f32[136,128]{1,0:T(8,128)S(1)}, u32[]{:S(2)}, u32[]{:S(2)}) collective-permute-start(f32[136,128]{1,0:T(8,128)S(1)} %get-tuple-element.52), channel_id=1, source_target_pairs={{0,1},{1,0},{2,3},{3,2},{4,5},{5,4},{6,7},{7,6},{8,9},{9,8},{10,11... | collective-permute-start | bytes 208904 | tf_op jit(solution)/shard_map/ppermute | solution.py:21
  75.9 4.4 %collective-permute-start.30 = (f32[136,128]{1,0:T(8,128)S(1)}, f32[136,128]{1,0:T(8,128)S(1)}, u32[]{:S(2)}, u32[]{:S(2)}) collective-permute-start(f32[136,128]{1,0:T(8,128)S(1)} %get-tuple-element.54), channel_id=1, source_target_pairs={{0,2},{1,3},{2,0},{3,1},{4,6},{5,7},{6,4},{7,5},{8,10},{9,11},{10,... | collective-permute-start | bytes 208904 | tf_op jit(solution)/shard_map/ppermute | solution.py:21
  77.2 4.5 %collective-permute-start.32 = (f32[136,128]{1,0:T(8,128)S(1)}, f32[136,128]{1,0:T(8,128)S(1)}, u32[]{:S(2)}, u32[]{:S(2)}) collective-permute-start(f32[136,128]{1,0:T(8,128)S(1)} %get-tuple-element.56), channel_id=1, source_target_pairs={{0,3},{1,2},{2,1},{3,0},{4,7},{5,6},{6,5},{7,4},{8,11},{9,10},{10,... | collective-permute-start | bytes 208904 | tf_op jit(solution)/shard_map/ppermute | solution.py:21
  77.5 4.2 %collective-permute-start.27 = (f32[136,128]{1,0:T(8,128)S(1)}, f32[136,128]{1,0:T(8,128)S(1)}, u32[]{:S(2)}, u32[]{:S(2)}) collective-permute-start(f32[136,128]{1,0:T(8,128)S(1)} %get-tuple-element.51), channel_id=1, source_target_pairs={{0,1},{1,0},{2,3},{3,2},{4,5},{5,4},{6,7},{7,6},{8,9},{9,8},{10,11... | collective-permute-start | bytes 208904 | tf_op jit(solution)/shard_map/ppermute | solution.py:21
  78.5 5.1 %collective-permute-start.29 = (f32[136,128]{1,0:T(8,128)S(1)}, f32[136,128]{1,0:T(8,128)S(1)}, u32[]{:S(2)}, u32[]{:S(2)}) collective-permute-start(f32[136,128]{1,0:T(8,128)S(1)} %get-tuple-element.53), channel_id=1, source_target_pairs={{0,2},{1,3},{2,0},{3,1},{4,6},{5,7},{6,4},{7,5},{8,10},{9,11},{10,... | collective-permute-start | bytes 208904 | tf_op jit(solution)/shard_map/ppermute | solution.py:21
  79.7 4.8 %collective-permute-start.31 = (f32[136,128]{1,0:T(8,128)S(1)}, f32[136,128]{1,0:T(8,128)S(1)}, u32[]{:S(2)}, u32[]{:S(2)}) collective-permute-start(f32[136,128]{1,0:T(8,128)S(1)} %get-tuple-element.55), channel_id=1, source_target_pairs={{0,3},{1,2},{2,1},{3,0},{4,7},{5,6},{6,5},{7,4},{8,11},{9,10},{10,... | collective-permute-start | bytes 208904 | tf_op jit(solution)/shard_map/ppermute | solution.py:21
